TPU v7x, 32 devices: a whole 2x2x4 slice. The times are simulated.
32 devices in a mesh: fsdp: 8 (over y, x, core), dp: 4 (over z).
Axes of the slice: x: 2, y: 2, z: 4, core: 2. Of those that a mesh axis runs over, the one named last changes fastest.
Arguments:
- tokens: bfloat16 [4096, 1536], P(('fsdp', 'dp')), may hold values from -6 to 6
- lengths: int32 [32, 4], P('fsdp'), may hold values from 1 to 64, 128 in all within a row
- cotangent: bfloat16 [4096, 1536], P(('fsdp', 'dp')), may hold values from -6 to 6
- attn_gain: bfloat16 [1, 1536], P(None, 'fsdp'), may hold values from 0.5 to 1.5
- w_query: bfloat16 [1, 1536, 1536], P(None, 'fsdp', 'dp'), may hold values from -0.15625 to 0.15625
- w_key: bfloat16 [1, 1536, 768], P(None, 'fsdp', 'dp'), may hold values from -0.15625 to 0.15625
- w_value: bfloat16 [1, 1536, 768], P(None, 'fsdp', 'dp'), may hold values from -0.15625 to 0.15625
- w_out: bfloat16 [1, 1536, 1536], P(None, 'dp', 'fsdp'), may hold values from -0.875 to 0.875
- mlp_gain: bfloat16 [1, 1536], P(None, 'fsdp'), may hold values from 0.5 to 1.5
- w_gate: bfloat16 [1, 1536, 4096], P(None, 'fsdp', 'dp'), may hold values from -0.15625 to 0.15625
- w_up: bfloat16 [1, 1536, 4096], P(None, 'fsdp', 'dp'), may hold values from -0.15625 to 0.15625
- w_down: bfloat16 [1, 4096, 1536], P(None, 'dp', 'fsdp'), may hold values from -0.09375 to 0.09375
Outputs:
- output: bfloat16 [4096, 1536], P(('fsdp', 'dp'))
- grad_tokens: float32 [4096, 1536], P(('fsdp', 'dp'))
- grad_attn_gain: float32 [1, 1536], P(None, 'fsdp')
- grad_w_query: float32 [1, 1536, 1536], P(None, 'fsdp', 'dp')
- grad_w_key: float32 [1, 1536, 768], P(None, 'fsdp', 'dp')
- grad_w_value: float32 [1, 1536, 768], P(None, 'fsdp', 'dp')
- grad_w_out: float32 [1, 1536, 1536], P(None, 'dp', 'fsdp')
- grad_mlp_gain: float32 [1, 1536], P(None, 'fsdp')
- grad_w_gate: float32 [1, 1536, 4096], P(None, 'fsdp', 'dp')
- grad_w_up: float32 [1, 1536, 4096], P(None, 'fsdp', 'dp')
- grad_w_down: float32 [1, 4096, 1536], P(None, 'dp', 'fsdp')
Inputs may be any that keep to these rules, and one draw needn't show every extreme that they name: `lengths`: each row sums to 128 and its largest entry is 64.
All inputs are finite; a program needn't handle non-finite values.
Results may differ from a plain program's by a relative error of at most 0.019.
Values may be sent and summed in bfloat16 or wider, within the bound.
A program may use at most 320 MiB of HBM per device.

v0:
```python
from functools import partial

import jax
import jax.numpy as jnp
from jax import lax
from jax.sharding import PartitionSpec as P

HD = 96
LAYERS = 1


EPSILON = 1e-05
ROPE_BASE = 100000.0
NEG_FILL = -1e30


def layout(seq_lengths, rows_here):
    seg_ends = jnp.cumsum(seq_lengths)
    seg_starts = seg_ends - seq_lengths
    positions = jnp.arange(rows_here, dtype=jnp.int32)
    segment = jnp.sum((positions[:, None] >= seg_ends[None, :]).astype(jnp.int32), axis=1)
    member = segment[:, None] == jnp.arange(seq_lengths.shape[0], dtype=jnp.int32)[None, :]
    offset = jnp.sum(jnp.where(member, seg_starts[None, :], 0), axis=1)
    where_in = positions - offset
    allowed = (segment[:, None] == segment[None, :]) & (positions[None, :] <= positions[:, None])
    half_dim = HD // 2
    frequency = ROPE_BASE ** (-jnp.arange(half_dim, dtype=jnp.float32) / half_dim)
    angles = where_in.astype(jnp.float32)[:, None] * frequency[None, :]
    return (allowed, jnp.cos(angles), jnp.sin(angles))


def rotate(values, cosine, sine_tab, sign_flip):
    half_dim = values.shape[-1] // 2
    front_half = values[..., :half_dim]
    back_half = values[..., half_dim:]
    cos_part = cosine[:, None, :]
    sin_part = sign_flip * sine_tab[:, None, :]
    return jnp.concatenate(
        [
            front_half * cos_part - back_half * sin_part,
            back_half * cos_part + front_half * sin_part,
        ],
        axis=-1,
    )


def rms_scale(stream):
    return lax.rsqrt(jnp.mean(stream * stream, axis=-1, keepdims=True) + EPSILON)


def matmul(left, right):
    return jnp.dot(left, right, preferred_element_type=jnp.float32)


def inner_rows(left, right):
    return lax.dot_general(
        left, right, (((0,), (0,)), ((), ())), preferred_element_type=jnp.float32
    )


def times_transposed(left, right):
    return lax.dot_general(
        left, right, (((1,), (1,)), ((), ())), preferred_element_type=jnp.float32
    )


def attend(queries, keys_rot, values_in, allowed):
    rows_here = queries.shape[0]
    kv_heads = keys_rot.shape[1]
    grouped = queries.reshape(rows_here, kv_heads, queries.shape[1] // kv_heads, HD)
    scores = jnp.einsum(
        "qkgd,skd->kgqs", grouped, keys_rot, preferred_element_type=jnp.float32
    ) * HD ** (-0.5)
    scores = jnp.where(allowed[None, None], scores, NEG_FILL)
    row_top = jnp.max(scores, axis=-1, keepdims=True)
    log_total = row_top + jnp.log(jnp.sum(jnp.exp(scores - row_top), axis=-1, keepdims=True))
    attn_probs = jnp.where(allowed[None, None], jnp.exp(scores - log_total), 0.0)
    probs_low = attn_probs.astype(jnp.bfloat16)
    attn_mixed = jnp.einsum(
        "kgqs,skd->qkgd", probs_low, values_in, preferred_element_type=jnp.float32
    )
    return (attn_probs, attn_mixed.reshape(rows_here, queries.shape[1] * HD).astype(jnp.bfloat16))


def attend_back(queries, keys_rot, values_in, attn_probs, attn_mixed, grad_mixed):
    rows_here = queries.shape[0]
    kv_heads = keys_rot.shape[1]
    groups = queries.shape[1] // kv_heads
    grouped = queries.reshape(rows_here, kv_heads, groups, HD)
    grad_grouped = grad_mixed.reshape(rows_here, kv_heads, groups, HD)
    mixed_grouped = attn_mixed.reshape(rows_here, kv_heads, groups, HD)
    delta = jnp.sum(grad_grouped.astype(jnp.float32) * mixed_grouped.astype(jnp.float32), axis=-1)
    delta = jnp.transpose(delta, (1, 2, 0))[..., None]
    grad_probs = jnp.einsum(
        "qkgd,skd->kgqs", grad_grouped, values_in, preferred_element_type=jnp.float32
    )
    grad_score = (attn_probs * (grad_probs - delta) * HD ** (-0.5)).astype(jnp.bfloat16)
    probs_low = attn_probs.astype(jnp.bfloat16)
    grad_q = jnp.einsum(
        "kgqs,skd->qkgd", grad_score, keys_rot, preferred_element_type=jnp.float32
    ).reshape(rows_here, queries.shape[1], HD)
    grad_k = jnp.einsum("kgqs,qkgd->skd", grad_score, grouped, preferred_element_type=jnp.float32)
    grad_v = jnp.einsum(
        "kgqs,qkgd->skd", probs_low, grad_grouped, preferred_element_type=jnp.float32
    )
    return (grad_q, grad_k, grad_v)


def by_blocks(array_in, count):
    return array_in.reshape((count, array_in.shape[0] // count) + array_in.shape[1:])


def from_blocks(array_in):
    return array_in.reshape((array_in.shape[0] * array_in.shape[1],) + array_in.shape[2:])


def attend_blocks(queries, keys_rot, values_in, allowed):
    count = allowed.shape[0]
    attn_probs, attn_mixed = jax.vmap(attend)(
        by_blocks(queries, count), by_blocks(keys_rot, count), by_blocks(values_in, count), allowed
    )
    return (attn_probs, from_blocks(attn_mixed))


def attend_back_blocks(queries, keys_rot, values_in, attn_probs, attn_mixed, grad_mixed):
    count = attn_probs.shape[0]
    grad_q, grad_k, grad_v = jax.vmap(attend_back)(
        by_blocks(queries, count),
        by_blocks(keys_rot, count),
        by_blocks(values_in, count),
        attn_probs,
        by_blocks(attn_mixed, count),
        by_blocks(grad_mixed, count),
    )
    return (from_blocks(grad_q), from_blocks(grad_k), from_blocks(grad_v))


def layer_forward(stream, weights, allowed, cosine, sine_tab, spread, settle):
    attn_gain, w_query, w_key, w_value, w_out, mlp_gain, w_gate, w_up, w_down = weights
    scale_one = rms_scale(stream)
    normed_one = stream * scale_one
    attn_in = spread((normed_one * attn_gain.astype(jnp.float32)).astype(jnp.bfloat16))
    rows_here = attn_in.shape[0]
    queries = rotate(
        matmul(attn_in, w_query).reshape(rows_here, w_query.shape[1] // HD, HD),
        cosine,
        sine_tab,
        1.0,
    ).astype(jnp.bfloat16)
    keys_rot = rotate(
        matmul(attn_in, w_key).reshape(rows_here, w_key.shape[1] // HD, HD), cosine, sine_tab, 1.0
    ).astype(jnp.bfloat16)
    values_in = (
        matmul(attn_in, w_value).reshape(rows_here, w_value.shape[1] // HD, HD).astype(jnp.bfloat16)
    )
    attn_probs, attn_mixed = attend_blocks(queries, keys_rot, values_in, allowed)
    middle = stream + settle(matmul(attn_mixed, w_out))
    scale_two = rms_scale(middle)
    normed_two = middle * scale_two
    mlp_in = spread((normed_two * mlp_gain.astype(jnp.float32)).astype(jnp.bfloat16))
    gate_act = matmul(mlp_in, w_gate)
    up_act = matmul(mlp_in, w_up)
    hidden = (jax.nn.silu(gate_act) * up_act).astype(jnp.bfloat16)
    result = middle + settle(matmul(hidden, w_down))
    kept_state = (
        scale_one,
        normed_one,
        attn_in,
        queries,
        keys_rot,
        values_in,
        attn_probs,
        attn_mixed,
        scale_two,
        normed_two,
        mlp_in,
        gate_act,
        up_act,
        hidden,
    )
    return (result, kept_state)


def layer_backward(stream, weights, allowed, cosine, sine_tab, grad_stream, spread, settle):
    attn_gain, w_query, w_key, w_value, w_out, mlp_gain, w_gate, w_up, w_down = weights
    _, kept_state = layer_forward(stream, weights, allowed, cosine, sine_tab, spread, settle)
    (
        scale_one,
        normed_one,
        attn_in,
        queries,
        keys_rot,
        values_in,
        attn_probs,
        attn_mixed,
        scale_two,
        normed_two,
        mlp_in,
        gate_act,
        up_act,
        hidden,
    ) = kept_state
    rows_here = attn_in.shape[0]
    grad_low = spread(grad_stream.astype(jnp.bfloat16))
    grad_down = inner_rows(hidden, grad_low)
    grad_hidden = times_transposed(grad_low, w_down)
    sigmoid_gate = jax.nn.sigmoid(gate_act)
    grad_up_act = (grad_hidden * gate_act * sigmoid_gate).astype(jnp.bfloat16)
    grad_gate_act = (
        grad_hidden * up_act * sigmoid_gate * (1.0 + gate_act * (1.0 - sigmoid_gate))
    ).astype(jnp.bfloat16)
    grad_gate = inner_rows(mlp_in, grad_gate_act)
    grad_up = inner_rows(mlp_in, grad_up_act)
    grad_mlp_in = settle(
        times_transposed(grad_gate_act, w_gate) + times_transposed(grad_up_act, w_up)
    )
    grad_mlp_gain = jnp.sum(grad_mlp_in * normed_two, axis=0)
    grad_normed = grad_mlp_in * mlp_gain.astype(jnp.float32)
    grad_middle = grad_stream + scale_two * (
        grad_normed - normed_two * jnp.mean(grad_normed * normed_two, axis=-1, keepdims=True)
    )
    grad_middle_low = spread(grad_middle.astype(jnp.bfloat16))
    grad_out = inner_rows(attn_mixed, grad_middle_low)
    grad_mixed = times_transposed(grad_middle_low, w_out).astype(jnp.bfloat16)
    grad_q, grad_k, grad_v = attend_back_blocks(
        queries, keys_rot, values_in, attn_probs, attn_mixed, grad_mixed
    )
    grad_q = (
        rotate(grad_q, cosine, sine_tab, -1.0)
        .reshape(rows_here, w_query.shape[1])
        .astype(jnp.bfloat16)
    )
    grad_k = (
        rotate(grad_k, cosine, sine_tab, -1.0)
        .reshape(rows_here, w_key.shape[1])
        .astype(jnp.bfloat16)
    )
    grad_v = grad_v.reshape(rows_here, w_value.shape[1]).astype(jnp.bfloat16)
    grad_query = inner_rows(attn_in, grad_q)
    grad_key = inner_rows(attn_in, grad_k)
    grad_value = inner_rows(attn_in, grad_v)
    grad_attn_in = settle(
        times_transposed(grad_q, w_query)
        + times_transposed(grad_k, w_key)
        + times_transposed(grad_v, w_value)
    )
    grad_attn_gain = jnp.sum(grad_attn_in * normed_one, axis=0)
    grad_normed_one = grad_attn_in * attn_gain.astype(jnp.float32)
    grad_input = grad_middle + scale_one * (
        grad_normed_one
        - normed_one * jnp.mean(grad_normed_one * normed_one, axis=-1, keepdims=True)
    )
    return (
        grad_input,
        (
            grad_attn_gain,
            grad_query,
            grad_key,
            grad_value,
            grad_out,
            grad_mlp_gain,
            grad_gate,
            grad_up,
            grad_down,
        ),
    )


def fetch_fsdp(shards, layer_idx):
    return (
        lax.all_gather(shards[1][layer_idx], "fsdp", axis=0, tiled=True),
        lax.all_gather(shards[2][layer_idx], "fsdp", axis=0, tiled=True),
        lax.all_gather(shards[3][layer_idx], "fsdp", axis=0, tiled=True),
        lax.all_gather(shards[4][layer_idx], "fsdp", axis=1, tiled=True),
        lax.all_gather(shards[6][layer_idx], "fsdp", axis=0, tiled=True),
        lax.all_gather(shards[7][layer_idx], "fsdp", axis=0, tiled=True),
        lax.all_gather(shards[8][layer_idx], "fsdp", axis=1, tiled=True),
        lax.all_gather(shards[0][layer_idx], "fsdp", axis=0, tiled=True),
        lax.all_gather(shards[5][layer_idx], "fsdp", axis=0, tiled=True),
    )


def fetch_fsdp_back(shards, layer_idx):
    return (
        lax.all_gather(shards[1][layer_idx], "fsdp", axis=0, tiled=True),
        lax.all_gather(shards[2][layer_idx], "fsdp", axis=0, tiled=True),
        lax.all_gather(shards[3][layer_idx], "fsdp", axis=0, tiled=True),
        lax.all_gather(shards[4][layer_idx], "fsdp", axis=1, tiled=True),
        lax.all_gather(shards[6][layer_idx], "fsdp", axis=0, tiled=True),
        lax.all_gather(shards[7][layer_idx], "fsdp", axis=0, tiled=True),
        lax.all_gather(shards[8][layer_idx], "fsdp", axis=1, tiled=True),
        lax.all_gather(shards[0][layer_idx], "fsdp", axis=0, tiled=True),
        lax.all_gather(shards[5][layer_idx], "fsdp", axis=0, tiled=True),
    )


def arrange(matrices, pieces):
    return (
        pieces[7],
        matrices[0],
        matrices[1],
        matrices[2],
        matrices[3],
        pieces[8],
        matrices[4],
        matrices[5],
        matrices[6],
    )


def body(
    tokens,
    lengths,
    cotangent,
    attn_gain,
    w_query,
    w_key,
    w_value,
    w_out,
    mlp_gain,
    w_gate,
    w_up,
    w_down,
):
    shards = (attn_gain, w_query, w_key, w_value, w_out, mlp_gain, w_gate, w_up, w_down)

    def spread(rows_in):
        return rows_in

    def settle(terms_in):
        return terms_in

    block_lengths = lax.dynamic_slice_in_dim(lengths, lax.axis_index("dp"), 1, 0)
    allowed, cosine, sine_tab = jax.vmap(partial(layout, rows_here=tokens.shape[0]))(block_lengths)
    cosine = from_blocks(cosine)
    sine_tab = from_blocks(sine_tab)
    stream = tokens.astype(jnp.float32)
    weights_kept = []
    layer_idx = 0
    pieces = fetch_fsdp(shards, layer_idx)
    weights = arrange(
        (
            lax.all_gather(pieces[0], "dp", axis=1, tiled=True),
            lax.all_gather(pieces[1], "dp", axis=1, tiled=True),
            lax.all_gather(pieces[2], "dp", axis=1, tiled=True),
            lax.all_gather(pieces[3], "dp", axis=0, tiled=True),
            lax.all_gather(pieces[4], "dp", axis=1, tiled=True),
            lax.all_gather(pieces[5], "dp", axis=1, tiled=True),
            lax.all_gather(pieces[6], "dp", axis=0, tiled=True),
        ),
        pieces,
    )
    weights_kept.append(weights)
    inputs_kept = [stream]
    stream, _ = layer_forward(stream, weights, allowed, cosine, sine_tab, spread, settle)
    output = stream.astype(jnp.bfloat16)
    grad_stream = cotangent.astype(jnp.float32)
    grads_by_layer = [None] * LAYERS
    for layer_idx in reversed(range(LAYERS)):
        pieces = fetch_fsdp_back(shards, layer_idx)
        weights = arrange(
            (
                lax.all_gather(pieces[0], "dp", axis=1, tiled=True),
                lax.all_gather(pieces[1], "dp", axis=1, tiled=True),
                lax.all_gather(pieces[2], "dp", axis=1, tiled=True),
                lax.all_gather(pieces[3], "dp", axis=0, tiled=True),
                lax.all_gather(pieces[4], "dp", axis=1, tiled=True),
                lax.all_gather(pieces[5], "dp", axis=1, tiled=True),
                lax.all_gather(pieces[6], "dp", axis=0, tiled=True),
            ),
            pieces,
        )
        grad_stream, terms = layer_backward(
            inputs_kept[layer_idx], weights, allowed, cosine, sine_tab, grad_stream, spread, settle
        )
        gains = lax.psum((terms[0], terms[5]), "dp")
        owned = (
            lax.psum_scatter(
                lax.psum_scatter(
                    terms[1].astype(jnp.bfloat16), "dp", scatter_dimension=1, tiled=True
                ),
                "fsdp",
                scatter_dimension=0,
                tiled=True,
            ).astype(jnp.float32),
            lax.psum_scatter(
                lax.psum_scatter(
                    terms[2].astype(jnp.bfloat16), "dp", scatter_dimension=1, tiled=True
                ),
                "fsdp",
                scatter_dimension=0,
                tiled=True,
            ).astype(jnp.float32),
            lax.psum_scatter(
                lax.psum_scatter(
                    terms[3].astype(jnp.bfloat16), "dp", scatter_dimension=1, tiled=True
                ),
                "fsdp",
                scatter_dimension=0,
                tiled=True,
            ).astype(jnp.float32),
            lax.psum_scatter(
                lax.psum_scatter(
                    terms[4].astype(jnp.bfloat16), "dp", scatter_dimension=0, tiled=True
                ),
                "fsdp",
                scatter_dimension=1,
                tiled=True,
            ).astype(jnp.float32),
            lax.psum_scatter(
                lax.psum_scatter(
                    terms[6].astype(jnp.bfloat16), "dp", scatter_dimension=1, tiled=True
                ),
                "fsdp",
                scatter_dimension=0,
                tiled=True,
            ).astype(jnp.float32),
            lax.psum_scatter(
                lax.psum_scatter(
                    terms[7].astype(jnp.bfloat16), "dp", scatter_dimension=1, tiled=True
                ),
                "fsdp",
                scatter_dimension=0,
                tiled=True,
            ).astype(jnp.float32),
            lax.psum_scatter(
                lax.psum_scatter(
                    terms[8].astype(jnp.bfloat16), "dp", scatter_dimension=0, tiled=True
                ),
                "fsdp",
                scatter_dimension=1,
                tiled=True,
            ).astype(jnp.float32),
            lax.psum_scatter(
                gains[0].astype(jnp.bfloat16), "fsdp", scatter_dimension=0, tiled=True
            ).astype(jnp.float32),
            lax.psum_scatter(
                gains[1].astype(jnp.bfloat16), "fsdp", scatter_dimension=0, tiled=True
            ).astype(jnp.float32),
        )
        grads_by_layer[layer_idx] = arrange(owned, owned)
    stacked = tuple((jnp.stack([grads_by_layer[0][slot_idx]]) for slot_idx in range(9)))
    return (output, grad_stream) + stacked


def solution(mesh):
    placed = (
        P(("fsdp", "dp"), None),
        P("fsdp", None),
        P(("fsdp", "dp"), None),
        P(None, "fsdp"),
        P(None, "fsdp", "dp"),
        P(None, "fsdp", "dp"),
        P(None, "fsdp", "dp"),
        P(None, "dp", "fsdp"),
        P(None, "fsdp"),
        P(None, "fsdp", "dp"),
        P(None, "fsdp", "dp"),
        P(None, "dp", "fsdp"),
    )
    return jax.shard_map(
        body,
        mesh=mesh,
        in_specs=placed,
        out_specs=(
            P(("fsdp", "dp"), None),
            P(("fsdp", "dp"), None),
            P(None, "fsdp"),
            P(None, "fsdp", "dp"),
            P(None, "fsdp", "dp"),
            P(None, "fsdp", "dp"),
            P(None, "dp", "fsdp"),
            P(None, "fsdp"),
            P(None, "fsdp", "dp"),
            P(None, "fsdp", "dp"),
            P(None, "dp", "fsdp"),
        ),
        check_vma=False,
    )
```

profile of v0, /device:TPU:8, one launch (start us, length us, event | category | flops | bytes accessed | tf_op | source)
XLA Modules:
  0.0 2371.1 jit_solution(4178363083196030990)
XLA Ops:
  47.3 17.2 all-gather.37.cloned.1.call-done
  64.6 34.0 %all-gather.45.cloned.1.call-done = bf16[1,1536,1024]{2,1,0:T(8,128)(2,1)} async-done(((bf16[1,192,1024]{2,1,0:T(8,128)(2,1)}), bf16[1,1536,1024]{2,1,0:T(8,128)(2,1)}) %all-gather.45.cloned.1.call-update) | async-done | bytes 3145744 | tf_op jit(solution)/shard_map/all_gather | solution.py:276
  98.7 33.9 %all-gather.49.cloned.1.call-done = bf16[1,1024,1536]{1,2,0:T(8,128)(2,1)} async-done(((bf16[1,1024,192]{1,2,0:T(8,128)(2,1)}), bf16[1,1024,1536]{1,2,0:T(8,128)(2,1)}) %all-gather.49.cloned.1.call-update) | async-done | bytes 3145744 | tf_op jit(solution)/shard_map/all_gather | solution.py:277
  132.7 33.9 %all-gather.41.cloned.1.call-done = bf16[1,1536,1024]{2,1,0:T(8,128)(2,1)} async-done(((bf16[1,192,1024]{2,1,0:T(8,128)(2,1)}), bf16[1,1536,1024]{2,1,0:T(8,128)(2,1)}) %all-gather.41.cloned.1.call-update) | async-done | bytes 3145744 | tf_op jit(solution)/shard_map/all_gather | solution.py:275
  183.4 33.6 %all-gather.29.cloned.1.call-done = bf16[1,1536,768]{1,2,0:T(8,128)(2,1)} async-done(((bf16[1,1536,192]{1,2,0:T(8,128)(2,1)}), bf16[1,1536,768]{1,2,0:T(8,128)(2,1)}) %all-gather.29.cloned.1.call-update) | async-done | bytes 2359312 | tf_op jit(solution)/shard_map/all_gather | solution.py:345
  219.8 48.2 %all-gather.31.cloned.1.call-done = bf16[1,1536,768]{1,2,0:T(8,128)(2,1)} async-done(((bf16[1,1536,192]{1,2,0:T(8,128)(2,1)}), bf16[1,1536,768]{1,2,0:T(8,128)(2,1)}) %all-gather.31.cloned.1.call-update) | async-done | bytes 2359312 | tf_op jit(solution)/shard_map/all_gather | solution.py:344
  270.5 86.3 %all-gather.35.cloned.1.call-done = bf16[1,1536,1536]{2,1,0:T(8,128)(2,1)} async-done(((bf16[1,1536,384]{2,1,0:T(8,128)(2,1)}), bf16[1,1536,1536]{2,1,0:T(8,128)(2,1)}) %all-gather.35.cloned.1.call-update) | async-done | bytes 4718608 | tf_op jit(solution)/shard_map/all_gather | solution.py:343
  362.2 84.0 %all-gather.39.cloned.1.call-done = bf16[1,1536,1536]{1,2,0:T(8,128)(2,1)} async-done(((bf16[1,384,1536]{1,2,0:T(8,128)(2,1)}), bf16[1,1536,1536]{1,2,0:T(8,128)(2,1)}) %all-gather.39.cloned.1.call-update) | async-done | bytes 4718608 | tf_op jit(solution)/shard_map/all_gather | solution.py:346
  451.1 212.7 %all-gather.47.cloned.1.call-done = bf16[1,1536,4096]{2,1,0:T(8,128)(2,1)} async-done(((bf16[1,1536,1024]{2,1,0:T(8,128)(2,1)}), bf16[1,1536,4096]{2,1,0:T(8,128)(2,1)}) %all-gather.47.cloned.1.call-update) | async-done | bytes 12582928 | tf_op jit(solution)/shard_map/all_gather | solution.py:348
  671.5 210.3 %all-gather.51.cloned.1.call-done = bf16[1,4096,1536]{1,2,0:T(8,128)(2,1)} async-done(((bf16[1,1024,1536]{1,2,0:T(8,128)(2,1)}), bf16[1,4096,1536]{1,2,0:T(8,128)(2,1)}) %all-gather.51.cloned.1.call-update) | async-done | bytes 12582928 | tf_op jit(solution)/shard_map/all_gather | solution.py:349
  889.5 210.1 %all-gather.43.cloned.1.call-done = bf16[1,1536,4096]{2,1,0:T(8,128)(2,1)} async-done(((bf16[1,1536,1024]{2,1,0:T(8,128)(2,1)}), bf16[1,1536,4096]{2,1,0:T(8,128)(2,1)}) %all-gather.43.cloned.1.call-update) | async-done | bytes 12582928 | tf_op jit(solution)/shard_map/all_gather | solution.py:347
  1188.3 47.0 %reduce-scatter.27.cloned.1.call-done = bf16[1536,192]{0,1:T(8,128)(2,1)} async-done(((bf16[1536,768]{0,1:T(8,128)(2,1)}), bf16[1536,192]{0,1:T(8,128)(2,1)}) %reduce-scatter.27.cloned.1.call-update) | async-done | bytes 589840 | tf_op jit(solution)/shard_map/reduce_scatter | solution.py:387
  1237.6 85.2 %reduce-scatter.31.cloned.1.call-done = bf16[384,1536]{1,0:T(8,128)(2,1)} async-done(((bf16[1536,1536]{1,0:T(8,128)(2,1)}), bf16[384,1536]{1,0:T(8,128)(2,1)}) %reduce-scatter.31.cloned.1.call-update) | async-done | bytes 1179664 | tf_op jit(solution)/shard_map/reduce_scatter | solution.py:403
  1325.3 85.5 %reduce-scatter.43.cloned.1.call-done = bf16[384,1536]{1,0:T(8,128)(2,1)} async-done(((bf16[1536,1536]{1,0:T(8,128)(2,1)}), bf16[384,1536]{1,0:T(8,128)(2,1)}) %reduce-scatter.43.cloned.1.call-update) | async-done | bytes 1179664
  1413.3 212.2 %reduce-scatter.41.cloned.1.call-done = bf16[1024,1536]{1,0:T(8,128)(2,1)} async-done(((bf16[4096,1536]{1,0:T(8,128)(2,1)}), bf16[1024,1536]{1,0:T(8,128)(2,1)}) %reduce-scatter.41.cloned.1.call-update) | async-done | bytes 3145744 | tf_op jit(solution)/shard_map/reduce_scatter | solution.py:427
  1630.2 210.4 %reduce-scatter.33.cloned.1.call-done = bf16[1536,1024]{1,0:T(8,128)(2,1)} async-done(((bf16[1536,4096]{1,0:T(8,128)(2,1)}), bf16[1536,1024]{1,0:T(8,128)(2,1)}) %reduce-scatter.33.cloned.1.call-update) | async-done | bytes 3145744 | tf_op jit(solution)/shard_map/reduce_scatter | solution.py:411
  1840.7 215.2 %reduce-scatter.37.cloned.1.call-done = bf16[1536,1024]{1,0:T(8,128)(2,1)} async-done(((bf16[1536,4096]{1,0:T(8,128)(2,1)}), bf16[1536,1024]{1,0:T(8,128)(2,1)}) %reduce-scatter.37.cloned.1.call-update) | async-done | bytes 3145744 | tf_op jit(solution)/shard_map/reduce_scatter | solution.py:419
  2064.0 15.2 all-reduce.4
  2105.9 28.4 %reduce-scatter.45.cloned.1.call-done = bf16[192,192]{1,0:T(8,128)(2,1)} async-done(((bf16[1536,192]{1,0:T(8,128)(2,1)}), bf16[192,192]{1,0:T(8,128)(2,1)}) %reduce-scatter.45.cloned.1.call-update) | async-done | bytes 73744
  2136.1 38.2 %reduce-scatter.49.cloned.1.call-done = bf16[192,384]{1,0:T(8,128)(2,1)} async-done(((bf16[1536,384]{1,0:T(8,128)(2,1)}), bf16[192,384]{1,0:T(8,128)(2,1)}) %reduce-scatter.49.cloned.1.call-update) | async-done | bytes 147472
  2176.2 38.0 %reduce-scatter.25.cloned.1.call-done = bf16[192,384]{1,0:T(8,128)(2,1)} async-done(((bf16[1536,384]{1,0:T(8,128)(2,1)}), bf16[192,384]{1,0:T(8,128)(2,1)}) %reduce-scatter.25.cloned.1.call-update) | async-done | bytes 147472 | tf_op jit(solution)/shard_map/reduce_scatter | solution.py:378
  2215.9 47.7 %reduce-scatter.51.cloned.1.call-done = bf16[192,1024]{1,0:T(8,128)(2,1)} async-done(((bf16[1536,1024]{1,0:T(8,128)(2,1)}), bf16[192,1024]{1,0:T(8,128)(2,1)}) %reduce-scatter.51.cloned.1.call-update) | async-done | bytes 393232
  2266.0 47.0 %reduce-scatter.35.cloned.1.call-done = bf16[192,1024]{1,0:T(8,128)(2,1)} async-done(((bf16[1536,1024]{1,0:T(8,128)(2,1)}), bf16[192,1024]{1,0:T(8,128)(2,1)}) %reduce-scatter.35.cloned.1.call-update) | async-done | bytes 393232 | tf_op jit(solution)/shard_map/reduce_scatter | solution.py:410
  2315.0 47.4 %reduce-scatter.39.cloned.1.call-done = bf16[192,1024]{1,0:T(8,128)(2,1)} async-done(((bf16[1536,1024]{1,0:T(8,128)(2,1)}), bf16[192,1024]{1,0:T(8,128)(2,1)}) %reduce-scatter.39.cloned.1.call-update) | async-done | bytes 393232 | tf_op jit(solution)/shard_map/reduce_scatter | solution.py:418
  (241 shorter events, 233.1 us)
Async XLA Ops:
  8.7 90.0 %all-gather.45.cloned.1.call-start = ((), (), s32[]{:S(2)}) async-start(), calls=%async_computation.31 | async-start | bytes 3538944 | tf_op jit(solution)/shard_map/all_gather | solution.py:276
  9.4 123.2 %all-gather.49.cloned.1.call-start = ((), (), s32[]{:S(2)}) async-start(), calls=%async_computation.33 | async-start | bytes 3538944 | tf_op jit(solution)/shard_map/all_gather | solution.py:277
  10.0 156.6 %all-gather.41.cloned.1.call-start = ((), (), s32[]{:S(2)}) async-start(), calls=%async_computation.29 | async-start | bytes 3538944 | tf_op jit(solution)/shard_map/all_gather | solution.py:275
  10.6 206.5 %all-gather.29.cloned.1.call-start = ((), (), s32[]{:S(2)}) async-start(), calls=%async_computation.23 | async-start | bytes 2949120 | tf_op jit(solution)/shard_map/all_gather | solution.py:345
  29.0 239.0 %all-gather.31.cloned.1.call-start = ((), (), s32[]{:S(2)}) async-start(), calls=%async_computation.24 | async-start | bytes 2949120 | tf_op jit(solution)/shard_map/all_gather | solution.py:344
  46.5 310.3 %all-gather.35.cloned.1.call-start = ((), (), s32[]{:S(2)}) async-start(), calls=%async_computation.26 | async-start | bytes 5898240 | tf_op jit(solution)/shard_map/all_gather | solution.py:343
  47.3 399.0 %all-gather.39.cloned.1.call-start = ((), (), s32[]{:S(2)}) async-start(), calls=%async_computation.28 | async-start | bytes 5898240 | tf_op jit(solution)/shard_map/all_gather | solution.py:346
  64.6 599.2 %all-gather.47.cloned.1.call-start = ((), (), s32[]{:S(2)}) async-start(), calls=%async_computation.32 | async-start | bytes 15728640 | tf_op jit(solution)/shard_map/all_gather | solution.py:348
  98.7 783.1 %all-gather.51.cloned.1.call-start = ((), (), s32[]{:S(2)}) async-start(), calls=%async_computation.34 | async-start | bytes 15728640 | tf_op jit(solution)/shard_map/all_gather | solution.py:349
  132.7 966.9 %all-gather.43.cloned.1.call-start = ((), (), s32[]{:S(2)}) async-start(), calls=%async_computation.30 | async-start | bytes 15728640 | tf_op jit(solution)/shard_map/all_gather | solution.py:347
  166.6 1019.4 %reduce-scatter.29.cloned.1.call-start = ((), (), s32[]{:S(2)}) async-start(), calls=%async_computation.16 | async-start | bytes 2949120 | tf_op jit(solution)/shard_map/reduce_scatter | solution.py:395
  1137.6 97.6 %reduce-scatter.27.cloned.1.call-start = ((), (), s32[]{:S(2)}) async-start(), calls=%async_computation.15 | async-start | bytes 2949120 | tf_op jit(solution)/shard_map/reduce_scatter | solution.py:387
  1146.2 176.7 %reduce-scatter.31.cloned.1.call-start = ((), (), s32[]{:S(2)}) async-start(), calls=%async_computation.17 | async-start | bytes 5898240 | tf_op jit(solution)/shard_map/reduce_scatter | solution.py:403
  1149.8 261.1 %reduce-scatter.43.cloned.1.call-start = ((), (), s32[]{:S(2)}) async-start(), calls=%async_computation.35 | async-start | bytes 5898240
  1161.5 464.0 %reduce-scatter.41.cloned.1.call-start = ((), (), s32[]{:S(2)}) async-start(), calls=%async_computation.22 | async-start | bytes 15728640 | tf_op jit(solution)/shard_map/reduce_scatter | solution.py:427
  1169.2 671.4 %reduce-scatter.33.cloned.1.call-start = ((), (), s32[]{:S(2)}) async-start(), calls=%async_computation.18 | async-start | bytes 15728640 | tf_op jit(solution)/shard_map/reduce_scatter | solution.py:411
  1177.8 878.0 %reduce-scatter.37.cloned.1.call-start = ((), (), s32[]{:S(2)}) async-start(), calls=%async_computation.20 | async-start | bytes 15728640 | tf_op jit(solution)/shard_map/reduce_scatter | solution.py:419
  1185.6 918.5 %reduce-scatter.47.cloned.1.call-start = ((), (), s32[]{:S(2)}) async-start(), calls=%async_computation.37 | async-start | bytes 884736
  1188.3 946.0 %reduce-scatter.45.cloned.1.call-start = ((), (), s32[]{:S(2)}) async-start(), calls=%async_computation.36 | async-start | bytes 884736
  1237.5 936.7 %reduce-scatter.49.cloned.1.call-start = ((), (), s32[]{:S(2)}) async-start(), calls=%async_computation.38 | async-start | bytes 1327104
  1325.2 889.0 %reduce-scatter.25.cloned.1.call-start = ((), (), s32[]{:S(2)}) async-start(), calls=%async_computation.14 | async-start | bytes 1327104 | tf_op jit(solution)/shard_map/reduce_scatter | solution.py:378
  1413.2 850.4 %reduce-scatter.51.cloned.1.call-start = ((), (), s32[]{:S(2)}) async-start(), calls=%async_computation.39 | async-start | bytes 3538944
  1630.1 682.9 %reduce-scatter.35.cloned.1.call-start = ((), (), s32[]{:S(2)}) async-start(), calls=%async_computation.19 | async-start | bytes 3538944 | tf_op jit(solution)/shard_map/reduce_scatter | solution.py:410
  1840.6 521.7 %reduce-scatter.39.cloned.1.call-start = ((), (), s32[]{:S(2)}) async-start(), calls=%async_computation.21 | async-start | bytes 3538944 | tf_op jit(solution)/shard_map/reduce_scatter | solution.py:418
  (47 other events, 2676.4 us)
Sparse Core Ops, SparseCore 0:
  66.5 32.1 all-gather.44
  100.4 32.1 all-gather.48
  134.4 32.1 all-gather.40
  168.6 48.4 all-gather.28
  219.2 48.7 all-gather.30
  269.6 87.2 all-gather.34
  358.5 87.7 all-gather.38
  447.7 216.0 all-gather.46
  665.4 216.3 all-gather.50
  883.2 216.3 all-gather.42
  1137.8 48.1 reduce-scatter.28
  1188.2 47.0 reduce-scatter.26
  1237.4 85.3 reduce-scatter.30
  1325.0 85.7 reduce-scatter.42
  1413.0 212.3 reduce-scatter.40
  1627.7 212.8 reduce-scatter.32
  1843.0 212.8 reduce-scatter.36
  2059.4 36.1 reduce-scatter.46
  2099.4 34.8 reduce-scatter.44
  2137.5 36.6 reduce-scatter.48
  2177.5 36.6 reduce-scatter.24
  2217.5 46.0 reduce-scatter.50
  2266.9 46.0 reduce-scatter.34
  2316.3 46.0 reduce-scatter.38
  (2 shorter events, 52.6 us)
where the time goes:
time: 2380 us; the launch traced here: 2370 us
  waiting for transfers between devices  2110 us (89%)
  matrix products  114 us (5%)
  blocking collectives  70.6 us (3%)
  local copies, waits for them, and re-layouts  45.8 us (2%)
    reduce_scatter x1, waiting for transfers between devices, body(): lax.psum_scatter(terms[7].astype(jnp.bfloat16), 'dp', scatter_dimension=1...  215 us
    all_gather x1, waiting for transfers between devices, body(): lax.all_gather(pieces[5], 'dp', axis=1, tiled=True)  213 us
    reduce_scatter x1, waiting for transfers between devices, body(): lax.psum_scatter(terms[8].astype(jnp.bfloat16), 'dp', scatter_dimension=0...  212 us
    reduce_scatter x1, waiting for transfers between devices, body(): lax.psum_scatter(terms[6].astype(jnp.bfloat16), 'dp', scatter_dimension=1...  210 us
    all_gather x1, waiting for transfers between devices, body(): lax.all_gather(pieces[6], 'dp', axis=0, tiled=True)  210 us
    all_gather x1, waiting for transfers between devices, body(): lax.all_gather(pieces[4], 'dp', axis=1, tiled=True)  210 us
    unnamed x31, waiting for transfers between devices  204 us
    all_gather x1, waiting for transfers between devices, body(): lax.all_gather(pieces[0], 'dp', axis=1, tiled=True)  86.3 us
  transfers between devices with their start and end apart: 26, of which 24 were waited for; matrix products, arithmetic and copies ran while one was open for 5% of the time, Pallas kernels for 0%

commit v1 on v0

--- a/solution.py
+++ b/solution.py
@@ -325,31 +325,21 @@
     shards = (attn_gain, w_query, w_key, w_value, w_out, mlp_gain, w_gate, w_up, w_down)
 
     def spread(rows_in):
-        return rows_in
+        return lax.all_gather(rows_in, "dp", axis=0, tiled=True)
 
     def settle(terms_in):
-        return terms_in
-
-    block_lengths = lax.dynamic_slice_in_dim(lengths, lax.axis_index("dp"), 1, 0)
-    allowed, cosine, sine_tab = jax.vmap(partial(layout, rows_here=tokens.shape[0]))(block_lengths)
+        return lax.psum_scatter(
+            terms_in.astype(jnp.bfloat16), "dp", scatter_dimension=0, tiled=True
+        ).astype(jnp.float32)
+
+    allowed, cosine, sine_tab = jax.vmap(partial(layout, rows_here=tokens.shape[0]))(lengths)
     cosine = from_blocks(cosine)
     sine_tab = from_blocks(sine_tab)
     stream = tokens.astype(jnp.float32)
     weights_kept = []
     layer_idx = 0
     pieces = fetch_fsdp(shards, layer_idx)
-    weights = arrange(
-        (
-            lax.all_gather(pieces[0], "dp", axis=1, tiled=True),
-            lax.all_gather(pieces[1], "dp", axis=1, tiled=True),
-            lax.all_gather(pieces[2], "dp", axis=1, tiled=True),
-            lax.all_gather(pieces[3], "dp", axis=0, tiled=True),
-            lax.all_gather(pieces[4], "dp", axis=1, tiled=True),
-            lax.all_gather(pieces[5], "dp", axis=1, tiled=True),
-            lax.all_gather(pieces[6], "dp", axis=0, tiled=True),
-        ),
-        pieces,
-    )
+    weights = arrange(pieces[:7], pieces)
     weights_kept.append(weights)
     inputs_kept = [stream]
     stream, _ = layer_forward(stream, weights, allowed, cosine, sine_tab, spread, settle)
@@ -357,76 +347,50 @@
     grad_stream = cotangent.astype(jnp.float32)
     grads_by_layer = [None] * LAYERS
     for layer_idx in reversed(range(LAYERS)):
-        pieces = fetch_fsdp_back(shards, layer_idx)
-        weights = arrange(
-            (
-                lax.all_gather(pieces[0], "dp", axis=1, tiled=True),
-                lax.all_gather(pieces[1], "dp", axis=1, tiled=True),
-                lax.all_gather(pieces[2], "dp", axis=1, tiled=True),
-                lax.all_gather(pieces[3], "dp", axis=0, tiled=True),
-                lax.all_gather(pieces[4], "dp", axis=1, tiled=True),
-                lax.all_gather(pieces[5], "dp", axis=1, tiled=True),
-                lax.all_gather(pieces[6], "dp", axis=0, tiled=True),
-            ),
-            pieces,
-        )
+        weights = weights_kept[layer_idx]
         grad_stream, terms = layer_backward(
             inputs_kept[layer_idx], weights, allowed, cosine, sine_tab, grad_stream, spread, settle
         )
         gains = lax.psum((terms[0], terms[5]), "dp")
         owned = (
             lax.psum_scatter(
-                lax.psum_scatter(
-                    terms[1].astype(jnp.bfloat16), "dp", scatter_dimension=1, tiled=True
-                ),
+                terms[1].astype(jnp.bfloat16),
                 "fsdp",
                 scatter_dimension=0,
                 tiled=True,
             ).astype(jnp.float32),
             lax.psum_scatter(
-                lax.psum_scatter(
-                    terms[2].astype(jnp.bfloat16), "dp", scatter_dimension=1, tiled=True
-                ),
+                terms[2].astype(jnp.bfloat16),
                 "fsdp",
                 scatter_dimension=0,
                 tiled=True,
             ).astype(jnp.float32),
             lax.psum_scatter(
-                lax.psum_scatter(
-                    terms[3].astype(jnp.bfloat16), "dp", scatter_dimension=1, tiled=True
-                ),
+                terms[3].astype(jnp.bfloat16),
                 "fsdp",
                 scatter_dimension=0,
                 tiled=True,
             ).astype(jnp.float32),
             lax.psum_scatter(
-                lax.psum_scatter(
-                    terms[4].astype(jnp.bfloat16), "dp", scatter_dimension=0, tiled=True
-                ),
+                terms[4].astype(jnp.bfloat16),
                 "fsdp",
                 scatter_dimension=1,
                 tiled=True,
             ).astype(jnp.float32),
             lax.psum_scatter(
-                lax.psum_scatter(
-                    terms[6].astype(jnp.bfloat16), "dp", scatter_dimension=1, tiled=True
-                ),
+                terms[6].astype(jnp.bfloat16),
                 "fsdp",
                 scatter_dimension=0,
                 tiled=True,
             ).astype(jnp.float32),
             lax.psum_scatter(
-                lax.psum_scatter(
-                    terms[7].astype(jnp.bfloat16), "dp", scatter_dimension=1, tiled=True
-                ),
+                terms[7].astype(jnp.bfloat16),
                 "fsdp",
                 scatter_dimension=0,
                 tiled=True,
             ).astype(jnp.float32),
             lax.psum_scatter(
-                lax.psum_scatter(
-                    terms[8].astype(jnp.bfloat16), "dp", scatter_dimension=0, tiled=True
-                ),
+                terms[8].astype(jnp.bfloat16),
                 "fsdp",
                 scatter_dimension=1,
                 tiled=True,

time: 2380 us -> 810 us (0.34)
  waiting for transfers between devices: 2110 us -> 604 us
  matrix products: 114 us -> 75.1 us
  local copies, waits for them, and re-layouts: 45.8 us -> 12.8 us
    all_gather x7 -> x4, waiting for transfers between devices: 885 us -> 103 us  [spread(): return lax.all_gather(rows_in, 'dp', axis=0, tiled=True)]
    reduce_scatter x9 -> x11, waiting for transfers between devices: 903 us -> 364 us  [the longest x4 108 us: settle(): lax.psum_scatter(terms_in.astype(jnp.bfloat16), 'dp', scatter_dimension=0...]
    unnamed x31 -> x20, waiting for transfers between devices: 204 us -> 4.21 us
    unnamed x111 -> x96, local copies, waits for them, and re-layouts: 36.6 us -> 4.68 us
  transfers between devices with their start and end apart: 26 -> 20, of which waited for: 24 -> 20; matrix products, arithmetic and copies ran while one was open for 5% -> 11% of each run, Pallas kernels for 0% -> 0%
where the time goes in v1:
time: 810 us; the launch traced here: 806 us
  waiting for transfers between devices  604 us (75%)
  matrix products  75.1 us (9%)
  blocking collectives  63.1 us (8%)
  other arithmetic  32.9 us (4%)
  between operations  16.2 us (2%)
  local copies, waits for them, and re-layouts  12.8 us (2%)
    reduce_scatter x4, waiting for transfers between devices, settle(): lax.psum_scatter(terms_in.astype(jnp.bfloat16), 'dp', scatter_dimension=0...  108 us
    all_gather x4, waiting for transfers between devices, spread(): return lax.all_gather(rows_in, 'dp', axis=0, tiled=True)  103 us
    reduce_scatter x1, waiting for transfers between devices, body(): lax.psum_scatter(terms[7].astype(jnp.bfloat16), 'fsdp', scatter_dimension...  47.5 us
    reduce_scatter x1, waiting for transfers between devices, body(): lax.psum_scatter(terms[6].astype(jnp.bfloat16), 'fsdp', scatter_dimension...  47.3 us
    reduce_scatter x1, waiting for transfers between devices, body(): lax.psum_scatter(terms[4].astype(jnp.bfloat16), 'fsdp', scatter_dimension...  38.2 us
    reduce_scatter x1, waiting for transfers between devices, body(): lax.psum_scatter(terms[1].astype(jnp.bfloat16), 'fsdp', scatter_dimension...  38.2 us
    reduce_scatter x1, waiting for transfers between devices, body(): lax.psum_scatter(terms[2].astype(jnp.bfloat16), 'fsdp', scatter_dimension...  37 us
    reduce_scatter x1, waiting for transfers between devices, body(): lax.psum_scatter(terms[3].astype(jnp.bfloat16), 'fsdp', scatter_dimension...  36 us
  transfers between devices with their start and end apart: 20, of which 20 were waited for; matrix products, arithmetic and copies ran while one was open for 11% of the time, Pallas kernels for 0%

profile of v1, /device:TPU:8, one launch (start us, length us, event | category | flops | bytes accessed | tf_op | source)
XLA Modules:
  0.0 806.0 jit_solution(16388538002550053874)
XLA Ops:
  12.3 14.5 %all-reduce.6 = (bf16[1536]{0:T(1024)(128)(2,1)S(1)}, bf16[1536]{0:T(1024)(128)(2,1)}) all-reduce(bf16[1536]{0:T(1024)(128)(2,1)S(1)} %dynamic-update-slice, bf16[1536]{0:T(1024)(128)(2,1)S(1)} %dynamic-update-slice.1), channel_id=2, replica_groups=mesh['fsdp'=8,'dp'=4] {'fsdp'}, use_global_device_ids=true, to_apply=%add | all-reduce | flops 3072 | bytes 12288
  30.9 9.4 %all-gather.2 = bf16[1,1536,192]{2,1,0:T(8,128)(2,1)S(1)} all-gather(bf16[1,192,192]{2,1,0:T(8,128)(2,1)S(1)} %copy-done.29), channel_id=4, replica_groups=mesh['fsdp'=8,'dp'=4] {'fsdp'}, dimensions={1}, use_global_device_ids=true | all-gather | bytes 663552 | tf_op jit(solution)/shard_map/all_gather | solution.py:272
  40.4 10.3 %all-gather.1 = bf16[1,1536,192]{2,1,0:T(8,128)(2,1)S(1)} all-gather(bf16[1,192,192]{2,1,0:T(8,128)(2,1)S(1)} %copy-done.30), channel_id=3, replica_groups=mesh['fsdp'=8,'dp'=4] {'fsdp'}, dimensions={1}, use_global_device_ids=true | all-gather | bytes 663552 | tf_op jit(solution)/shard_map/all_gather | solution.py:273
  51.8 12.6 %all-gather.19.cloned.1.call-done = bf16[512,1536]{1,0:T(8,128)(2,1)} async-done(((bf16[128,1536]{1,0:T(8,128)(2,1)}), bf16[512,1536]{1,0:T(8,128)(2,1)}) %all-gather.19.cloned.1.call-update) | async-done | bytes 1572880 | tf_op jit(solution)/shard_map/all_gather | solution.py:328
  68.9 21.1 %all-gather.27.cloned.1.call-done = bf16[1,1536,384]{2,1,0:T(8,128)(2,1)} async-done(((bf16[1,192,384]{2,1,0:T(8,128)(2,1)}), bf16[1,1536,384]{2,1,0:T(8,128)(2,1)}) %all-gather.27.cloned.1.call-update) | async-done | bytes 1179664 | tf_op jit(solution)/shard_map/all_gather | solution.py:271
  95.0 20.8 %all-gather.29.cloned.1.call-done = bf16[1,384,1536]{1,2,0:T(8,128)(2,1)} async-done(((bf16[1,384,192]{1,2,0:T(8,128)(2,1)}), bf16[1,384,1536]{1,2,0:T(8,128)(2,1)}) %all-gather.29.cloned.1.call-update) | async-done | bytes 1179664 | tf_op jit(solution)/shard_map/all_gather | solution.py:274
  120.0 33.6 %reduce-scatter.12.cloned.1.call-done = bf16[128,1536]{1,0:T(8,128)(2,1)} async-done(((bf16[512,1536]{1,0:T(8,128)(2,1)}), bf16[128,1536]{1,0:T(8,128)(2,1)}) %reduce-scatter.12.cloned.1.call-update) | async-done | bytes 393232 | tf_op jit(solution)/shard_map/reduce_scatter | solution.py:331
  159.2 28.5 %all-gather.33.cloned.1.call-done = bf16[1,1536,1024]{2,1,0:T(8,128)(2,1)} async-done(((bf16[1,192,1024]{2,1,0:T(8,128)(2,1)}), bf16[1,1536,1024]{2,1,0:T(8,128)(2,1)}) %all-gather.33.cloned.1.call-update) | async-done | bytes 3145744 | tf_op jit(solution)/shard_map/all_gather | solution.py:276
  187.7 38.2 %all-gather.21.cloned.1.call-done = bf16[512,1536]{1,0:T(8,128)(2,1)} async-done(((bf16[128,1536]{1,0:T(8,128)(2,1)}), bf16[512,1536]{1,0:T(8,128)(2,1)}) %all-gather.21.cloned.1.call-update) | async-done | bytes 1572880 | tf_op jit(solution)/shard_map/all_gather | solution.py:328
  231.4 28.3 %all-gather.31.cloned.1.call-done = bf16[1,1536,1024]{2,1,0:T(8,128)(2,1)} async-done(((bf16[1,192,1024]{2,1,0:T(8,128)(2,1)}), bf16[1,1536,1024]{2,1,0:T(8,128)(2,1)}) %all-gather.31.cloned.1.call-update) | async-done | bytes 3145744 | tf_op jit(solution)/shard_map/all_gather | solution.py:275
  265.2 32.2 %all-gather.23.cloned.1.call-done = bf16[512,1536]{1,0:T(8,128)(2,1)} async-done(((bf16[128,1536]{1,0:T(8,128)(2,1)}), bf16[512,1536]{1,0:T(8,128)(2,1)}) %all-gather.23.cloned.1.call-update) | async-done | bytes 1572880 | tf_op jit(solution)/shard_map/all_gather | solution.py:328
  297.5 33.9 %all-gather.35.cloned.1.call-done = bf16[1,1024,1536]{1,2,0:T(8,128)(2,1)} async-done(((bf16[1,1024,192]{1,2,0:T(8,128)(2,1)}), bf16[1,1024,1536]{1,2,0:T(8,128)(2,1)}) %all-gather.35.cloned.1.call-update) | async-done | bytes 3145744 | tf_op jit(solution)/shard_map/all_gather | solution.py:277
  344.3 34.2 %reduce-scatter.16.cloned.1.call-done = bf16[128,1536]{1,0:T(8,128)(2,1)} async-done(((bf16[512,1536]{1,0:T(8,128)(2,1)}), bf16[128,1536]{1,0:T(8,128)(2,1)}) %reduce-scatter.16.cloned.1.call-update) | async-done | bytes 393232 | tf_op jit(solution)/shard_map/reduce_scatter | solution.py:331
  398.9 20.2 %all-gather.25.cloned.1.call-done = bf16[512,1536]{1,0:T(8,128)(2,1)} async-done(((bf16[128,1536]{1,0:T(8,128)(2,1)}), bf16[512,1536]{1,0:T(8,128)(2,1)}) %all-gather.25.cloned.1.call-update) | async-done | bytes 1572880 | tf_op jit(solution)/shard_map/all_gather | solution.py:328
  456.1 12.1 %reduce-scatter.32.cloned.1.call-done = bf16[1024,192]{0,1:T(8,128)(2,1)} async-done(((bf16[1024,1536]{0,1:T(8,128)(2,1)}), bf16[1024,192]{0,1:T(8,128)(2,1)}) %reduce-scatter.32.cloned.1.call-update) | async-done | bytes 393232 | tf_op jit(solution)/shard_map/reduce_scatter | solution.py:392
  470.2 47.5 %reduce-scatter.30.cloned.1.call-done = bf16[192,1024]{1,0:T(8,128)(2,1)} async-done(((bf16[1536,1024]{1,0:T(8,128)(2,1)}), bf16[192,1024]{1,0:T(8,128)(2,1)}) %reduce-scatter.30.cloned.1.call-update) | async-done | bytes 393232 | tf_op jit(solution)/shard_map/reduce_scatter | solution.py:386
  519.7 47.3 %reduce-scatter.28.cloned.1.call-done = bf16[192,1024]{1,0:T(8,128)(2,1)} async-done(((bf16[1536,1024]{1,0:T(8,128)(2,1)}), bf16[192,1024]{1,0:T(8,128)(2,1)}) %reduce-scatter.28.cloned.1.call-update) | async-done | bytes 393232 | tf_op jit(solution)/shard_map/reduce_scatter | solution.py:380
  569.0 36.0 %reduce-scatter.24.cloned.1.call-done = bf16[192,192]{1,0:T(8,128)(2,1)} async-done(((bf16[1536,192]{1,0:T(8,128)(2,1)}), bf16[192,192]{1,0:T(8,128)(2,1)}) %reduce-scatter.24.cloned.1.call-update) | async-done | bytes 73744 | tf_op jit(solution)/shard_map/reduce_scatter | solution.py:368
  606.6 37.0 %reduce-scatter.22.cloned.1.call-done = bf16[192,192]{1,0:T(8,128)(2,1)} async-done(((bf16[1536,192]{1,0:T(8,128)(2,1)}), bf16[192,192]{1,0:T(8,128)(2,1)}) %reduce-scatter.22.cloned.1.call-update) | async-done | bytes 73744 | tf_op jit(solution)/shard_map/reduce_scatter | solution.py:362
  645.1 38.2 %reduce-scatter.26.cloned.1.call-done = bf16[384,192]{0,1:T(8,128)(2,1)} async-done(((bf16[384,1536]{0,1:T(8,128)(2,1)}), bf16[384,192]{0,1:T(8,128)(2,1)}) %reduce-scatter.26.cloned.1.call-update) | async-done | bytes 147472 | tf_op jit(solution)/shard_map/reduce_scatter | solution.py:374
  685.0 38.2 %reduce-scatter.20.cloned.1.call-done = bf16[192,384]{1,0:T(8,128)(2,1)} async-done(((bf16[1536,384]{1,0:T(8,128)(2,1)}), bf16[192,384]{1,0:T(8,128)(2,1)}) %reduce-scatter.20.cloned.1.call-update) | async-done | bytes 147472 | tf_op jit(solution)/shard_map/reduce_scatter | solution.py:356
  724.8 34.8 %reduce-scatter.18.cloned.1.call-done = bf16[128,1536]{1,0:T(8,128)(2,1)} async-done(((bf16[512,1536]{1,0:T(8,128)(2,1)}), bf16[128,1536]{1,0:T(8,128)(2,1)}) %reduce-scatter.18.cloned.1.call-update) | async-done | bytes 393232 | tf_op jit(solution)/shard_map/reduce_scatter | solution.py:331
  760.9 16.8 %all-reduce.4 = (bf16[1536]{0:T(1024)(128)(2,1)S(1)}, bf16[1536]{0:T(1024)(128)(2,1)S(1)}) all-reduce(f32[1536]{0:T(1024)S(1)} %get-tuple-element.13, f32[1536]{0:T(1024)S(1)} %copy-done.31), channel_id=1, replica_groups=mesh['fsdp'=8,'dp'=4] {'dp'}, use_global_device_ids=true, to_apply=%region_15.16 | all-reduce | flops 3072 | bytes 18432 | tf_op jit(solution)/shard_map/psum | solution.py:354
  777.7 12.0 %all-reduce.5 = (bf16[1536]{0:T(1024)(128)(2,1)S(1)}, bf16[1536]{0:T(1024)(128)(2,1)S(1)}) all-reduce(bf16[1536]{0:T(1024)(128)(2,1)S(1)} %get-tuple-element.15, bf16[1536]{0:T(1024)(128)(2,1)S(1)} %get-tuple-element.16), channel_id=15, replica_groups=mesh['fsdp'=8,'dp'=4] {'fsdp'}, use_global_device_ids=true, to_apply=%region_16.17.clone | all-reduce | flops 3072 | bytes 12288
  (219 shorter events, 132.0 us)
Async XLA Ops:
  7.2 57.2 %all-gather.19.cloned.1.call-start = ((), (), s32[]{:S(2)}) async-start(), calls=%async_computation.11 | async-start | bytes 1966080 | tf_op jit(solution)/shard_map/all_gather | solution.py:328
  28.8 61.2 %all-gather.27.cloned.1.call-start = ((), (), s32[]{:S(2)}) async-start(), calls=%async_computation.26 | async-start | bytes 1327104 | tf_op jit(solution)/shard_map/all_gather | solution.py:271
  29.6 86.2 %all-gather.29.cloned.1.call-start = ((), (), s32[]{:S(2)}) async-start(), calls=%async_computation.27 | async-start | bytes 1327104 | tf_op jit(solution)/shard_map/all_gather | solution.py:274
  30.3 123.3 %reduce-scatter.12.cloned.1.call-start = ((), (), s32[]{:S(2)}) async-start(), calls=%async_computation.12 | async-start | bytes 1966080 | tf_op jit(solution)/shard_map/reduce_scatter | solution.py:331
  119.3 68.4 %all-gather.33.cloned.1.call-start = ((), (), s32[]{:S(2)}) async-start(), calls=%async_computation.29 | async-start | bytes 3538944 | tf_op jit(solution)/shard_map/all_gather | solution.py:276
  119.9 106.0 %all-gather.21.cloned.1.call-start = ((), (), s32[]{:S(2)}) async-start(), calls=%async_computation.13 | async-start | bytes 1966080 | tf_op jit(solution)/shard_map/all_gather | solution.py:328
  156.7 103.0 %all-gather.31.cloned.1.call-start = ((), (), s32[]{:S(2)}) async-start(), calls=%async_computation.28 | async-start | bytes 3538944 | tf_op jit(solution)/shard_map/all_gather | solution.py:275
  157.5 140.0 %all-gather.23.cloned.1.call-start = ((), (), s32[]{:S(2)}) async-start(), calls=%async_computation.15 | async-start | bytes 1966080 | tf_op jit(solution)/shard_map/all_gather | solution.py:328
  158.2 173.1 %all-gather.35.cloned.1.call-start = ((), (), s32[]{:S(2)}) async-start(), calls=%async_computation.30 | async-start | bytes 3538944 | tf_op jit(solution)/shard_map/all_gather | solution.py:277
  158.9 219.5 %reduce-scatter.16.cloned.1.call-start = ((), (), s32[]{:S(2)}) async-start(), calls=%async_computation.16 | async-start | bytes 1966080 | tf_op jit(solution)/shard_map/reduce_scatter | solution.py:331
  344.2 75.0 %all-gather.25.cloned.1.call-start = ((), (), s32[]{:S(2)}) async-start(), calls=%async_computation.17 | async-start | bytes 1966080 | tf_op jit(solution)/shard_map/all_gather | solution.py:328
  382.7 85.6 %reduce-scatter.32.cloned.1.call-start = ((), (), s32[]{:S(2)}) async-start(), calls=%async_computation.25 | async-start | bytes 3538944 | tf_op jit(solution)/shard_map/reduce_scatter | solution.py:392
  388.0 129.7 %reduce-scatter.30.cloned.1.call-start = ((), (), s32[]{:S(2)}) async-start(), calls=%async_computation.24 | async-start | bytes 3538944 | tf_op jit(solution)/shard_map/reduce_scatter | solution.py:386
  393.4 173.7 %reduce-scatter.28.cloned.1.call-start = ((), (), s32[]{:S(2)}) async-start(), calls=%async_computation.23 | async-start | bytes 3538944 | tf_op jit(solution)/shard_map/reduce_scatter | solution.py:380
  398.9 206.2 %reduce-scatter.24.cloned.1.call-start = ((), (), s32[]{:S(2)}) async-start(), calls=%async_computation.21 | async-start | bytes 884736 | tf_op jit(solution)/shard_map/reduce_scatter | solution.py:368
  431.3 212.2 %reduce-scatter.22.cloned.1.call-start = ((), (), s32[]{:S(2)}) async-start(), calls=%async_computation.20 | async-start | bytes 884736 | tf_op jit(solution)/shard_map/reduce_scatter | solution.py:362
  434.5 248.8 %reduce-scatter.26.cloned.1.call-start = ((), (), s32[]{:S(2)}) async-start(), calls=%async_computation.22 | async-start | bytes 1327104 | tf_op jit(solution)/shard_map/reduce_scatter | solution.py:374
  438.3 284.8 %reduce-scatter.20.cloned.1.call-start = ((), (), s32[]{:S(2)}) async-start(), calls=%async_computation.19 | async-start | bytes 1327104 | tf_op jit(solution)/shard_map/reduce_scatter | solution.py:356
  443.7 315.8 %reduce-scatter.18.cloned.1.call-start = ((), (), s32[]{:S(2)}) async-start(), calls=%async_computation.18 | async-start | bytes 1966080 | tf_op jit(solution)/shard_map/reduce_scatter | solution.py:331
  449.3 347.2 %reduce-scatter.14.cloned.1.call-start = ((), (), s32[]{:S(2)}) async-start(), calls=%async_computation.14 | async-start | bytes 1966080 | tf_op jit(solution)/shard_map/reduce_scatter | solution.py:331
  519.7 276.7 %copy-start.7 = (bf16[128,1536]{1,0:T(8,128)(2,1)S(1)}, bf16[128,1536]{1,0:T(8,128)(2,1)}, u32[]{:S(2)}) copy-start(bf16[128,1536]{1,0:T(8,128)(2,1)} %param.14) | copy-start | bytes 1179652
  519.7 276.7 %copy-start.8 = (bf16[128,1536]{1,0:T(8,128)(2,1)S(1)}, bf16[128,1536]{1,0:T(8,128)(2,1)}, u32[]{:S(2)}) copy-start(bf16[128,1536]{1,0:T(8,128)(2,1)} %reduce-scatter.16.cloned.1.call-done) | copy-start | bytes 1179652
  519.7 276.7 %copy-start.33 = (f32[128]{0:T(128)S(1)}, f32[128]{0:T(128)}, u32[]{:S(2)}) copy-start(f32[128]{0:T(128)} %copy-done.32) | copy-start | bytes 1540
  519.7 276.7 %copy-start.39 = (f32[128]{0:T(128)S(1)}, f32[128]{0:T(128)}, u32[]{:S(2)}) copy-start(f32[128]{0:T(128)} %copy-done.38) | copy-start | bytes 1540
  (41 other events, 1179.9 us)
Sparse Core Ops, SparseCore 0:
  28.9 35.3 all-gather.18
  66.2 23.6 all-gather.26
  91.8 23.9 all-gather.28
  119.4 34.0 reduce-scatter.11
  155.3 32.3 all-gather.32
  189.7 36.1 all-gather.20
  227.7 31.9 all-gather.30
  261.3 36.1 all-gather.22
  299.3 31.9 all-gather.34
  344.3 34.0 reduce-scatter.15
  382.8 36.3 all-gather.24
  422.4 45.8 reduce-scatter.31
  471.6 46.0 reduce-scatter.29
  521.0 46.0 reduce-scatter.27
  570.1 34.9 reduce-scatter.23
  608.6 34.9 reduce-scatter.21
  646.6 36.6 reduce-scatter.25
  686.4 36.6 reduce-scatter.19
  725.4 34.0 reduce-scatter.17
  761.7 34.6 reduce-scatter.13

commit v2 on v1

v2 whole, which is shorter than its diff:
```python
from functools import partial

import jax
import jax.numpy as jnp
from jax import lax
from jax.experimental import pallas as pl
from jax.experimental.pallas import tpu as pltpu
from jax.sharding import PartitionSpec as P

HD = 96
HALF = 48
LANES = 128
EPSILON = 1e-05
ROPE_BASE = 100000.0
NEG_FILL = -1e30
MESH = pl.DeviceIdType.MESH
BF = jnp.bfloat16
F32 = jnp.float32
TILE = 256
CHUNK = 32


def mm(left, right):
    return jnp.dot(left, right, preferred_element_type=F32)


def mm_nt(left, right):
    return lax.dot_general(left, right, (((1,), (1,)), ((), ())), preferred_element_type=F32)


def mm_tn(left, right):
    return lax.dot_general(left, right, (((0,), (0,)), ((), ())), preferred_element_type=F32)


def loop(count, body):
    def step(index, carry):
        body(index)
        return carry

    lax.fori_loop(0, count, step, 0)


def flip(chip, bits):
    other, bit = chip, 1
    while bit <= bits:
        if bits & bit:
            other = other + bit * (1 - 2 * ((chip // bit) % 2))
        bit *= 2
    return other


def layer_kernel(dims, *refs):
    n, chips, rows, width, nq, nkv, ff, nseq = dims
    nf = 2 * chips
    shard = width // nf
    total = n * rows
    widths = (nq * LANES + 2 * nkv * LANES, nq * LANES, ff, ff, ff)
    refs = list(refs)

    def take(count):
        taken = refs[:count]
        del refs[:count]
        return taken

    (lengths, freq, tokens, cot, gains_in) = take(5)
    srcs = take(5)
    (out_ref, gtok_ref, gains_out) = take(3)
    gouts = take(5)
    landing = take(5)
    weights = take(5)
    (x_buf, ct_buf, mi_buf, gm_buf) = take(4)
    (qkv, gqkv, probs, mixed, gmixed, hid, gg, gu) = take(8)
    (t_one, t_two) = take(2)
    (s_buf, r_buf, p_zero, p_one, middle, gmid) = take(6)
    (sc_one, sc_two, cos_t, sin_t) = take(4)
    (gain_in, gain_row, gain_z, gain_f, stage) = take(5)
    send_b = take(1)[0]
    sums = take(5)
    from_partner = take(5)
    (w_ss, w_fs, w_rs, w_ls) = take(4)
    (z_ss, z_rs) = take(2)
    (rs_ss, rs_rs) = take(2)
    (b_ss, b_rs, i_ss, i_rs, l_sem) = take(5)

    f = lax.axis_index("fsdp")
    d = lax.axis_index("dp")
    p = f // 2
    c = f % 2

    def at_f(index):
        return {"fsdp": index, "dp": d}

    def at_d(index):
        return {"fsdp": f, "dp": index}

    partner = p * 2 + 1 - c

    def remote(src, dst, ss, rs, where):
        return pltpu.make_async_remote_copy(
            src_ref=src, dst_ref=dst, send_sem=ss, recv_sem=rs, device_id=where, device_id_type=MESH
        )

    def block(ref, index, size=rows):
        return ref.at[pl.ds(pl.multiple_of(index * size, size), size)]

    def cols(index, size=TILE):
        return pl.ds(pl.multiple_of(index * size, size), size)

    barrier = pltpu.get_barrier_semaphore()
    for k in range(1, chips):
        pl.semaphore_signal(
            barrier, inc=1, device_id=at_f(flip(p, k) * 2 + c), device_id_type=MESH
        )
    pl.semaphore_signal(barrier, inc=1, device_id=at_f(partner), device_id_type=MESH)

    @pl.when(d > 0)
    def _():
        pl.semaphore_signal(barrier, inc=1, device_id=at_d(d - 1), device_id_type=MESH)

    @pl.when(d < n - 1)
    def _():
        pl.semaphore_signal(barrier, inc=1, device_id=at_d(d + 1), device_id_type=MESH)

    ends = (d == 0).astype(jnp.int32) + (d == n - 1).astype(jnp.int32)
    pl.semaphore_wait(barrier, chips + 2 - ends)

    class Gather:
        def __init__(self, slot, src, dst, size):
            self.slot, self.src, self.dst, self.size = slot, src, dst, size

        def part(self, index):
            return block(self.dst, index, self.size)

        def direct(self, k):
            where = partner if k == 0 else flip(p, k) * 2 + c
            return remote(
                self.src, self.part(f), w_ss.at[self.slot, k], w_rs.at[self.slot, f], at_f(where)
            )

        def onward(self, k):
            index = flip(p, k) * 2 + c
            return remote(
                self.part(index),
                self.part(index),
                w_fs.at[self.slot, k],
                w_rs.at[self.slot, index],
                at_f(partner),
            )

        def own(self):
            return pltpu.make_async_copy(self.src, self.part(f), w_ls.at[self.slot])

        def start(self):
            for k in list(range(1, chips)) + [0]:
                self.direct(k).start()
            self.own().start()

        def forward(self):
            for k in range(1, chips):
                copy = self.onward(k)
                copy.wait_recv()
                copy.start()

        def finish(self):
            for k in range(chips):
                index = flip(p, k) * 2 + 1 - c
                remote(
                    self.part(index),
                    self.part(index),
                    w_fs.at[self.slot, k],
                    w_rs.at[self.slot, index],
                    at_f(partner),
                ).wait_recv()
            self.own().wait()

        def drain(self):
            for k in range(chips):
                self.direct(k).wait_send()
            for k in range(1, chips):
                self.onward(k).wait_send()

    class Line:
        def __init__(self, slot, buf, size=rows, src=None):
            self.slot, self.buf, self.size, self.src = slot, buf, size, src

        def copy(self, index, side, own=False):
            part = block(self.buf, index, self.size)
            src = self.src if own and self.src is not None else part
            where = d + 1 if side == 0 else d - 1
            return remote(
                src, part, z_ss.at[self.slot, side, index], z_rs.at[self.slot, index], at_d(where)
            )

        def start(self):
            @pl.when(d < n - 1)
            def _():
                self.copy(d, 0, True).start()

            @pl.when(d > 0)
            def _():
                self.copy(d, 1, True).start()

        def step(self, s):
            @pl.when(d - s >= 0)
            def _():
                copy = self.copy(d - s, 0)
                copy.wait_recv()

                @pl.when(d < n - 1)
                def _():
                    copy.start()

            @pl.when(d + s < n)
            def _():
                copy = self.copy(d + s, 1)
                copy.wait_recv()

                @pl.when(d > 0)
                def _():
                    copy.start()

        def drain(self):
            for j in range(n):

                @pl.when((j <= d) & (d < n - 1))
                def _():
                    self.copy(j, 0).wait_send()

                @pl.when((j >= d) & (d > 0))
                def _():
                    self.copy(j, 1).wait_send()

    class Reduce:
        def __init__(self, slot, partial_of, sends, gets):
            self.slot, self.partial_of, self.sends, self.gets = slot, partial_of, sends, gets

        def copy(self, index, where, slot):
            return remote(
                block(self.sends, index),
                block(self.gets, slot),
                rs_ss.at[self.slot, index],
                rs_rs.at[self.slot, slot],
                at_d(where),
            )

        def got(self, slot):
            remote(
                block(self.gets, slot),
                block(self.gets, slot),
                rs_ss.at[self.slot, 0],
                rs_rs.at[self.slot, slot],
                at_d(d),
            ).wait_recv()

        def combine(self, acc, index, has_more):
            send, get = block(self.sends, index), block(self.gets, index)

            @pl.when(has_more)
            def _():
                self.got(index)

                def rows_of(i):
                    r = pl.ds(pl.multiple_of(i * CHUNK, CHUNK), CHUNK)
                    send[r, :] = (acc[r, :] + get[r, :].astype(F32)).astype(BF)

                loop(rows // CHUNK, rows_of)

            @pl.when(jnp.logical_not(has_more))
            def _():
                def rows_of(i):
                    r = pl.ds(pl.multiple_of(i * CHUNK, CHUNK), CHUNK)
                    send[r, :] = acc[r, :].astype(BF)

                loop(rows // CHUNK, rows_of)

        def step(self, s):
            right, left = d + s, d - s

            @pl.when(right < n)
            def _():
                self.partial_of(right, p_zero)

            @pl.when(left >= 0)
            def _():
                self.partial_of(left, p_one)

            @pl.when(right < n)
            def _():
                self.combine(p_zero, right, d > 0)
                self.copy(right, d + 1, right).start()

            @pl.when(left >= 0)
            def _():
                self.combine(p_one, left, d < n - 1)
                self.copy(left, d - 1, n if s == 1 else left).start()

        def final(self):
            self.partial_of(d, p_zero)

            def add(slot):
                self.got(slot)
                get = block(self.gets, slot)

                def rows_of(i):
                    r = pl.ds(pl.multiple_of(i * CHUNK, CHUNK), CHUNK)
                    p_zero[r, :] = p_zero[r, :] + get[r, :].astype(F32)

                loop(rows // CHUNK, rows_of)

            @pl.when(d > 0)
            def _():
                add(d)

            @pl.when(d < n - 1)
            def _():
                add(n)

        def drain(self):
            for j in range(n):

                @pl.when(d != j)
                def _():
                    self.copy(j, d, j).wait_send()

    class Grad:
        def __init__(self, group, turned, terms):
            self.group, self.turned, self.terms = group, turned, terms
            self.width = widths[group]

        def rows_for(self, index):
            return pl.ds(pl.multiple_of(index * shard, shard), shard)

        def hand_over(self, k):
            chip = flip(p, k)
            return remote(
                send_b.at[k, :, pl.ds(0, self.width)],
                from_partner[self.group].at[chip],
                b_ss.at[self.group, k],
                b_rs.at[self.group, chip],
                at_f(partner),
            )

        def ship(self, k):
            chip = flip(p, k)
            return remote(
                sums[self.group].at[chip],
                landing[self.group].at[k - 1],
                i_ss.at[self.group, k - 1],
                i_rs.at[self.group, k - 1],
                at_f(chip * 2 + c),
            )

        def send(self, k):
            left = self.turned.at[self.rows_for(flip(p, k) * 2 + 1 - c)]

            def tile(t):
                send_b[k, :, cols(t)] = mm(left[...], self.terms[:, cols(t)]).astype(BF)

            loop(self.width // TILE, tile)
            self.hand_over(k).start()

        def own(self, k):
            chip = flip(p, k)
            left = self.turned.at[self.rows_for(chip * 2 + c)]
            remote(
                from_partner[self.group].at[chip],
                from_partner[self.group].at[chip],
                b_ss.at[self.group, k],
                b_rs.at[self.group, chip],
                at_f(partner),
            ).wait_recv()

            def tile(t):
                term = mm(left[...], self.terms[:, cols(t)])
                other = from_partner[self.group][chip, :, cols(t)].astype(F32)
                sums[self.group][chip, :, cols(t)] = (term + other).astype(BF)

            loop(self.width // TILE, tile)
            if k > 0:
                self.ship(k).start()

        def send_all(self):
            for k in list(range(1, chips)) + [0]:
                self.send(k)

        def own_all(self):
            for k in list(range(1, chips)) + [0]:
                self.own(k)
            for k in range(chips):
                self.hand_over(k).wait_send()

        def fetch(self, k):
            return pltpu.make_async_copy(
                landing[self.group].at[k - 1],
                stage.at[k - 1, :, pl.ds(0, self.width)],
                l_sem.at[k - 1],
            )

        def finish(self):
            for k in range(1, chips):
                self.ship(k).wait()
                self.fetch(k).start()
            for k in range(1, chips):
                self.fetch(k).wait()
            out = gouts[self.group]

            def tile(t):
                acc = sums[self.group][p, :, cols(t)].astype(F32)
                for k in range(1, chips):
                    acc = acc + stage[k - 1, :, cols(t)].astype(F32)
                out[:, cols(t)] = acc

            loop(self.width // TILE, tile)

    def row_blocks(body):
        loop(rows // CHUNK, lambda i: body(pl.ds(pl.multiple_of(i * CHUNK, CHUNK), CHUNK)))

    def turn(src, dst):
        def lane_block(t):
            dst[cols(t, LANES), :] = src[pl.ds(0, total), cols(t, LANES)].T

        loop(width // LANES, lane_block)

    gathers = [Gather(g, srcs[g], weights[g], shard) for g in range(5)]
    gain_gather = Gather(5, gains_in, gain_in, 8)
    tok_line = Line(0, x_buf, src=tokens)
    cot_line = Line(1, ct_buf, src=cot)
    mi_line = Line(2, mi_buf)
    gm_line = Line(3, gm_buf)
    gain_line = Line(4, gain_z, 8)

    tok_line.start()
    gathers[0].start()
    gain_gather.start()
    for g in range(1, 5):
        gathers[g].start()
    block(x_buf, d)[...] = tokens[...]
    block(ct_buf, d)[...] = cot[...]

    def segments(b, shape, dim):
        index = lax.broadcasted_iota(jnp.int32, shape, dim)
        segment = jnp.zeros(shape, jnp.int32)
        offset = jnp.zeros(shape, jnp.int32)
        end = jnp.int32(0)
        for k in range(nseq):
            end = end + lengths[b, k]
            past = index >= end
            segment = segment + past.astype(jnp.int32)
            offset = jnp.where(past, end, offset)
        return index, segment, offset

    def tables(b):
        index, _, offset = segments(b, (rows, LANES), 0)
        angle = (index - offset).astype(F32) * freq[...]
        lane = lax.broadcasted_iota(jnp.int32, (rows, LANES), 1)
        sine = jnp.sin(angle)
        block(cos_t, b)[...] = jnp.cos(angle)
        block(sin_t, b)[...] = jnp.where(lane < LANES // 2, -sine, sine)

    loop(n, tables)
    tok_line.step(1)
    gathers[0].forward()
    gain_gather.forward()
    for s in range(2, n):
        tok_line.step(s)
    cot_line.start()
    gathers[0].finish()
    gain_gather.finish()

    gain_row[...] = gain_in[pl.ds(0, 8), :]
    for k in range(1, nf):
        gain_row[...] = gain_row[...] + gain_in[pl.ds(8 * k, 8), :]

    def rms(value):
        mean = jnp.sum(value * value, axis=-1, keepdims=True) / width
        return lax.rsqrt(mean + EPSILON)

    def norm_one(i):
        r = pl.ds(pl.multiple_of(i * CHUNK, CHUNK), CHUNK)
        value = x_buf[r, :].astype(F32)
        scale = rms(value)
        sc_one[r, :] = scale
        mi_buf[r, :] = (value * scale * gain_row[0:1, :]).astype(BF)

    loop(total // CHUNK, norm_one)

    def rope(value, sign, cos_v, sin_v):
        return value * cos_v + sign * (pltpu.roll(value, LANES // 2, 1) * sin_v)

    heads = nq + 2 * nkv
    half_rows = min(total, 2 * rows)

    def qkv_rows(m):
        r = pl.ds(pl.multiple_of(m * half_rows, half_rows), half_rows)
        cos_v, sin_v = cos_t[r, :], sin_t[r, :]
        for t in range(heads // 2):
            both = mm(mi_buf[r, :], weights[0][:, 2 * t * LANES : 2 * (t + 1) * LANES])
            for h in (2 * t, 2 * t + 1):
                value = both[:, (h - 2 * t) * LANES : (h - 2 * t + 1) * LANES]
                if h < nq + nkv:
                    value = rope(value, 1.0, cos_v, sin_v)
                qkv[r, h * LANES : (h + 1) * LANES] = value.astype(BF)

    loop(total // half_rows, qkv_rows)
    gathers[1].forward()

    def head(ref, r, h):
        return ref[r, h * LANES : (h + 1) * LANES]

    def attend(b):
        r = pl.ds(pl.multiple_of(b * rows, rows), rows)
        t_index, t_seg, _ = segments(b, (rows, rows), 0)
        s_index, s_seg, _ = segments(b, (rows, rows), 1)
        allowed = (t_seg == s_seg) & (s_index <= t_index)
        for h in range(nq):
            kv = h // (nq // nkv)
            score = mm_nt(head(qkv, r, h), head(qkv, r, nq + kv)) * HD ** (-0.5)
            score = jnp.where(allowed, score, NEG_FILL)
            top = jnp.max(score, axis=-1, keepdims=True)
            log_total = top + jnp.log(jnp.sum(jnp.exp(score - top), axis=-1, keepdims=True))
            prob = jnp.where(allowed, jnp.exp(score - log_total), 0.0)
            probs[b * nq + h] = prob
            mixed[r, h * LANES : (h + 1) * LANES] = mm(
                prob.astype(BF), head(qkv, r, nq + nkv + kv)
            ).astype(BF)

    loop(n, attend)
    cot_line.step(1)
    gathers[1].finish()

    def by_turned(pairs):
        def partial_of(j, acc):
            r = pl.ds(pl.multiple_of(j * rows, rows), rows)

            def tile(t):
                value = None
                for left, weight in pairs:
                    term = mm_nt(left[r, :], weight[cols(t), :])
                    value = term if value is None else value + term
                acc[:, cols(t)] = value

            loop(width // TILE, tile)

        return partial_of

    after_attn = Reduce(0, by_turned([(mixed, weights[1])]), s_buf, r_buf)
    extra = [
        lambda: gathers[2].forward(),
        lambda: gathers[3].forward(),
    ]
    for s in range(n - 1, 0, -1):
        after_attn.step(s)
        if 2 <= n - s + 1 < n:
            cot_line.step(n - s + 1)
        if extra:
            extra.pop(0)()
    for todo in extra:
        todo()
    after_attn.final()

    own_rows = d * rows

    def norm_two(i):
        r = pl.ds(pl.multiple_of(i * CHUNK, CHUNK), CHUNK)
        value = tokens[r, :].astype(F32) + p_zero[r, :]
        scale = rms(value)
        middle[r, :] = value
        sc_two[r, :] = scale
        here = pl.ds(pl.multiple_of(own_rows + i * CHUNK, CHUNK), CHUNK)
        mi_buf[here, :] = (value * scale * gain_row[1:2, :]).astype(BF)

    loop(rows // CHUNK, norm_two)
    mi_line.start()
    mi_line.step(1)
    gathers[4].forward()
    cot_line.drain()
    turn(ct_buf, t_one)
    for s in range(2, n):
        mi_line.step(s)
    for g in (2, 3, 4):
        gathers[g].finish()
    after_attn.drain()

    tiles_ff = ff // TILE

    def feed(index):
        m, t = index // tiles_ff, index % tiles_ff
        r = pl.ds(pl.multiple_of(m * half_rows, half_rows), half_rows)
        left = mi_buf[r, :]
        gate = mm(left, weights[2][:, cols(t)])
        up = mm(left, weights[3][:, cols(t)])
        grad_hidden = mm(ct_buf[r, :], weights[4][:, cols(t)])
        sig = 1.0 / (1.0 + jnp.exp(-gate))
        hid[r, cols(t)] = (gate * sig * up).astype(BF)
        gu[r, cols(t)] = (grad_hidden * gate * sig).astype(BF)
        gg[r, cols(t)] = (grad_hidden * up * sig * (1.0 + gate * (1.0 - sig))).astype(BF)

    loop((total // half_rows) * tiles_ff, feed)
    mi_line.drain()
    turn(mi_buf, t_two)

    after_mlp = Reduce(1, by_turned([(gg, weights[2]), (gu, weights[3])]), s_buf, r_buf)
    down = Grad(4, t_one, hid)
    gate_g = Grad(2, t_two, gg)
    up_g = Grad(3, t_two, gu)
    work = [down.send_all, down.own_all, gate_g.send_all]
    for s in range(n - 1, 0, -1):
        after_mlp.step(s)
        if work:
            work.pop(0)()
    for todo in work:
        todo()
    after_mlp.final()

    def back_two(i):
        r = pl.ds(pl.multiple_of(i * CHUNK, CHUNK), CHUNK)
        term = p_zero[r, :]
        scale = sc_two[r, :]
        normed = middle[r, :] * scale
        gain_sum = jnp.sum(term * normed, axis=0, keepdims=True)
        dn = term * gain_row[1:2, :]
        mean = jnp.sum(dn * normed, axis=-1, keepdims=True) / width
        value = cot[r, :].astype(F32) + scale * (dn - normed * mean)
        gmid[r, :] = value
        here = pl.ds(pl.multiple_of(own_rows + i * CHUNK, CHUNK), CHUNK)
        gm_buf[here, :] = value.astype(BF)
        gain_own[1:2, :] = gain_own[1:2, :] + gain_sum

    gain_own = block(gain_z, d, 8)
    gain_own[...] = jnp.zeros((8, width), F32)
    loop(rows // CHUNK, back_two)
    gm_line.start()
    after_mlp.drain()

    output = Reduce(2, by_turned([(hid, weights[4])]), ct_buf, mi_buf)
    work = [gate_g.own_all, up_g.send_all, up_g.own_all]
    for s in range(1, n):
        output.step(n - s)
        gm_line.step(s)
        if work:
            work.pop(0)()
    for todo in work:
        todo()
    turn(gm_buf, t_one)

    def grad_mixed(index):
        tiles = widths[1] // TILE
        m, t = index // tiles, index % tiles
        r = pl.ds(pl.multiple_of(m * half_rows, half_rows), half_rows)
        gmixed[r, cols(t)] = mm(gm_buf[r, :], weights[1][:, cols(t)]).astype(BF)

    loop((total // half_rows) * (widths[1] // TILE), grad_mixed)

    def attend_back(b):
        r = pl.ds(pl.multiple_of(b * rows, rows), rows)
        cos_v, sin_v = cos_t[r, :], sin_t[r, :]
        group = nq // nkv
        for kv in range(nkv):
            key, val = head(qkv, r, nq + kv), head(qkv, r, nq + nkv + kv)
            grad_k = grad_v = None
            for h in range(kv * group, (kv + 1) * group):
                query, gm_h = head(qkv, r, h), head(gmixed, r, h)
                prob = probs[b * nq + h]
                delta = jnp.sum(
                    gm_h.astype(F32) * head(mixed, r, h).astype(F32), axis=-1, keepdims=True
                )
                grad_p = mm_nt(gm_h, val)
                grad_s = (prob * (grad_p - delta) * HD ** (-0.5)).astype(BF)
                grad_q = mm(grad_s, key)
                gqkv[r, h * LANES : (h + 1) * LANES] = rope(grad_q, -1.0, cos_v, sin_v).astype(BF)
                k_term, v_term = mm_tn(grad_s, query), mm_tn(prob.astype(BF), gm_h)
                grad_k = k_term if grad_k is None else grad_k + k_term
                grad_v = v_term if grad_v is None else grad_v + v_term
            k_at, v_at = (nq + kv) * LANES, (nq + nkv + kv) * LANES
            gqkv[r, k_at : k_at + LANES] = rope(grad_k, -1.0, cos_v, sin_v).astype(BF)
            gqkv[r, v_at : v_at + LANES] = grad_v.astype(BF)

    loop(n, attend_back)

    base_in = by_turned([(gqkv, weights[0])])

    def grad_in(j, acc):
        base_in(j, acc)

        def add_gain(i):
            r = pl.ds(pl.multiple_of(i * CHUNK, CHUNK), CHUNK)
            there = pl.ds(pl.multiple_of(j * rows + i * CHUNK, CHUNK), CHUNK)
            normed = x_buf[there, :].astype(F32) * sc_one[there, :]
            gain_own[0:1, :] = gain_own[0:1, :] + jnp.sum(
                acc[r, :] * normed, axis=0, keepdims=True
            )

        loop(rows // CHUNK, add_gain)

    after_in = Reduce(3, grad_in, s_buf, r_buf)
    out_g = Grad(1, t_one, mixed)
    qkv_g = Grad(0, t_two, gqkv)

    def turn_attn_in():
        def one(b):
            there = pl.ds(pl.multiple_of(b * rows, rows), rows)

            def lane_block(t):
                value = x_buf[there, cols(t, LANES)].astype(F32) * sc_one[there, :]
                value = (value * gain_row[0:1, cols(t, LANES)]).astype(BF)
                t_two[cols(t, LANES), cols(b, rows)] = value.T

            loop(width // LANES, lane_block)

        loop(n, one)

    work = [turn_attn_in, qkv_g.send_all, qkv_g.own_all]
    for s in range(n - 1, 0, -1):
        after_in.step(s)
        if work:
            work.pop(0)()
    for todo in work:
        todo()
    out_g.send_all()
    out_g.own_all()
    after_in.final()

    def back_one(i):
        r = pl.ds(pl.multiple_of(i * CHUNK, CHUNK), CHUNK)
        there = pl.ds(pl.multiple_of(own_rows + i * CHUNK, CHUNK), CHUNK)
        scale = sc_one[there, :]
        normed = tokens[r, :].astype(F32) * scale
        dm = p_zero[r, :] * gain_row[0:1, :]
        mean = jnp.sum(dm * normed, axis=-1, keepdims=True) / width
        gtok_ref[r, :] = gmid[r, :] + scale * (dm - normed * mean)

    loop(rows // CHUNK, back_one)
    gain_line.start()
    output.final()

    def write_out(i):
        r = pl.ds(pl.multiple_of(i * CHUNK, CHUNK), CHUNK)
        out_ref[r, :] = (middle[r, :] + p_zero[r, :]).astype(BF)

    loop(rows // CHUNK, write_out)
    for s in range(1, n):
        gain_line.step(s)
    gain_sum = gain_z[pl.ds(0, 8), :]
    for k in range(1, n):
        gain_sum = gain_sum + gain_z[pl.ds(8 * k, 8), :]
    gain_row[...] = gain_sum
    gain_back = Gather(6, gain_row, gain_f, 8)
    gain_back.start()
    gain_back.forward()
    for grad in (down, gate_g, up_g, qkv_g, out_g):
        grad.finish()
    gain_back.finish()
    gain_sum = gain_f[pl.ds(0, 8), :]
    for k in range(1, nf):
        gain_sum = gain_sum + gain_f[pl.ds(8 * k, 8), :]
    gains_out[...] = gain_sum

    output.drain()
    after_in.drain()
    for line in (tok_line, gm_line, gain_line):
        line.drain()
    for gather in gathers + [gain_gather, gain_back]:
        gather.drain()


def run_layer(lengths, freq, tokens, cot, gains, shards, sizes):
    n, chips, nq, nkv = sizes
    rows, width = tokens.shape
    total = n * rows
    nf = 2 * chips
    shard = shards[0].shape[0]
    ff = shards[2].shape[1]
    widths = tuple(s.shape[1] for s in shards)
    dims = (n, chips, rows, width, nq, nkv, ff, lengths.shape[1])
    vmem = pl.BlockSpec(memory_space=pltpu.VMEM)
    anywhere = pl.BlockSpec(memory_space=pl.ANY)
    out_shape = (
        [
            jax.ShapeDtypeStruct((rows, width), BF),
            jax.ShapeDtypeStruct((rows, width), F32),
            jax.ShapeDtypeStruct((8, width), F32),
        ]
        + [jax.ShapeDtypeStruct((shard, w), F32) for w in widths]
        + [jax.ShapeDtypeStruct((chips - 1, shard, w), BF) for w in widths]
    )
    widest = max(widths)
    scratch = (
        [pltpu.VMEM((width, w), BF) for w in widths]
        + [
            pltpu.VMEM((total, width), BF),
            pltpu.VMEM((total, width), BF),
            pltpu.VMEM((total + rows, width), BF),
            pltpu.VMEM((total, width), BF),
            pltpu.VMEM((total, widths[0]), BF),
            pltpu.VMEM((total, widths[0]), BF),
            pltpu.VMEM((n * nq, rows, rows), F32),
            pltpu.VMEM((total, widths[1]), BF),
            pltpu.VMEM((total, widths[1]), BF),
            pltpu.VMEM((total, ff), BF),
            pltpu.VMEM((total, ff), BF),
            pltpu.VMEM((total, ff), BF),
            pltpu.VMEM((width, total), BF),
            pltpu.VMEM((width, total), BF),
            pltpu.VMEM((total, width), BF),
            pltpu.VMEM((total + rows, width), BF),
            pltpu.VMEM((rows, width), F32),
            pltpu.VMEM((rows, width), F32),
            pltpu.VMEM((rows, width), F32),
            pltpu.VMEM((rows, width), F32),
            pltpu.VMEM((total, 1), F32),
            pltpu.VMEM((rows, 1), F32),
            pltpu.VMEM((total, LANES), F32),
            pltpu.VMEM((total, LANES), F32),
            pltpu.VMEM((nf * 8, width), F32),
            pltpu.VMEM((8, width), F32),
            pltpu.VMEM((n * 8, width), F32),
            pltpu.VMEM((nf * 8, width), F32),
            pltpu.VMEM((chips - 1, shard, widest), BF),
            pltpu.VMEM((chips, shard, widest), BF),
        ]
        + [pltpu.VMEM((chips, shard, w), BF) for w in widths]
        + [pltpu.VMEM((chips, shard, w), BF) for w in widths]
        + [
            pltpu.SemaphoreType.DMA((7, chips)),
            pltpu.SemaphoreType.DMA((7, chips)),
            pltpu.SemaphoreType.DMA((7, nf)),
            pltpu.SemaphoreType.DMA((7,)),
            pltpu.SemaphoreType.DMA((5, 2, n)),
            pltpu.SemaphoreType.DMA((5, n)),
            pltpu.SemaphoreType.DMA((4, n)),
            pltpu.SemaphoreType.DMA((4, n + 1)),
            pltpu.SemaphoreType.DMA((5, chips)),
            pltpu.SemaphoreType.DMA((5, chips)),
            pltpu.SemaphoreType.DMA((5, chips)),
            pltpu.SemaphoreType.DMA((5, chips)),
            pltpu.SemaphoreType.DMA((chips,)),
        ]
    )
    return pl.pallas_call(
        partial(layer_kernel, dims),
        out_shape=out_shape,
        in_specs=[pl.BlockSpec(memory_space=pltpu.SMEM)] + [vmem] * 4 + [anywhere] * 5,
        out_specs=[vmem] * 8 + [anywhere] * 5,
        scratch_shapes=scratch,
        compiler_params=pltpu.CompilerParams(
            collective_id=0, has_side_effects=True, vmem_limit_bytes=67043328
        ),
        name="layer",
    )(lengths, freq, tokens, cot, gains, *shards)


def split_pad(weight, heads):
    lead = weight.shape[0]
    halves = weight.reshape(lead, heads, 2, HALF)
    return jnp.pad(halves, ((0, 0), (0, 0), (0, 0), (0, LANES // 2 - HALF))).reshape(lead, -1)


def end_pad(weight, heads):
    lead = weight.shape[0]
    return jnp.pad(
        weight.reshape(lead, heads, HD), ((0, 0), (0, 0), (0, LANES - HD))
    ).reshape(lead, -1)


def split_take(grad, heads):
    lead = grad.shape[0]
    return grad.reshape(lead, heads, 2, LANES // 2)[..., :HALF].reshape(lead, heads * HD)


def end_take(grad, heads):
    lead = grad.shape[0]
    return grad.reshape(lead, heads, LANES)[..., :HD].reshape(lead, heads * HD)


def body(
    n,
    chips,
    tokens,
    lengths,
    cotangent,
    attn_gain,
    w_query,
    w_key,
    w_value,
    w_out,
    mlp_gain,
    w_gate,
    w_up,
    w_down,
):
    shard = attn_gain.shape[1]
    width = tokens.shape[1]
    nq = w_query.shape[2] // HD
    nkv = w_key.shape[2] // HD
    start = lax.axis_index("fsdp") * shard
    both = jnp.concatenate([attn_gain, mlp_gain], axis=0).astype(F32)
    gains = lax.dynamic_update_slice(jnp.zeros((8, width), F32), both, (0, start))
    frequency = ROPE_BASE ** (-jnp.arange(HALF, dtype=F32) / HALF)
    frequency = jnp.pad(frequency, (0, LANES // 2 - HALF))
    freq = jnp.concatenate([frequency, frequency])[None, :]
    shards = (
        jnp.concatenate(
            [split_pad(w_query[0], nq), split_pad(w_key[0], nkv), end_pad(w_value[0], nkv)], axis=1
        ),
        end_pad(w_out[0].T, nq),
        w_gate[0],
        w_up[0],
        w_down[0].T,
    )
    results = run_layer(
        lengths, freq, tokens, cotangent, gains, shards, (n, chips, nq, nkv)
    )
    output, grad_tokens, gain_rows, g_qkv, g_out, g_gate, g_up, g_down = results[:8]
    gain_cut = lax.dynamic_slice(gain_rows, (0, start), (2, shard))
    q_end, k_end = nq * LANES, (nq + nkv) * LANES
    return (
        output,
        grad_tokens,
        gain_cut[0:1],
        split_take(g_qkv[:, :q_end], nq)[None],
        split_take(g_qkv[:, q_end:k_end], nkv)[None],
        end_take(g_qkv[:, k_end:], nkv)[None],
        end_take(g_out, nq).T[None],
        gain_cut[1:2],
        g_gate[None],
        g_up[None],
        g_down.T[None],
    )


def solution(mesh):
    placed = (
        P(("fsdp", "dp"), None),
        P("fsdp", None),
        P(("fsdp", "dp"), None),
        P(None, "fsdp"),
        P(None, "fsdp", "dp"),
        P(None, "fsdp", "dp"),
        P(None, "fsdp", "dp"),
        P(None, "dp", "fsdp"),
        P(None, "fsdp"),
        P(None, "fsdp", "dp"),
        P(None, "fsdp", "dp"),
        P(None, "dp", "fsdp"),
    )
    return jax.shard_map(
        partial(body, mesh.shape["dp"], mesh.shape["fsdp"] // 2),
        mesh=mesh,
        in_specs=placed,
        out_specs=(
            P(("fsdp", "dp"), None),
            P(("fsdp", "dp"), None),
            P(None, "fsdp"),
            P(None, "fsdp", "dp"),
            P(None, "fsdp", "dp"),
            P(None, "fsdp", "dp"),
            P(None, "dp", "fsdp"),
            P(None, "fsdp"),
            P(None, "fsdp", "dp"),
            P(None, "fsdp", "dp"),
            P(None, "dp", "fsdp"),
        ),
        check_vma=False,
    )
```

time: 810 us -> 262 us (0.32)
  waiting for transfers between devices: 604 us -> 0 us
  Pallas kernels: 0 us -> 241 us
  matrix products: 75.1 us -> 0 us
  blocking collectives: 63.1 us -> 0 us
  other arithmetic: 32.9 us -> 2.14 us
  between operations: 16.2 us -> 0.89 us
    reduce_scatter x11 -> x0, waiting for transfers between devices: 364 us -> none  [the longest x4 108 us: settle(): lax.psum_scatter(terms_in.astype(jnp.bfloat16), 'dp', scatter_dimension=0...]
    pallas_call x0 -> x1, Pallas kernels: none -> 241 us  [run_layer(): pl.pallas_call(partial(layer_kernel, dims), out_shape=out_shape, in_specs...]
    all_gather x9 -> x0, waiting for transfers between devices: 236 us -> none  [the longest x4 103 us: spread(): return lax.all_gather(rows_in, 'dp', axis=0, tiled=True)]
    dot_general x27 -> x0, matrix products: 75.1 us -> none  [the longest x7 25.1 us: matmul(): return jnp.dot(left, right, preferred_element_type=jnp.float32)]
    unnamed x2 -> x0, blocking collectives: 26.6 us -> none
    all_gather x2 -> x0, blocking collectives: 19.8 us -> none  [the longest x1 10.3 us: fetch_fsdp(): lax.all_gather(shards[3][layer_idx], 'fsdp', axis=0, tiled=True)]
    psum x1 -> x0, blocking collectives: 16.8 us -> none  [body(): gains = lax.psum((terms[0], terms[5]), 'dp')]
    another operation x13 -> x0, other arithmetic: 15.2 us -> none  [the longest x9 13.6 us: body(): jnp.stack([grads_by_layer[0][slot_idx]])]
  transfers between devices with their start and end apart: 20 -> 0, of which waited for: 20 -> 0; matrix products, arithmetic and copies ran while one was open for 11% -> 0% of each run, Pallas kernels for 0% -> 0%
where the time goes in v2:
time: 262 us; the launch traced here: 259 us
  Pallas kernels  241 us (92%)
  local copies, waits for them, and re-layouts  15 us (6%)
    pallas_call x1, Pallas kernels, run_layer(): pl.pallas_call(partial(layer_kernel, dims), out_shape=out_shape, in_specs...  241 us
    unnamed x33, local copies, waits for them, and re-layouts  8.92 us

profile of v2, /device:TPU:8, one launch (start us, length us, event | category | flops | bytes accessed | tf_op | source)
XLA Modules:
  0.0 259.3 jit_solution(11551958632541478682)
XLA Ops:
  0.7 0.7 maximum_convert_fusion
  1.4 0.4 dynamic_update_slice.3.refs_4_
  1.8 1.1 copy.23
  3.6 0.8 pad_maximum_fusion.refs_5_
  4.4 0.1 reshape.55
  4.7 0.7 copy.35
  5.4 0.6 maximum_bitcast_fusion.refs_1_
  6.0 241.3 %layer.1 = (bf16[128,1536]{1,0:T(8,128)(2,1)}, f32[128,1536]{1,0:T(8,128)}, f32[8,1536]{1,0:T(8,128)}, f32[192,1024]{1,0:T(8,128)}, f32[192,512]{1,0:T(8,128)}, ...) custom-call(s32[4,4]{1,0:T(4,128)} %refs_0_.1, ...), custom_call_target="tpu_custom_call" | custom-call | tf_op jit(solution)/shard_map/layer/pallas_call | solution.py:839
  247.3 1.4 fusion.1
  248.8 1.0 fusion
  249.8 0.1 copy.28
  250.0 0.8 copy.30
  250.9 0.8 broadcast_in_dim_reshape.11
  251.8 0.2 copy.27
  252.0 0.9 copy.29
  252.9 0.1 reshape.60
  253.0 0.9 reshape.61
  254.0 0.7 copy.43
  254.7 0.9 copy.44
  255.6 0.9 copy.45
  256.5 0.5 copy-done.1
  257.0 0.9 copy.46
  257.9 0.5 copy-done
  258.4 0.9 copy.47
  (36 shorter events, 0.9 us)
Async XLA Ops:
  0.6 2.5 copy-start.9
  0.7 2.7 %copy-start.10 = (bf16[1,192,192]{2,1,0:T(8,128)(2,1)S(1)}, bf16[1,192,192]{2,1,0:T(8,128)(2,1)}, u32[]{:S(2)}) copy-start(bf16[1,192,192]{2,1,0:T(8,128)(2,1)} %param.18) | copy-start | bytes 221188
  1.8 1.1 copy-start.7
  3.0 1.4 copy-start.8
  249.8 1.9 copy-start.4
  251.8 1.1 copy-start.6
  252.0 2.0 copy-start.5
  252.9 1.8 copy-start.3
  254.0 1.6 copy-start.2
  255.6 1.4 copy-start.1
  257.0 1.4 copy-start

commit v3 on v2

v3 whole, which is shorter than its diff:
```python
from functools import partial

import jax
import jax.numpy as jnp
from jax import lax
from jax.experimental import pallas as pl
from jax.experimental.pallas import tpu as pltpu
from jax.sharding import PartitionSpec as P

HD = 96
HALF = 48
LANES = 128
EPSILON = 1e-05
ROPE_BASE = 100000.0
NEG_FILL = -1e30
MESH = pl.DeviceIdType.MESH
BF = jnp.bfloat16
F32 = jnp.float32
TILE = 256
CHUNK = 32


def mm(left, right):
    return jnp.dot(left, right, preferred_element_type=F32)


def mm_nt(left, right):
    return lax.dot_general(left, right, (((1,), (1,)), ((), ())), preferred_element_type=F32)


def mm_tn(left, right):
    return lax.dot_general(left, right, (((0,), (0,)), ((), ())), preferred_element_type=F32)


def loop(count, body):
    def step(index, carry):
        body(index)
        return carry

    lax.fori_loop(0, count, step, 0)


def flip(chip, bits):
    other, bit = chip, 1
    while bit <= bits:
        if bits & bit:
            other = other + bit * (1 - 2 * ((chip // bit) % 2))
        bit *= 2
    return other


def layer_kernel(dims, *refs):
    n, chips, rows, width, nq, nkv, ff, nseq = dims
    nf = 2 * chips
    shard = width // nf
    total = n * rows
    half = rows // 2
    q_wide, kv_wide = nq * LANES, nkv * LANES
    widths = (q_wide + 2 * kv_wide, q_wide, ff, ff, ff)
    near = [1] if chips > 1 else []
    far = [2 * k for k in range(1, chips // 2)]
    refs = list(refs)

    def take(count):
        taken = refs[:count]
        del refs[:count]
        return taken

    (lengths, freq, tokens, cot, gain_a, gain_m, w_q, w_k, w_v, w_o, w_d, w_g, w_u) = take(13)
    (out_ref, gtok_ref, out_ga, out_gm, out_q, out_k, out_v, out_o, out_g, out_u, out_d) = take(11)
    landing = take(5)
    weights = take(5)
    (x_buf, ct_buf, mi_buf, gm_buf) = take(4)
    (qkv, gqkv, probs, mixed, gmixed, hid, gg, gu) = take(8)
    (t_one, t_two) = take(2)
    (s_buf, r_buf, own_sum, middle, gmid) = take(5)
    (sc_one, sc_two, cos_t, sin_t) = take(4)
    (gains_in, gain_in, gain_row, gain_z, gain_f, stage) = take(6)
    (pick_rope, pick_end, same) = take(3)
    send_b = take(1)[0]
    sums = take(5)
    from_partner = take(5)
    (w_ss, w_fs, w_qs, w_rs, w_ls) = take(5)
    (z_ss, z_rs) = take(2)
    (rs_ss, rs_rs) = take(2)
    (b_ss, b_rs, i_ss, i_rs, l_sem) = take(5)

    f = lax.axis_index("fsdp")
    d = lax.axis_index("dp")
    p = f // 2
    c = f % 2

    def at_f(index):
        return {"fsdp": index, "dp": d}

    def at_d(index):
        return {"fsdp": f, "dp": index}

    partner = p * 2 + 1 - c

    def remote(src, dst, ss, rs, where):
        return pltpu.make_async_remote_copy(
            src_ref=src, dst_ref=dst, send_sem=ss, recv_sem=rs, device_id=where, device_id_type=MESH
        )

    def span(index, size):
        return pl.ds(pl.multiple_of(index * size, size), size)

    def block(ref, index, size=rows):
        return ref.at[span(index, size)]

    def cols(index, size=TILE):
        return span(index, size)

    barrier = pltpu.get_barrier_semaphore()
    for k in range(1, chips):
        pl.semaphore_signal(
            barrier, inc=1, device_id=at_f(flip(p, k) * 2 + c), device_id_type=MESH
        )
    pl.semaphore_signal(barrier, inc=1, device_id=at_f(partner), device_id_type=MESH)

    @pl.when(d > 0)
    def _():
        pl.semaphore_signal(barrier, inc=1, device_id=at_d(d - 1), device_id_type=MESH)

    @pl.when(d < n - 1)
    def _():
        pl.semaphore_signal(barrier, inc=1, device_id=at_d(d + 1), device_id_type=MESH)

    ends = (d == 0).astype(jnp.int32) + (d == n - 1).astype(jnp.int32)

    class Gather:
        def __init__(self, slot, dst, size, src=None):
            self.slot, self.dst, self.size = slot, dst, size
            self.src = self.part(f) if src is None else src
            self.local = src is not None

        def part(self, index):
            return block(self.dst, index, self.size)

        def direct(self, k):
            where = partner if k == 0 else flip(p, k) * 2 + c
            return remote(
                self.src, self.part(f), w_ss.at[self.slot, k], w_rs.at[self.slot, f], at_f(where)
            )

        def onward(self, k):
            index = flip(p, k) * 2 + c
            return remote(
                self.part(index),
                self.part(index),
                w_fs.at[self.slot, k],
                w_rs.at[self.slot, index],
                at_f(partner),
            )

        def across(self, first, second):
            index = flip(p, first) * 2 + c
            return remote(
                self.part(index),
                self.part(index),
                w_qs.at[self.slot, first + second],
                w_rs.at[self.slot, index],
                at_f(flip(p, second) * 2 + c),
            )

        def own(self):
            return pltpu.make_async_copy(self.src, self.part(f), w_ls.at[self.slot])

        def start(self):
            for k in near + far + [0]:
                self.direct(k).start()
            if self.local:
                self.own().start()

        def relay(self):
            for core, first, second in ((0, near, far), (1, far, near)):

                @pl.when(c == core)
                def _():
                    for k in first:
                        copy = self.onward(k)
                        copy.wait_recv()
                        for other in second:
                            self.across(k, other).start()
                        copy.start()

        def forward(self):
            for core, second in ((0, far), (1, near)):

                @pl.when(c == core)
                def _():
                    for k in second:
                        copy = self.onward(k)
                        copy.wait_recv()
                        copy.start()

            for k in near:
                for other in far:
                    copy = self.onward(k + other)
                    copy.wait_recv()
                    copy.start()

        def finish(self):
            for k in range(chips):
                index = flip(p, k) * 2 + 1 - c
                remote(
                    self.part(index),
                    self.part(index),
                    w_fs.at[self.slot, k],
                    w_rs.at[self.slot, index],
                    at_f(partner),
                ).wait_recv()
            if self.local:
                self.own().wait()

        def drain(self):
            for k in near + far + [0]:
                self.direct(k).wait_send()
            for k in range(1, chips):
                self.onward(k).wait_send()
            for k in near:
                for other in far:
                    remote(
                        self.part(f),
                        self.part(f),
                        w_qs.at[self.slot, k + other],
                        w_rs.at[self.slot, f],
                        at_f(partner),
                    ).wait_send()

    class Line:
        def __init__(self, slot, buf, size=rows, parts=1, src=None):
            self.slot, self.buf, self.size, self.parts, self.src = slot, buf, size, parts, src

        def copy(self, index, side, h, own=False):
            piece = self.size // self.parts
            part = block(self.buf, index * self.parts + h, piece)
            src = self.src if own and self.src is not None else part
            where = d + 1 if side == 0 else d - 1
            return remote(
                src,
                part,
                z_ss.at[self.slot, side, h, index],
                z_rs.at[self.slot, h, index],
                at_d(where),
            )

        def start(self, h=0):
            @pl.when(d < n - 1)
            def _():
                self.copy(d, 0, h, True).start()

            @pl.when(d > 0)
            def _():
                self.copy(d, 1, h, True).start()

        def step(self, s, h=0):
            @pl.when(d - s >= 0)
            def _():
                copy = self.copy(d - s, 0, h)
                copy.wait_recv()

                @pl.when(d < n - 1)
                def _():
                    copy.start()

            @pl.when(d + s < n)
            def _():
                copy = self.copy(d + s, 1, h)
                copy.wait_recv()

                @pl.when(d > 0)
                def _():
                    copy.start()

        def drain(self):
            for h in range(self.parts):
                for j in range(n):

                    @pl.when((j <= d) & (d < n - 1))
                    def _():
                        self.copy(j, 0, h).wait_send()

                    @pl.when((j >= d) & (d > 0))
                    def _():
                        self.copy(j, 1, h).wait_send()

    class Reduce:
        def __init__(self, slot, tiles_of, sends, gets):
            self.slot, self.tiles_of, self.sends, self.gets = slot, tiles_of, sends, gets

        def copy(self, index, where, slot, h):
            return remote(
                block(self.sends, 2 * index + h, half),
                block(self.gets, 2 * slot + h, half),
                rs_ss.at[self.slot, h, index],
                rs_rs.at[self.slot, h, slot],
                at_d(where),
            )

        def got(self, slot, h):
            part = block(self.gets, 2 * slot + h, half)
            remote(
                part, part, rs_ss.at[self.slot, h, 0], rs_rs.at[self.slot, h, slot], at_d(d)
            ).wait_recv()

        def right(self, index, h):
            return self.copy(index, d + 1, index, h)

        def left(self, index, h, last):
            return self.copy(index, d - 1, n if last else index, h)

        def compute(self):
            def store(j):
                def put(t, value):
                    self.sends[span(j, rows), cols(t)] = value.astype(BF)

                return put

            def keep(t, value):
                own_sum[:, cols(t)] = value

            def one(i):
                right, left = d + n - 1 - i, d - (n - 1 - i)

                @pl.when(right < n)
                def _():
                    self.tiles_of(right, store(right))

                @pl.when((right < n) & (i == 0))
                def _():
                    self.right(right, 0).start()

                @pl.when(left >= 0)
                def _():
                    self.tiles_of(left, store(left))

                @pl.when((left >= 0) & (i == 0))
                def _():
                    self.left(left, 0, n == 2).start()

            loop(n - 1, one)
            self.tiles_of(d, keep)

        def add_into(self, index, h):
            self.got(index, h)

            def some(i):
                r = pl.ds(pl.multiple_of(index * rows + h * half + i * CHUNK, CHUNK), CHUNK)
                self.sends[r, :] = (
                    self.sends[r, :].astype(F32) + self.gets[r, :].astype(F32)
                ).astype(BF)

            loop(half // CHUNK, some)

        def advance(self, s, h):
            right, left = d + s, d - s

            @pl.when(right < n)
            def _():
                @pl.when(d > 0)
                def _():
                    self.add_into(right, h)

                self.right(right, h).start()

            @pl.when(left >= 0)
            def _():
                @pl.when(d < n - 1)
                def _():
                    self.add_into(left, h)

                self.left(left, h, s == 1).start()

        def final(self, h):
            def add(slot):
                self.got(slot, h)

                def some(i):
                    r = pl.ds(pl.multiple_of(h * half + i * CHUNK, CHUNK), CHUNK)
                    there = pl.ds(
                        pl.multiple_of(slot * rows + h * half + i * CHUNK, CHUNK), CHUNK
                    )
                    own_sum[r, :] = own_sum[r, :] + self.gets[there, :].astype(F32)

                loop(half // CHUNK, some)

            @pl.when(d > 0)
            def _():
                add(d)

            @pl.when(d < n - 1)
            def _():
                add(n)

        def drain(self):
            for h in range(2):
                for j in range(n):

                    @pl.when(d != j)
                    def _():
                        self.copy(j, d, j, h).wait_send()

    class Grad:
        def __init__(self, group, turned, terms, emit):
            self.group, self.turned, self.terms, self.emit = group, turned, terms, emit
            self.width = widths[group]

        def hand_over(self, k):
            chip = flip(p, k)
            return remote(
                send_b.at[k, :, pl.ds(0, self.width)],
                from_partner[self.group].at[chip],
                b_ss.at[self.group, k],
                b_rs.at[self.group, chip],
                at_f(partner),
            )

        def ship(self, k):
            chip = flip(p, k)
            return remote(
                sums[self.group].at[chip],
                landing[self.group].at[k - 1],
                i_ss.at[self.group, k - 1],
                i_rs.at[self.group, k - 1],
                at_f(chip * 2 + c),
            )

        def send(self, k):
            left = self.turned.at[span(flip(p, k) * 2 + 1 - c, shard)]

            def tile(t):
                send_b[k, :, cols(t)] = mm(left[...], self.terms[:, cols(t)]).astype(BF)

            loop(self.width // TILE, tile)
            self.hand_over(k).start()

        def own(self, k):
            chip = flip(p, k)
            left = self.turned.at[span(chip * 2 + c, shard)]
            part = from_partner[self.group].at[chip]
            remote(
                part, part, b_ss.at[self.group, k], b_rs.at[self.group, chip], at_f(partner)
            ).wait_recv()

            def tile(t):
                term = mm(left[...], self.terms[:, cols(t)])
                other = from_partner[self.group][chip, :, cols(t)].astype(F32)
                sums[self.group][chip, :, cols(t)] = (term + other).astype(BF)

            loop(self.width // TILE, tile)
            if k > 0:
                self.ship(k).start()

        def send_all(self):
            for k in list(range(1, chips)) + [0]:
                self.send(k)

        def own_all(self):
            for k in list(range(1, chips)) + [0]:
                self.own(k)
            for k in range(chips):
                self.hand_over(k).wait_send()

        def fetch(self, k):
            return pltpu.make_async_copy(
                landing[self.group].at[k - 1],
                stage.at[k - 1, :, pl.ds(0, self.width)],
                l_sem.at[k - 1],
            )

        def finish(self):
            for k in range(1, chips):
                self.ship(k).wait()
                self.fetch(k).start()
            for k in range(1, chips):
                self.fetch(k).wait()

            def parts(lanes):
                yield sums[self.group][p, :, lanes]
                for k in range(1, chips):
                    yield stage[k - 1, :, lanes]

            self.emit(parts)

    def total_of(values):
        result = None
        for value in values:
            result = value if result is None else result + value
        return result

    def emit_plain(out):
        def emit(parts):
            def tile(t):
                out[:, cols(t)] = total_of(v.astype(F32) for v in parts(cols(t)))

            loop(ff // TILE, tile)

        return emit

    def emit_down(parts):
        def tile(t):
            out_d[cols(t), :] = total_of(mm_nt(same[...], v) for v in parts(cols(t)))

        loop(ff // TILE, tile)

    def emit_out(parts):
        lanes = pl.ds(0, q_wide)
        out_o[...] = total_of(mm_nt(pick_end[...], v) for v in parts(lanes))

    def emit_qkv(parts):
        kv_rows = nkv * HD
        lanes = pl.ds(0, q_wide)
        out_q[...] = total_of(mm_nt(v, pick_rope[...]) for v in parts(lanes))
        lanes = pl.ds(q_wide, kv_wide)
        pick = pick_rope[0:kv_rows, 0:kv_wide]
        out_k[...] = total_of(mm_nt(v, pick) for v in parts(lanes))
        lanes = pl.ds(q_wide + kv_wide, kv_wide)
        pick = pick_end[0:kv_rows, 0:kv_wide]
        out_v[...] = total_of(mm_nt(v, pick) for v in parts(lanes))

    def turn(src, dst):
        def lane_block(t):
            dst[cols(t, LANES), :] = src[pl.ds(0, total), cols(t, LANES)].T

        loop(width // LANES, lane_block)

    def at(s, work):
        if s == 0:
            work(d)
            return

        def side(i):
            j = d - s + 2 * s * i

            @pl.when((j >= 0) & (j < n))
            def _():
                work(j)

        loop(2, side)

    def one_hot(split):
        shape = (nq * HD, q_wide)
        row = lax.broadcasted_iota(jnp.int32, shape, 0)
        lane = lax.broadcasted_iota(jnp.int32, shape, 1)
        inside = lane % LANES
        start = (lane // LANES) * HD
        if split:
            gap = LANES // 2 - HALF
            upper = inside >= LANES // 2
            source = start + jnp.where(upper, inside - gap, inside)
            real = (inside % (LANES // 2)) < HALF
        else:
            source = start + inside
            real = inside < HD
        return jnp.where(real & (row == source), 1.0, 0.0).astype(BF)

    pick_rope[...] = one_hot(True)
    pick_end[...] = one_hot(False)
    square = (TILE, TILE)
    same[...] = jnp.where(
        lax.broadcasted_iota(jnp.int32, square, 0) == lax.broadcasted_iota(jnp.int32, square, 1),
        1.0,
        0.0,
    ).astype(BF)
    mine = span(f, shard)
    kv_rows = nkv * HD
    weights[0][mine, 0:q_wide] = mm(w_q[...], pick_rope[...]).astype(BF)
    weights[0][mine, q_wide : q_wide + kv_wide] = mm(
        w_k[...], pick_rope[0:kv_rows, 0:kv_wide]
    ).astype(BF)
    weights[0][mine, q_wide + kv_wide : q_wide + 2 * kv_wide] = mm(
        w_v[...], pick_end[0:kv_rows, 0:kv_wide]
    ).astype(BF)
    eye = same[0:shard, 0:shard]
    weights[1][mine, :] = mm(mm_nt(eye, w_o[...]).astype(BF), pick_end[...]).astype(BF)
    weights[4][mine, :] = mm_nt(eye, w_d[...]).astype(BF)
    gains_in[...] = jnp.zeros((8, width), F32)
    gains_in[0:1, 0:shard] = gain_a[...].astype(F32)
    gains_in[1:2, 0:shard] = gain_m[...].astype(F32)
    block(gain_in, f, 8)[...] = pltpu.roll(gains_in[...], f * shard, 1)

    gathers = [
        Gather(0, weights[0], shard),
        Gather(1, weights[1], shard),
        Gather(2, weights[2], shard, w_g),
        Gather(3, weights[3], shard, w_u),
        Gather(4, weights[4], shard),
    ]
    gain_gather = Gather(5, gain_in, 8)
    tok_line = Line(0, x_buf, src=tokens)
    cot_line = Line(1, ct_buf, src=cot)
    mi_line = Line(2, mi_buf, parts=2)
    gm_line = Line(3, gm_buf, parts=2)
    gain_line = Line(4, gain_z, 8)

    block(x_buf, d)[...] = tokens[...]
    block(ct_buf, d)[...] = cot[...]

    def segments(b, shape, dim):
        index = lax.broadcasted_iota(jnp.int32, shape, dim)
        segment = jnp.zeros(shape, jnp.int32)
        offset = jnp.zeros(shape, jnp.int32)
        end = jnp.int32(0)
        for k in range(nseq):
            end = end + lengths[b, k]
            past = index >= end
            segment = segment + past.astype(jnp.int32)
            offset = jnp.where(past, end, offset)
        return index, segment, offset

    def tables(b):
        index, _, offset = segments(b, (rows, LANES), 0)
        angle = (index - offset).astype(F32) * freq[...]
        lane = lax.broadcasted_iota(jnp.int32, (rows, LANES), 1)
        sine = jnp.sin(angle)
        block(cos_t, b)[...] = jnp.cos(angle)
        block(sin_t, b)[...] = jnp.where(lane < LANES // 2, -sine, sine)

    pl.semaphore_wait(barrier, chips + 2 - ends)
    tok_line.start()
    gain_gather.start()
    gathers[0].start()
    gathers[1].start()
    loop(n, tables)
    gain_gather.relay()
    gain_gather.forward()
    gain_gather.finish()
    gain_row[...] = total_of(gain_in[pl.ds(8 * k, 8), :] for k in range(nf))

    def rms(value):
        mean = jnp.sum(value * value, axis=-1, keepdims=True) / width
        return lax.rsqrt(mean + EPSILON)

    def norm_one(j):
        def some(i):
            r = pl.ds(pl.multiple_of(j * rows + i * CHUNK, CHUNK), CHUNK)
            value = x_buf[r, :].astype(F32)
            scale = rms(value)
            sc_one[r, :] = scale
            mi_buf[r, :] = (value * scale * gain_row[0:1, :]).astype(BF)

        loop(rows // CHUNK, some)

    def rope(value, sign, cos_v, sin_v):
        return value * cos_v + sign * (pltpu.roll(value, LANES // 2, 1) * sin_v)

    heads = nq + 2 * nkv

    def head(ref, r, h):
        return ref[r, h * LANES : (h + 1) * LANES]

    def attend(b):
        r = span(b, rows)
        cos_v, sin_v = cos_t[r, :], sin_t[r, :]
        for t in range(heads // 2):
            both = mm(mi_buf[r, :], weights[0][:, 2 * t * LANES : 2 * (t + 1) * LANES])
            for h in (2 * t, 2 * t + 1):
                value = both[:, (h - 2 * t) * LANES : (h - 2 * t + 1) * LANES]
                if h < nq + nkv:
                    value = rope(value, 1.0, cos_v, sin_v)
                qkv[r, h * LANES : (h + 1) * LANES] = value.astype(BF)
        t_index, t_seg, _ = segments(b, (rows, rows), 0)
        s_index, s_seg, _ = segments(b, (rows, rows), 1)
        allowed = (t_seg == s_seg) & (s_index <= t_index)
        for h in range(nq):
            kv = h // (nq // nkv)
            score = mm_nt(head(qkv, r, h), head(qkv, r, nq + kv)) * HD ** (-0.5)
            score = jnp.where(allowed, score, NEG_FILL)
            top = jnp.max(score, axis=-1, keepdims=True)
            log_total = top + jnp.log(jnp.sum(jnp.exp(score - top), axis=-1, keepdims=True))
            prob = jnp.where(allowed, jnp.exp(score - log_total), 0.0)
            probs[b * nq + h] = prob
            mixed[r, h * LANES : (h + 1) * LANES] = mm(
                prob.astype(BF), head(qkv, r, nq + nkv + kv)
            ).astype(BF)

    norm_one(d)
    tok_line.step(1)
    gathers[0].relay()
    gathers[2].start()
    at(1, norm_one)
    early = min(2, n - 1)
    if early == 2:
        tok_line.step(2)
        at(2, norm_one)
    gathers[1].relay()
    gathers[3].start()
    gathers[0].forward()
    gathers[0].finish()
    for s in range(early + 1):
        at(s, attend)
    gathers[2].relay()
    gathers[4].start()
    gathers[1].forward()
    for s in range(early + 1, n):
        tok_line.step(s)
        at(s, norm_one)
        at(s, attend)
    gathers[1].finish()

    def by_turned(pairs, also=None):
        def tiles_of(j, put):
            r = span(j, rows)

            def tile(t):
                value = total_of(mm_nt(left[r, :], weight[cols(t), :]) for left, weight in pairs)
                put(t, value)
                if also is not None:
                    also(j, t, value)

            loop(width // TILE, tile)

        return tiles_of

    def run(work):
        if work:
            todo = work.pop(0)
            if todo is not None:
                todo()

    def reduce_then_gather(red, finish_half, line, work):
        red.compute()
        run(work)
        for s in range(n - 2, 0, -1):
            red.advance(s, 0)
            run(work)
        red.advance(n - 1, 1)
        red.final(0)
        finish_half(0)
        line.start(0)
        for i in range(1, n - 1):
            red.advance(n - 1 - i, 1)
            run(work)
            line.step(i, 0)
        red.final(1)
        finish_half(1)
        line.start(1)
        line.step(n - 1, 0)

    def norm_two(h):
        def some(i):
            r = pl.ds(pl.multiple_of(h * half + i * CHUNK, CHUNK), CHUNK)
            value = tokens[r, :].astype(F32) + own_sum[r, :]
            scale = rms(value)
            middle[r, :] = value
            sc_two[r, :] = scale
            here = pl.ds(pl.multiple_of(d * rows + h * half + i * CHUNK, CHUNK), CHUNK)
            mi_buf[here, :] = (value * scale * gain_row[1:2, :]).astype(BF)

        loop(half // CHUNK, some)

    def up_stage():
        gathers[3].relay()
        gathers[2].forward()

    def down_stage():
        gathers[4].relay()
        gathers[3].forward()

    def cot_step(s):
        return lambda: cot_line.step(s)

    after_attn = Reduce(0, by_turned([(mixed, weights[1])]), s_buf, r_buf)
    work = [cot_line.start, up_stage, None, cot_step(1), down_stage]
    work += [cot_step(s) for s in range(2, n)]
    reduce_then_gather(after_attn, norm_two, mi_line, work)
    while work:
        run(work)
    gathers[4].forward()
    for g in (2, 3, 4):
        gathers[g].finish()

    def feed(j):
        r = span(j, rows)

        def tile(t):
            left = mi_buf[r, :]
            gate = mm(left, weights[2][:, cols(t)])
            up = mm(left, weights[3][:, cols(t)])
            grad_hidden = mm(ct_buf[r, :], weights[4][:, cols(t)])
            sig = 1.0 / (1.0 + jnp.exp(-gate))
            hid[r, cols(t)] = (gate * sig * up).astype(BF)
            gu[r, cols(t)] = (grad_hidden * gate * sig).astype(BF)
            gg[r, cols(t)] = (grad_hidden * up * sig * (1.0 + gate * (1.0 - sig))).astype(BF)

        loop(ff // TILE, tile)

    mi_line.step(1, 1)
    at(0, feed)
    at(1, feed)
    for s in range(2, n):
        mi_line.step(s, 1)
        if s == 2:
            turn(ct_buf, t_one)
        at(s, feed)
    if n == 2:
        turn(ct_buf, t_one)
    after_attn.drain()
    mi_line.drain()
    cot_line.drain()

    gain_own = block(gain_z, d, 8)
    gain_own[...] = jnp.zeros((8, width), F32)

    def back_two(h):
        def some(i):
            r = pl.ds(pl.multiple_of(h * half + i * CHUNK, CHUNK), CHUNK)
            term = own_sum[r, :]
            scale = sc_two[r, :]
            normed = middle[r, :] * scale
            gain_sum = jnp.sum(term * normed, axis=0, keepdims=True)
            dn = term * gain_row[1:2, :]
            mean = jnp.sum(dn * normed, axis=-1, keepdims=True) / width
            value = cot[r, :].astype(F32) + scale * (dn - normed * mean)
            gmid[r, :] = value
            here = pl.ds(pl.multiple_of(d * rows + h * half + i * CHUNK, CHUNK), CHUNK)
            gm_buf[here, :] = value.astype(BF)
            gain_own[1:2, :] = gain_own[1:2, :] + gain_sum

        loop(half // CHUNK, some)

    after_mlp = Reduce(1, by_turned([(gg, weights[2]), (gu, weights[3])]), s_buf, r_buf)
    down = Grad(4, t_one, hid, emit_down)
    gate_g = Grad(2, t_two, gg, emit_plain(out_g))
    up_g = Grad(3, t_two, gu, emit_plain(out_u))

    def turn_mi():
        turn(mi_buf, t_two)

    work = [turn_mi, down.send_all, down.own_all, gate_g.send_all, gate_g.own_all]
    reduce_then_gather(after_mlp, back_two, gm_line, work)
    while work:
        run(work)
    after_mlp.drain()

    def back(b):
        r = span(b, rows)

        def tile(t):
            gmixed[r, cols(t)] = mm(gm_buf[r, :], weights[1][:, cols(t)]).astype(BF)

        loop(q_wide // TILE, tile)
        cos_v, sin_v = cos_t[r, :], sin_t[r, :]
        group = nq // nkv
        for kv in range(nkv):
            key, val = head(qkv, r, nq + kv), head(qkv, r, nq + nkv + kv)
            grad_k = grad_v = None
            for h in range(kv * group, (kv + 1) * group):
                query, gm_h = head(qkv, r, h), head(gmixed, r, h)
                prob = probs[b * nq + h]
                delta = jnp.sum(
                    gm_h.astype(F32) * head(mixed, r, h).astype(F32), axis=-1, keepdims=True
                )
                grad_p = mm_nt(gm_h, val)
                grad_s = (prob * (grad_p - delta) * HD ** (-0.5)).astype(BF)
                grad_q = mm(grad_s, key)
                gqkv[r, h * LANES : (h + 1) * LANES] = rope(grad_q, -1.0, cos_v, sin_v).astype(BF)
                k_term, v_term = mm_tn(grad_s, query), mm_tn(prob.astype(BF), gm_h)
                grad_k = k_term if grad_k is None else grad_k + k_term
                grad_v = v_term if grad_v is None else grad_v + v_term
            k_at, v_at = (nq + kv) * LANES, (nq + nkv + kv) * LANES
            gqkv[r, k_at : k_at + LANES] = rope(grad_k, -1.0, cos_v, sin_v).astype(BF)
            gqkv[r, v_at : v_at + LANES] = grad_v.astype(BF)

    output = Reduce(2, by_turned([(hid, weights[4])]), ct_buf, mi_buf)

    gm_line.step(1, 1)
    at(0, back)
    at(1, back)
    for s in range(2, n):
        gm_line.step(s, 1)
        at(s, back)

    def add_gain(j, t, value):
        r = span(j, rows)
        normed = x_buf[r, cols(t)].astype(F32) * sc_one[r, :]
        gain_own[0:1, cols(t)] = gain_own[0:1, cols(t)] + jnp.sum(
            value * normed, axis=0, keepdims=True
        )

    def write_out(h):
        def some(i):
            r = pl.ds(pl.multiple_of(h * half + i * CHUNK, CHUNK), CHUNK)
            out_ref[r, :] = (middle[r, :] + own_sum[r, :]).astype(BF)

        loop(half // CHUNK, some)

    output.compute()
    work = [up_g.send_all, up_g.own_all]
    for s in range(n - 1, 0, -1):
        if s < n - 1:
            output.advance(s, 0)
        output.advance(s, 1)
        run(work)
    while work:
        run(work)
    for h in range(2):
        output.final(h)
        write_out(h)

    after_in = Reduce(3, by_turned([(gqkv, weights[0])], add_gain), s_buf, r_buf)
    out_g_grad = Grad(1, t_one, mixed, emit_out)
    qkv_g = Grad(0, t_two, gqkv, emit_qkv)

    def turn_attn_in():
        def one(b):
            there = span(b, rows)

            def lane_block(t):
                value = x_buf[there, cols(t, LANES)].astype(F32) * sc_one[there, :]
                value = (value * gain_row[0:1, cols(t, LANES)]).astype(BF)
                t_two[cols(t, LANES), cols(b, rows)] = value.T

            loop(width // LANES, lane_block)

        loop(n, one)

    def turn_gm():
        turn(gm_buf, t_one)

    after_in.compute()
    gain_line.start()
    turn_attn_in()
    qkv_g.send_all()
    work = [qkv_g.own_all, turn_gm, out_g_grad.send_all, out_g_grad.own_all]
    steps = list(range(1, n))
    for s in range(n - 1, 0, -1):
        if s < n - 1:
            after_in.advance(s, 0)
        after_in.advance(s, 1)
        run(work)
        if steps:
            gain_line.step(steps.pop(0))
    while work:
        run(work)
    block(gain_f, f, 8)[...] = total_of(gain_z[pl.ds(8 * k, 8), :] for k in range(n))
    gain_back = Gather(6, gain_f, 8)
    gain_back.start()
    down.finish()
    gate_g.finish()
    gain_back.relay()
    gain_back.forward()
    up_g.finish()

    def back_one(h):
        def some(i):
            r = pl.ds(pl.multiple_of(h * half + i * CHUNK, CHUNK), CHUNK)
            there = pl.ds(pl.multiple_of(d * rows + h * half + i * CHUNK, CHUNK), CHUNK)
            scale = sc_one[there, :]
            normed = tokens[r, :].astype(F32) * scale
            dm = own_sum[r, :] * gain_row[0:1, :]
            mean = jnp.sum(dm * normed, axis=-1, keepdims=True) / width
            gtok_ref[r, :] = gmid[r, :] + scale * (dm - normed * mean)

        loop(half // CHUNK, some)

    for h in range(2):
        after_in.final(h)
        back_one(h)
    qkv_g.finish()
    out_g_grad.finish()
    gain_back.finish()
    gain_sum = total_of(gain_f[pl.ds(8 * k, 8), :] for k in range(nf))
    gain_sum = pltpu.roll(gain_sum, (width - f * shard) % width, 1)
    out_ga[...] = gain_sum[0:1, 0:shard]
    out_gm[...] = gain_sum[1:2, 0:shard]

    output.drain()
    after_in.drain()
    for line in (tok_line, gm_line, gain_line):
        line.drain()
    for gather in gathers + [gain_gather, gain_back]:
        gather.drain()


def pass_on(*refs):
    count = (len(refs) - 2) // 3
    srcs, dsts, held = refs[:count], refs[count : 2 * count], refs[2 * count : 3 * count]
    in_sem, out_sem = refs[3 * count :]
    order = range(count)
    for i in order:
        pltpu.make_async_copy(srcs[i], held[i], in_sem.at[i]).start()
    for i in order:
        pltpu.make_async_copy(srcs[i], held[i], in_sem.at[i]).wait()
        pltpu.make_async_copy(held[i], dsts[i], out_sem.at[i]).start()
    for i in order:
        pltpu.make_async_copy(held[i], dsts[i], out_sem.at[i]).wait()


def run_layer(lengths, freq, tokens, cot, gain_a, gain_m, w_q, w_k, w_v, w_o, w_d, w_g, w_u, n, chips):
    rows, width = tokens.shape
    nq = w_q.shape[1] // HD
    nkv = w_k.shape[1] // HD
    total = n * rows
    nf = 2 * chips
    shard = w_q.shape[0]
    ff = w_g.shape[1]
    q_wide, kv_wide = nq * LANES, nkv * LANES
    widths = (q_wide + 2 * kv_wide, q_wide, ff, ff, ff)
    dims = (n, chips, rows, width, nq, nkv, ff, lengths.shape[1])
    vmem = pl.BlockSpec(memory_space=pltpu.VMEM)
    anywhere = pl.BlockSpec(memory_space=pl.ANY)
    results = [
        jax.ShapeDtypeStruct((rows, width), BF),
        jax.ShapeDtypeStruct((rows, width), F32),
        jax.ShapeDtypeStruct((1, shard), F32),
        jax.ShapeDtypeStruct((1, shard), F32),
    ] + [jax.ShapeDtypeStruct(w.shape, F32) for w in (w_q, w_k, w_v, w_o, w_g, w_u, w_d)]
    out_shape = results + [jax.ShapeDtypeStruct((chips - 1, shard, w), BF) for w in widths]
    widest = max(widths)
    scratch = (
        [pltpu.VMEM((width, w), BF) for w in widths]
        + [
            pltpu.VMEM((total, width), BF),
            pltpu.VMEM((total, width), BF),
            pltpu.VMEM((total + rows, width), BF),
            pltpu.VMEM((total, width), BF),
            pltpu.VMEM((total, widths[0]), BF),
            pltpu.VMEM((total, widths[0]), BF),
            pltpu.VMEM((n * nq, rows, rows), F32),
            pltpu.VMEM((total, q_wide), BF),
            pltpu.VMEM((total, q_wide), BF),
            pltpu.VMEM((total, ff), BF),
            pltpu.VMEM((total, ff), BF),
            pltpu.VMEM((total, ff), BF),
            pltpu.VMEM((width, total), BF),
            pltpu.VMEM((width, total), BF),
            pltpu.VMEM((total, width), BF),
            pltpu.VMEM((total + rows, width), BF),
            pltpu.VMEM((rows, width), F32),
            pltpu.VMEM((rows, width), F32),
            pltpu.VMEM((rows, width), F32),
            pltpu.VMEM((total, 1), F32),
            pltpu.VMEM((rows, 1), F32),
            pltpu.VMEM((total, LANES), F32),
            pltpu.VMEM((total, LANES), F32),
            pltpu.VMEM((8, width), F32),
            pltpu.VMEM((nf * 8, width), F32),
            pltpu.VMEM((8, width), F32),
            pltpu.VMEM((n * 8, width), F32),
            pltpu.VMEM((nf * 8, width), F32),
            pltpu.VMEM((chips - 1, shard, widest), BF),
            pltpu.VMEM((nq * HD, q_wide), BF),
            pltpu.VMEM((nq * HD, q_wide), BF),
            pltpu.VMEM((TILE, TILE), BF),
            pltpu.VMEM((chips, shard, widest), BF),
        ]
        + [pltpu.VMEM((chips, shard, w), BF) for w in widths]
        + [pltpu.VMEM((chips, shard, w), BF) for w in widths]
        + [
            pltpu.SemaphoreType.DMA((7, chips)),
            pltpu.SemaphoreType.DMA((7, chips)),
            pltpu.SemaphoreType.DMA((7, chips)),
            pltpu.SemaphoreType.DMA((7, nf)),
            pltpu.SemaphoreType.DMA((7,)),
            pltpu.SemaphoreType.DMA((5, 2, 2, n)),
            pltpu.SemaphoreType.DMA((5, 2, n)),
            pltpu.SemaphoreType.DMA((4, 2, n)),
            pltpu.SemaphoreType.DMA((4, 2, n + 1)),
            pltpu.SemaphoreType.DMA((5, chips)),
            pltpu.SemaphoreType.DMA((5, chips)),
            pltpu.SemaphoreType.DMA((5, chips)),
            pltpu.SemaphoreType.DMA((5, chips)),
            pltpu.SemaphoreType.DMA((chips,)),
        ]
    )
    made = pl.pallas_call(
        partial(layer_kernel, dims),
        out_shape=out_shape,
        in_specs=[pl.BlockSpec(memory_space=pltpu.SMEM)] + [vmem] * 10 + [anywhere] * 2,
        out_specs=[vmem] * 11 + [anywhere] * 5,
        scratch_shapes=scratch,
        compiler_params=pltpu.CompilerParams(
            collective_id=0, has_side_effects=True, vmem_limit_bytes=67043328
        ),
        name="layer",
    )(lengths, freq, tokens, cot, gain_a, gain_m, w_q, w_k, w_v, w_o, w_d, w_g, w_u)
    count = len(results)
    return pl.pallas_call(
        pass_on,
        out_shape=results,
        in_specs=[anywhere] * count,
        out_specs=[anywhere] * count,
        scratch_shapes=[pltpu.VMEM(r.shape, r.dtype) for r in results]
        + [pltpu.SemaphoreType.DMA((count,)), pltpu.SemaphoreType.DMA((count,))],
        compiler_params=pltpu.CompilerParams(vmem_limit_bytes=32 * 2**20),
        name="results",
    )(*made[:count])


def body(
    n,
    chips,
    tokens,
    lengths,
    cotangent,
    attn_gain,
    w_query,
    w_key,
    w_value,
    w_out,
    mlp_gain,
    w_gate,
    w_up,
    w_down,
):
    frequency = ROPE_BASE ** (-jnp.arange(HALF, dtype=F32) / HALF)
    frequency = jnp.pad(frequency, (0, LANES // 2 - HALF))
    freq = jnp.concatenate([frequency, frequency])[None, :]
    results = run_layer(
        lengths,
        freq,
        tokens,
        cotangent,
        attn_gain,
        mlp_gain,
        w_query[0],
        w_key[0],
        w_value[0],
        w_out[0],
        w_down[0],
        w_gate[0],
        w_up[0],
        n,
        chips,
    )
    output, grad_tokens, g_again, g_mgain, g_q, g_k, g_v, g_o, g_gate, g_up, g_down = results
    return (
        output,
        grad_tokens,
        g_again,
        g_q[None],
        g_k[None],
        g_v[None],
        g_o[None],
        g_mgain,
        g_gate[None],
        g_up[None],
        g_down[None],
    )


def solution(mesh):
    placed = (
        P(("fsdp", "dp"), None),
        P("fsdp", None),
        P(("fsdp", "dp"), None),
        P(None, "fsdp"),
        P(None, "fsdp", "dp"),
        P(None, "fsdp", "dp"),
        P(None, "fsdp", "dp"),
        P(None, "dp", "fsdp"),
        P(None, "fsdp"),
        P(None, "fsdp", "dp"),
        P(None, "fsdp", "dp"),
        P(None, "dp", "fsdp"),
    )
    return jax.shard_map(
        partial(body, mesh.shape["dp"], mesh.shape["fsdp"] // 2),
        mesh=mesh,
        in_specs=placed,
        out_specs=(
            P(("fsdp", "dp"), None),
            P(("fsdp", "dp"), None),
            P(None, "fsdp"),
            P(None, "fsdp", "dp"),
            P(None, "fsdp", "dp"),
            P(None, "fsdp", "dp"),
            P(None, "dp", "fsdp"),
            P(None, "fsdp"),
            P(None, "fsdp", "dp"),
            P(None, "fsdp", "dp"),
            P(None, "dp", "fsdp"),
        ),
        check_vma=False,
    )
```

time: 262 us -> 303 us (1.16)
  Pallas kernels: 241 us -> 284 us
    pallas_call x1, Pallas kernels: 241 us -> 281 us  [run_layer(): pl.pallas_call(partial(layer_kernel, dims), out_shape=out_shape, in_specs...]
    unnamed x33 -> x26, local copies, waits for them, and re-layouts: 8.92 us -> 16.4 us
    pallas_call x0 -> x1, Pallas kernels: none -> 3.21 us  [run_layer(): pl.pallas_call(pass_on, out_shape=results, in_specs=[anywhere] * count, o...]
where the time goes in v3:
time: 303 us; the launch traced here: 302 us
  Pallas kernels  284 us (94%)
  local copies, waits for them, and re-layouts  16.4 us (5%)
    pallas_call x1, Pallas kernels, run_layer(): pl.pallas_call(partial(layer_kernel, dims), out_shape=out_shape, in_specs...  281 us
    unnamed x26, local copies, waits for them, and re-layouts  16.4 us

profile of v3, /device:TPU:8, one launch (start us, length us, event | category | flops | bytes accessed | tf_op | source)
XLA Modules:
  0.0 301.8 jit_solution(11535813739312371757)
XLA Ops:
  0.7 0.6 maximum_bitcast_fusion.refs_1_
  1.3 1.7 copy.23
  3.0 2.0 copy.24
  5.0 280.9 %layer.1 = (bf16[128,1536]{1,0:T(8,128)(2,1)}, f32[128,1536]{1,0:T(8,128)}, f32[1,192]{1,0:T(1,128)}, f32[1,192]{1,0:T(1,128)}, f32[192,384]{1,0:T(8,128)}, /*in...) custom-call(s32[4,4]{1,0:T(4,128)} %refs_0_.1, ...), custom_call_target="tpu_custom_call" | custom-call | tf_op jit(solution)/shard_map/layer/pallas_call | solution.py:1069
  285.9 0.0 copy-start
  285.9 1.2 copy-done
  287.1 0.0 copy-start.1
  287.1 1.1 copy-done.1
  288.2 0.0 copy-start.2
  288.2 1.1 copy-done.2
  289.3 0.0 copy-start.3
  289.4 1.1 copy-done.3
  290.5 0.0 copy-start.4
  290.5 1.0 copy-done.4
  291.5 0.0 copy-start.5
  291.5 1.0 copy-done.5
  292.5 1.0 copy-done.6
  293.4 0.9 copy-done.7
  294.4 0.9 copy-done.8
  295.3 0.6 copy-done.9
  295.9 0.6 copy-done.10
  296.5 3.2 %results.1 = (bf16[128,1536]{1,0:T(8,128)(2,1)}, f32[128,1536]{1,0:T(8,128)}, f32[1,192]{1,0:T(1,128)}, f32[1,192]{1,0:T(1,128)}, f32[192,384]{1,0:T(8,128)}, /*...) custom-call(bf16[128,1536]{1,0:T(8,128)(2,1)S(1)} %copy-done.4, ...), custom_call_target="tpu_custom_call" | custom-call | tf_op jit(solution)/shard_map/results/pallas_call | solution.py:1081
  299.8 0.9 copy.25
  300.6 1.2 copy.26
  (7 shorter events, 0.0 us)
Async XLA Ops:
  285.9 1.2 copy-start
  287.1 1.1 copy-start.1
  288.2 1.1 copy-start.2
  289.3 1.1 copy-start.3
  290.5 1.0 copy-start.4
  291.5 1.0 copy-start.5
  292.5 1.0 copy-start.6
  293.4 0.9 copy-start.7
  294.4 0.9 copy-start.8
  295.3 0.6 copy-start.9
  295.9 0.6 copy-start.10

commit v4 on v3

--- a/solution.py
+++ b/solution.py
@@ -57,6 +57,7 @@
     half = rows // 2
     q_wide, kv_wide = nq * LANES, nkv * LANES
     widths = (q_wide + 2 * kv_wide, q_wide, ff, ff, ff)
+    widest = max(widths)
     near = [1] if chips > 1 else []
     far = [2 * k for k in range(1, chips // 2)]
     refs = list(refs)
@@ -66,24 +67,29 @@
         del refs[:count]
         return taken
 
-    (lengths, freq, tokens, cot, gain_a, gain_m, w_q, w_k, w_v, w_o, w_d, w_g, w_u) = take(13)
+    (lengths, freq, gain_a, gain_m) = take(4)
+    (tokens, cot, w_q, w_k, w_v, w_o, w_d, w_g, w_u) = take(9)
     (out_ref, gtok_ref, out_ga, out_gm, out_q, out_k, out_v, out_o, out_g, out_u, out_d) = take(11)
-    landing = take(5)
+    far_landing = take(3)
+    near_landing = take(2)
+    landing = near_landing + far_landing
     weights = take(5)
     (x_buf, ct_buf, mi_buf, gm_buf) = take(4)
     (qkv, gqkv, probs, mixed, gmixed, hid, gg, gu) = take(8)
     (t_one, t_two) = take(2)
-    (s_buf, r_buf, own_sum, middle, gmid) = take(5)
+    (s_buf, r_buf, own_sum, middle, gmid, wide_tile) = take(6)
     (sc_one, sc_two, cos_t, sin_t) = take(4)
-    (gains_in, gain_in, gain_row, gain_z, gain_f, stage) = take(6)
-    (pick_rope, pick_end, same) = take(3)
+    (gain_in, gain_row, gain_own, gain_z, gain_f, stage) = take(6)
+    (pick_rope, pick_end) = take(2)
+    (q_in, k_in, v_in, o_in) = take(4)
+    (out_own, q_own, k_own, v_own, o_own, big_own) = take(6)
     send_b = take(1)[0]
     sums = take(5)
     from_partner = take(5)
     (w_ss, w_fs, w_qs, w_rs, w_ls) = take(5)
     (z_ss, z_rs) = take(2)
     (rs_ss, rs_rs) = take(2)
-    (b_ss, b_rs, i_ss, i_rs, l_sem) = take(5)
+    (b_ss, b_rs, i_ss, i_rs, l_sem, in_sem, out_sem) = take(7)
 
     f = lax.axis_index("fsdp")
     d = lax.axis_index("dp")
@@ -111,6 +117,22 @@
 
     def cols(index, size=TILE):
         return span(index, size)
+
+    loads = [
+        pltpu.make_async_copy(src, dst, in_sem.at[i])
+        for i, (src, dst) in enumerate(
+            (
+                (w_q, q_in),
+                (w_k, k_in),
+                (w_v, v_in),
+                (w_o, o_in),
+                (tokens, block(x_buf, d)),
+                (cot, block(ct_buf, d)),
+            )
+        )
+    ]
+    for copy in loads:
+        copy.start()
 
     barrier = pltpu.get_barrier_semaphore()
     for k in range(1, chips):
@@ -119,21 +141,18 @@
         )
     pl.semaphore_signal(barrier, inc=1, device_id=at_f(partner), device_id_type=MESH)
 
-    @pl.when(d > 0)
-    def _():
-        pl.semaphore_signal(barrier, inc=1, device_id=at_d(d - 1), device_id_type=MESH)
-
-    @pl.when(d < n - 1)
-    def _():
-        pl.semaphore_signal(barrier, inc=1, device_id=at_d(d + 1), device_id_type=MESH)
-
-    ends = (d == 0).astype(jnp.int32) + (d == n - 1).astype(jnp.int32)
+    for k in range(1, n):
+        pl.semaphore_signal(
+            barrier, inc=1, device_id=at_d((d + k) % n), device_id_type=MESH
+        )
 
     class Gather:
-        def __init__(self, slot, dst, size, src=None):
+        def __init__(self, slot, dst, size, src=None, plain=False):
             self.slot, self.dst, self.size = slot, dst, size
             self.src = self.part(f) if src is None else src
             self.local = src is not None
+            self.aimed = list(range(1, chips)) if plain else near + far
+            self.plain = plain
 
         def part(self, index):
             return block(self.dst, index, self.size)
@@ -168,7 +187,7 @@
             return pltpu.make_async_copy(self.src, self.part(f), w_ls.at[self.slot])
 
         def start(self):
-            for k in near + far + [0]:
+            for k in self.aimed + [0]:
                 self.direct(k).start()
             if self.local:
                 self.own().start()
@@ -186,6 +205,13 @@
                         copy.start()
 
         def forward(self):
+            if self.plain:
+                for k in range(1, chips):
+                    copy = self.onward(k)
+                    copy.wait_recv()
+                    copy.start()
+                return
+
             for core, second in ((0, far), (1, near)):
 
                 @pl.when(c == core)
@@ -215,10 +241,12 @@
                 self.own().wait()
 
         def drain(self):
-            for k in near + far + [0]:
+            for k in self.aimed + [0]:
                 self.direct(k).wait_send()
             for k in range(1, chips):
                 self.onward(k).wait_send()
+            if self.plain:
+                return
             for k in near:
                 for other in far:
                     remote(
@@ -236,7 +264,9 @@
         def copy(self, index, side, h, own=False):
             piece = self.size // self.parts
             part = block(self.buf, index * self.parts + h, piece)
-            src = self.src if own and self.src is not None else part
+            src = part
+            if own and self.src is not None:
+                src = self.src.at[pl.ds(h * piece, piece)]
             where = d + 1 if side == 0 else d - 1
             return remote(
                 src,
@@ -255,24 +285,41 @@
             def _():
                 self.copy(d, 1, h, True).start()
 
+        def pass_on(self, index, side, h):
+            copy = self.copy(index, side, h)
+            copy.wait_recv()
+            copy.start()
+
+        def inward(self, s, h=0):
+            @pl.when((d > 0) & (d < n // 2) & (d + s < n))
+            def _():
+                self.pass_on(d + s, 1, h)
+
+            @pl.when((d < n - 1) & (d >= n // 2) & (d - s >= 0))
+            def _():
+                self.pass_on(d - s, 0, h)
+
+        def outward(self, s, h=0):
+            @pl.when((d < n // 2) & (d - s >= 0))
+            def _():
+                self.pass_on(d - s, 0, h)
+
+            @pl.when((d >= n // 2) & (d + s < n))
+            def _():
+                self.pass_on(d + s, 1, h)
+
         def step(self, s, h=0):
-            @pl.when(d - s >= 0)
-            def _():
-                copy = self.copy(d - s, 0, h)
-                copy.wait_recv()
-
-                @pl.when(d < n - 1)
-                def _():
-                    copy.start()
-
-            @pl.when(d + s < n)
-            def _():
-                copy = self.copy(d + s, 1, h)
-                copy.wait_recv()
-
-                @pl.when(d > 0)
-                def _():
-                    copy.start()
+            self.inward(s, h)
+            self.outward(s, h)
+
+        def arrive(self, s, h=0):
+            @pl.when((d - s >= 0) & (d == n - 1))
+            def _():
+                self.copy(d - s, 0, h).wait_recv()
+
+            @pl.when((d + s < n) & (d == 0))
+            def _():
+                self.copy(d + s, 1, h).wait_recv()
 
         def drain(self):
             for h in range(self.parts):
@@ -287,8 +334,9 @@
                         self.copy(j, 1, h).wait_send()
 
     class Reduce:
-        def __init__(self, slot, tiles_of, sends, gets):
-            self.slot, self.tiles_of, self.sends, self.gets = slot, tiles_of, sends, gets
+        def __init__(self, slot, tile_of, sends, gets, also=None):
+            self.slot, self.tile_of, self.sends, self.gets = slot, tile_of, sends, gets
+            self.also = also
 
         def copy(self, index, where, slot, h):
             return remote(
@@ -312,36 +360,30 @@
             return self.copy(index, d - 1, n if last else index, h)
 
         def compute(self):
-            def store(j):
-                def put(t, value):
-                    self.sends[span(j, rows), cols(t)] = value.astype(BF)
-
-                return put
-
-            def keep(t, value):
-                own_sum[:, cols(t)] = value
-
-            def one(i):
-                right, left = d + n - 1 - i, d - (n - 1 - i)
-
-                @pl.when(right < n)
-                def _():
-                    self.tiles_of(right, store(right))
-
-                @pl.when((right < n) & (i == 0))
-                def _():
-                    self.right(right, 0).start()
-
-                @pl.when(left >= 0)
-                def _():
-                    self.tiles_of(left, store(left))
-
-                @pl.when((left >= 0) & (i == 0))
-                def _():
-                    self.left(left, 0, n == 2).start()
-
-            loop(n - 1, one)
-            self.tiles_of(d, keep)
+            def tile(t):
+                value = self.tile_of(t)
+                wide_tile[...] = value
+                own_sum[:, cols(t)] = wide_tile[span(d, rows), :]
+                self.sends[pl.ds(0, total), cols(t)] = value.astype(BF)
+                if self.also is not None:
+                    self.also(t, value)
+
+            loop(width // TILE, tile)
+
+        def launch(self, halves_first):
+            order = [(s, h) for h in range(2) for s in range(n - 1, 0, -1)]
+            if not halves_first:
+                order = [(s, h) for s in range(n - 1, 0, -1) for h in range(2)]
+
+            @pl.when(d == 0)
+            def _():
+                for s, h in order:
+                    self.right(d + s, h).start()
+
+            @pl.when(d == n - 1)
+            def _():
+                for s, h in order:
+                    self.left(d - s, h, s == 1).start()
 
         def add_into(self, index, h):
             self.got(index, h)
@@ -357,23 +399,20 @@
         def advance(self, s, h):
             right, left = d + s, d - s
 
-            @pl.when(right < n)
-            def _():
-                @pl.when(d > 0)
-                def _():
-                    self.add_into(right, h)
-
+            @pl.when((right < n) & (d > 0))
+            def _():
+                self.add_into(right, h)
                 self.right(right, h).start()
 
-            @pl.when(left >= 0)
-            def _():
-                @pl.when(d < n - 1)
-                def _():
-                    self.add_into(left, h)
-
+            @pl.when((left >= 0) & (d < n - 1))
+            def _():
+                self.add_into(left, h)
                 self.left(left, h, s == 1).start()
 
         def final(self, h):
+            self.final_into(own_sum, h)
+
+        def final_into(self, acc, h):
             def add(slot):
                 self.got(slot, h)
 
@@ -382,7 +421,7 @@
                     there = pl.ds(
                         pl.multiple_of(slot * rows + h * half + i * CHUNK, CHUNK), CHUNK
                     )
-                    own_sum[r, :] = own_sum[r, :] + self.gets[there, :].astype(F32)
+                    acc[r, :] = acc[r, :] + self.gets[there, :].astype(F32)
 
                 loop(half // CHUNK, some)
 
@@ -401,19 +440,21 @@
                     @pl.when(d != j)
                     def _():
                         self.copy(j, d, j, h).wait_send()
+
+    handing = []
 
     class Grad:
         def __init__(self, group, turned, terms, emit):
             self.group, self.turned, self.terms, self.emit = group, turned, terms, emit
             self.width = widths[group]
 
-        def hand_over(self, k):
-            chip = flip(p, k)
+        def hand_over(self):
+            src = send_b if self.width == widest else send_b.at[:, :, pl.ds(0, self.width)]
             return remote(
-                send_b.at[k, :, pl.ds(0, self.width)],
-                from_partner[self.group].at[chip],
-                b_ss.at[self.group, k],
-                b_rs.at[self.group, chip],
+                src,
+                from_partner[self.group],
+                b_ss.at[self.group],
+                b_rs.at[self.group],
                 at_f(partner),
             )
 
@@ -427,41 +468,39 @@
                 at_f(chip * 2 + c),
             )
 
-        def send(self, k):
-            left = self.turned.at[span(flip(p, k) * 2 + 1 - c, shard)]
+        def blocks_of(self, core, t):
+            left = jnp.concatenate(
+                [self.turned[span(q * 2 + core, shard), :] for q in range(chips)], axis=0
+            )
+            value = mm(left, self.terms[:, cols(t)])
+            return [value[q * shard : (q + 1) * shard] for q in range(chips)]
+
+        def release(self):
+            self.hand_over().wait_send()
+
+        def send_all(self):
+            if handing:
+                handing.pop().release()
 
             def tile(t):
-                send_b[k, :, cols(t)] = mm(left[...], self.terms[:, cols(t)]).astype(BF)
+                for q, value in enumerate(self.blocks_of(1 - c, t)):
+                    send_b[q, :, cols(t)] = value.astype(BF)
 
             loop(self.width // TILE, tile)
-            self.hand_over(k).start()
-
-        def own(self, k):
-            chip = flip(p, k)
-            left = self.turned.at[span(chip * 2 + c, shard)]
-            part = from_partner[self.group].at[chip]
-            remote(
-                part, part, b_ss.at[self.group, k], b_rs.at[self.group, chip], at_f(partner)
-            ).wait_recv()
+            self.hand_over().start()
+            handing.append(self)
+
+        def own_all(self):
+            self.hand_over().wait_recv()
 
             def tile(t):
-                term = mm(left[...], self.terms[:, cols(t)])
-                other = from_partner[self.group][chip, :, cols(t)].astype(F32)
-                sums[self.group][chip, :, cols(t)] = (term + other).astype(BF)
+                for q, value in enumerate(self.blocks_of(c, t)):
+                    other = from_partner[self.group][q, :, cols(t)].astype(F32)
+                    sums[self.group][q, :, cols(t)] = (value + other).astype(BF)
 
             loop(self.width // TILE, tile)
-            if k > 0:
+            for k in range(1, chips):
                 self.ship(k).start()
-
-        def send_all(self):
-            for k in list(range(1, chips)) + [0]:
-                self.send(k)
-
-        def own_all(self):
-            for k in list(range(1, chips)) + [0]:
-                self.own(k)
-            for k in range(chips):
-                self.hand_over(k).wait_send()
 
         def fetch(self, k):
             return pltpu.make_async_copy(
@@ -470,17 +509,24 @@
                 l_sem.at[k - 1],
             )
 
-        def finish(self):
+        def collect(self):
             for k in range(1, chips):
                 self.ship(k).wait()
-                self.fetch(k).start()
-            for k in range(1, chips):
-                self.fetch(k).wait()
+                if self.group >= 2:
+                    self.fetch(k).start()
+
+        def finish(self):
+            if self.group >= 2:
+                for k in range(1, chips):
+                    self.fetch(k).wait()
 
             def parts(lanes):
                 yield sums[self.group][p, :, lanes]
                 for k in range(1, chips):
-                    yield stage[k - 1, :, lanes]
+                    if self.group >= 2:
+                        yield stage[k - 1, :, lanes]
+                    else:
+                        yield landing[self.group][k - 1, :, lanes]
 
             self.emit(parts)
 
@@ -490,35 +536,47 @@
             result = value if result is None else result + value
         return result
 
+    stores = []
+
+    def store(src, dst):
+        copy = pltpu.make_async_copy(src, dst, out_sem.at[len(stores)])
+        copy.start()
+        stores.append(copy)
+
     def emit_plain(out):
         def emit(parts):
             def tile(t):
-                out[:, cols(t)] = total_of(v.astype(F32) for v in parts(cols(t)))
-
+                big_own[:, cols(t)] = total_of(v.astype(F32) for v in parts(cols(t)))
+
+            if big_stores:
+                big_stores.pop().wait()
             loop(ff // TILE, tile)
+            copy = pltpu.make_async_copy(big_own, out, l_sem.at[chips - 1])
+            copy.start()
+            big_stores.append(copy)
 
         return emit
 
-    def emit_down(parts):
-        def tile(t):
-            out_d[cols(t), :] = total_of(mm_nt(same[...], v) for v in parts(cols(t)))
-
-        loop(ff // TILE, tile)
+    big_stores = []
 
     def emit_out(parts):
         lanes = pl.ds(0, q_wide)
-        out_o[...] = total_of(mm_nt(pick_end[...], v) for v in parts(lanes))
+        o_own[...] = total_of(mm_nt(v, pick_end[...]) for v in parts(lanes))
+        store(o_own, out_o)
 
     def emit_qkv(parts):
         kv_rows = nkv * HD
         lanes = pl.ds(0, q_wide)
-        out_q[...] = total_of(mm_nt(v, pick_rope[...]) for v in parts(lanes))
+        q_own[...] = total_of(mm_nt(v, pick_rope[...]) for v in parts(lanes))
+        store(q_own, out_q)
         lanes = pl.ds(q_wide, kv_wide)
         pick = pick_rope[0:kv_rows, 0:kv_wide]
-        out_k[...] = total_of(mm_nt(v, pick) for v in parts(lanes))
+        k_own[...] = total_of(mm_nt(v, pick) for v in parts(lanes))
+        store(k_own, out_k)
         lanes = pl.ds(q_wide + kv_wide, kv_wide)
         pick = pick_end[0:kv_rows, 0:kv_wide]
-        out_v[...] = total_of(mm_nt(v, pick) for v in parts(lanes))
+        v_own[...] = total_of(mm_nt(v, pick) for v in parts(lanes))
+        store(v_own, out_v)
 
     def turn(src, dst):
         def lane_block(t):
@@ -558,45 +616,46 @@
 
     pick_rope[...] = one_hot(True)
     pick_end[...] = one_hot(False)
-    square = (TILE, TILE)
-    same[...] = jnp.where(
-        lax.broadcasted_iota(jnp.int32, square, 0) == lax.broadcasted_iota(jnp.int32, square, 1),
-        1.0,
-        0.0,
-    ).astype(BF)
     mine = span(f, shard)
     kv_rows = nkv * HD
-    weights[0][mine, 0:q_wide] = mm(w_q[...], pick_rope[...]).astype(BF)
+    for copy in loads[:4]:
+        copy.wait()
+    weights[0][mine, 0:q_wide] = mm(q_in[...], pick_rope[...]).astype(BF)
     weights[0][mine, q_wide : q_wide + kv_wide] = mm(
-        w_k[...], pick_rope[0:kv_rows, 0:kv_wide]
+        k_in[...], pick_rope[0:kv_rows, 0:kv_wide]
     ).astype(BF)
     weights[0][mine, q_wide + kv_wide : q_wide + 2 * kv_wide] = mm(
-        w_v[...], pick_end[0:kv_rows, 0:kv_wide]
+        v_in[...], pick_end[0:kv_rows, 0:kv_wide]
     ).astype(BF)
-    eye = same[0:shard, 0:shard]
-    weights[1][mine, :] = mm(mm_nt(eye, w_o[...]).astype(BF), pick_end[...]).astype(BF)
-    weights[4][mine, :] = mm_nt(eye, w_d[...]).astype(BF)
-    gains_in[...] = jnp.zeros((8, width), F32)
-    gains_in[0:1, 0:shard] = gain_a[...].astype(F32)
-    gains_in[1:2, 0:shard] = gain_m[...].astype(F32)
-    block(gain_in, f, 8)[...] = pltpu.roll(gains_in[...], f * shard, 1)
+    weights[1][mine, :] = mm(o_in[...], pick_end[...]).astype(BF)
+    gain_mine = block(gain_in, f, 8)
+    gain_mine[...] = jnp.zeros(gain_mine.shape, F32)
+    gain_mine[0:1, 0:shard] = gain_a[...].astype(F32)
+    gain_mine[1:2, 0:shard] = gain_m[...].astype(F32)
 
     gathers = [
-        Gather(0, weights[0], shard),
-        Gather(1, weights[1], shard),
+        Gather(0, weights[0], shard, plain=True),
+        Gather(1, weights[1], shard, plain=True),
         Gather(2, weights[2], shard, w_g),
         Gather(3, weights[3], shard, w_u),
-        Gather(4, weights[4], shard),
+        Gather(4, weights[4], shard, w_d),
     ]
-    gain_gather = Gather(5, gain_in, 8)
-    tok_line = Line(0, x_buf, src=tokens)
+    gain_gather = Gather(5, gain_in, 8, plain=True)
+    tok_line = Line(0, x_buf, parts=2, src=tokens)
     cot_line = Line(1, ct_buf, src=cot)
     mi_line = Line(2, mi_buf, parts=2)
     gm_line = Line(3, gm_buf, parts=2)
-    gain_line = Line(4, gain_z, 8)
-
-    block(x_buf, d)[...] = tokens[...]
-    block(ct_buf, d)[...] = cot[...]
+
+    def gain_swap(k):
+        mine = block(gain_z, d, 8)
+        return remote(
+            mine, mine, z_ss.at[4, 0, 0, k], z_rs.at[4, 0, d], at_d((d + k) % n)
+        )
+
+    def gain_got(k):
+        other = (d + k) % n
+        part = block(gain_z, other, 8)
+        remote(part, part, z_ss.at[4, 0, 0, k], z_rs.at[4, 0, other], at_d(d)).wait_recv()
 
     def segments(b, shape, dim):
         index = lax.broadcasted_iota(jnp.int32, shape, dim)
@@ -618,16 +677,25 @@
         block(cos_t, b)[...] = jnp.cos(angle)
         block(sin_t, b)[...] = jnp.where(lane < LANES // 2, -sine, sine)
 
-    pl.semaphore_wait(barrier, chips + 2 - ends)
-    tok_line.start()
+    loop(n, tables)
+    pl.semaphore_wait(barrier, chips + n - 1)
+    for h in range(2):
+        tok_line.start(h)
     gain_gather.start()
     gathers[0].start()
     gathers[1].start()
-    loop(n, tables)
-    gain_gather.relay()
+
+    @pl.when((d == 0) | (d == n - 1))
+    def _():
+        cot_line.start()
+
+    for g in range(2, 5):
+        gathers[g].start()
+    loads[4].wait()
     gain_gather.forward()
     gain_gather.finish()
-    gain_row[...] = total_of(gain_in[pl.ds(8 * k, 8), :] for k in range(nf))
+    for k in range(nf):
+        gain_row[:, k * shard : (k + 1) * shard] = gain_in[8 * k : 8 * k + 8, 0:shard]
 
     def rms(value):
         mean = jnp.sum(value * value, axis=-1, keepdims=True) / width
@@ -676,43 +744,44 @@
                 prob.astype(BF), head(qkv, r, nq + nkv + kv)
             ).astype(BF)
 
+    def tokens_at(s):
+        for h in range(2):
+            tok_line.step(s, h)
+            tok_line.arrive(s, h)
+
     norm_one(d)
-    tok_line.step(1)
-    gathers[0].relay()
-    gathers[2].start()
+    tokens_at(1)
     at(1, norm_one)
     early = min(2, n - 1)
     if early == 2:
-        tok_line.step(2)
+        for h in range(2):
+            tok_line.step(2, h)
+
+    @pl.when((d > 0) & (d < n - 1))
+    def _():
+        cot_line.start()
+
+    gathers[0].forward()
+    if early == 2:
+        for h in range(2):
+            tok_line.arrive(2, h)
         at(2, norm_one)
-    gathers[1].relay()
-    gathers[3].start()
-    gathers[0].forward()
     gathers[0].finish()
     for s in range(early + 1):
         at(s, attend)
-    gathers[2].relay()
-    gathers[4].start()
     gathers[1].forward()
+    cot_line.outward(1)
     for s in range(early + 1, n):
-        tok_line.step(s)
+        tokens_at(s)
         at(s, norm_one)
         at(s, attend)
     gathers[1].finish()
 
-    def by_turned(pairs, also=None):
-        def tiles_of(j, put):
-            r = span(j, rows)
-
-            def tile(t):
-                value = total_of(mm_nt(left[r, :], weight[cols(t), :]) for left, weight in pairs)
-                put(t, value)
-                if also is not None:
-                    also(j, t, value)
-
-            loop(width // TILE, tile)
-
-        return tiles_of
+    def by_turned(pairs):
+        def tile_of(t):
+            return total_of(mm_nt(left[...], weight[cols(t), :]) for left, weight in pairs)
+
+        return tile_of
 
     def run(work):
         if work:
@@ -722,55 +791,73 @@
 
     def reduce_then_gather(red, finish_half, line, work):
         red.compute()
+        red.launch(True)
         run(work)
         for s in range(n - 2, 0, -1):
             red.advance(s, 0)
             run(work)
-        red.advance(n - 1, 1)
         red.final(0)
         finish_half(0)
         line.start(0)
+        run(work)
         for i in range(1, n - 1):
             red.advance(n - 1 - i, 1)
+            if i == 1:
+                line.inward(i, 0)
             run(work)
-            line.step(i, 0)
         red.final(1)
         finish_half(1)
         line.start(1)
-        line.step(n - 1, 0)
+        for i in range(1, n - 1):
+            if i > 1:
+                line.inward(i, 0)
+            line.outward(i, 0)
+
+    def arrived(line, s):
+        line.step(s, 1)
+        line.arrive(s, 0)
+        line.arrive(s, 1)
 
     def norm_two(h):
         def some(i):
             r = pl.ds(pl.multiple_of(h * half + i * CHUNK, CHUNK), CHUNK)
-            value = tokens[r, :].astype(F32) + own_sum[r, :]
+            here = pl.ds(pl.multiple_of(d * rows + h * half + i * CHUNK, CHUNK), CHUNK)
+            value = x_buf[here, :].astype(F32) + own_sum[r, :]
             scale = rms(value)
             middle[r, :] = value
             sc_two[r, :] = scale
-            here = pl.ds(pl.multiple_of(d * rows + h * half + i * CHUNK, CHUNK), CHUNK)
             mi_buf[here, :] = (value * scale * gain_row[1:2, :]).astype(BF)
 
         loop(half // CHUNK, some)
 
-    def up_stage():
-        gathers[3].relay()
-        gathers[2].forward()
-
-    def down_stage():
-        gathers[4].relay()
-        gathers[3].forward()
-
-    def cot_step(s):
-        return lambda: cot_line.step(s)
+    def both(*todo):
+        def do():
+            for one in todo:
+                one()
+
+        return do
+
+    def cot_on(s):
+        def do():
+            cot_line.inward(s)
+            if s > 1:
+                cot_line.outward(s)
+
+        return do
 
     after_attn = Reduce(0, by_turned([(mixed, weights[1])]), s_buf, r_buf)
-    work = [cot_line.start, up_stage, None, cot_step(1), down_stage]
-    work += [cot_step(s) for s in range(2, n)]
+    work = [cot_on(1)]
+    work += [both(cot_on(2), gathers[2].relay)] if n > 2 else [gathers[2].relay]
+    work += [gathers[3].relay, None, gathers[4].relay, gathers[2].forward]
+    work += [cot_on(s) for s in range(3, n - 1)]
     reduce_then_gather(after_attn, norm_two, mi_line, work)
     while work:
         run(work)
+    gathers[3].forward()
     gathers[4].forward()
     for g in (2, 3, 4):
         gathers[g].finish()
+    loads[5].wait()
 
     def feed(j):
         r = span(j, rows)
@@ -787,21 +874,19 @@
 
         loop(ff // TILE, tile)
 
-    mi_line.step(1, 1)
     at(0, feed)
-    at(1, feed)
-    for s in range(2, n):
-        mi_line.step(s, 1)
-        if s == 2:
+    for s in range(1, n):
+        arrived(mi_line, s)
+        cot_line.arrive(s)
+        if s == n - 1:
+            at(s, feed)
             turn(ct_buf, t_one)
-        at(s, feed)
-    if n == 2:
-        turn(ct_buf, t_one)
+        else:
+            at(s, feed)
     after_attn.drain()
     mi_line.drain()
     cot_line.drain()
 
-    gain_own = block(gain_z, d, 8)
     gain_own[...] = jnp.zeros((8, width), F32)
 
     def back_two(h):
@@ -813,23 +898,37 @@
             gain_sum = jnp.sum(term * normed, axis=0, keepdims=True)
             dn = term * gain_row[1:2, :]
             mean = jnp.sum(dn * normed, axis=-1, keepdims=True) / width
-            value = cot[r, :].astype(F32) + scale * (dn - normed * mean)
+            here = pl.ds(pl.multiple_of(d * rows + h * half + i * CHUNK, CHUNK), CHUNK)
+            value = ct_buf[here, :].astype(F32) + scale * (dn - normed * mean)
             gmid[r, :] = value
-            here = pl.ds(pl.multiple_of(d * rows + h * half + i * CHUNK, CHUNK), CHUNK)
             gm_buf[here, :] = value.astype(BF)
             gain_own[1:2, :] = gain_own[1:2, :] + gain_sum
 
         loop(half // CHUNK, some)
 
     after_mlp = Reduce(1, by_turned([(gg, weights[2]), (gu, weights[3])]), s_buf, r_buf)
-    down = Grad(4, t_one, hid, emit_down)
+    down = Grad(4, t_one, hid, emit_plain(out_d))
     gate_g = Grad(2, t_two, gg, emit_plain(out_g))
     up_g = Grad(3, t_two, gu, emit_plain(out_u))
 
     def turn_mi():
         turn(mi_buf, t_two)
 
-    work = [turn_mi, down.send_all, down.own_all, gate_g.send_all, gate_g.own_all]
+    def attn_in_again(j):
+        def some(i):
+            r = pl.ds(pl.multiple_of(j * rows + i * CHUNK, CHUNK), CHUNK)
+            value = x_buf[r, :].astype(F32) * sc_one[r, :]
+            s_buf[r, :] = (value * gain_row[0:1, :]).astype(BF)
+
+        loop(rows // CHUNK, some)
+
+    work = [
+        both(turn_mi, down.send_all),
+        down.own_all,
+        gate_g.send_all,
+        both(gate_g.own_all, up_g.send_all),
+        up_g.own_all,
+    ]
     reduce_then_gather(after_mlp, back_two, gm_line, work)
     while work:
         run(work)
@@ -866,113 +965,115 @@
 
     output = Reduce(2, by_turned([(hid, weights[4])]), ct_buf, mi_buf)
 
-    gm_line.step(1, 1)
+    output.compute()
+    output.launch(False)
+    middle[...] = middle[...] + own_sum[...]
     at(0, back)
-    at(1, back)
-    for s in range(2, n):
-        gm_line.step(s, 1)
+    loop(n, attn_in_again)
+    turn(s_buf, t_two)
+    later = [(s, h) for s in range(n - 2, 0, -1) for h in range(2)]
+    for s in range(1, n):
+        arrived(gm_line, s)
         at(s, back)
-
-    def add_gain(j, t, value):
-        r = span(j, rows)
-        normed = x_buf[r, cols(t)].astype(F32) * sc_one[r, :]
-        gain_own[0:1, cols(t)] = gain_own[0:1, cols(t)] + jnp.sum(
-            value * normed, axis=0, keepdims=True
-        )
-
-    def write_out(h):
-        def some(i):
-            r = pl.ds(pl.multiple_of(h * half + i * CHUNK, CHUNK), CHUNK)
-            out_ref[r, :] = (middle[r, :] + own_sum[r, :]).astype(BF)
-
-        loop(half // CHUNK, some)
-
-    output.compute()
-    work = [up_g.send_all, up_g.own_all]
-    for s in range(n - 1, 0, -1):
-        if s < n - 1:
-            output.advance(s, 0)
-        output.advance(s, 1)
-        run(work)
+        if s < n - 1 and later:
+            output.advance(*later.pop(0))
+
+    def add_gain(t, value):
+        normed = x_buf[:, cols(t)].astype(F32) * sc_one[...]
+        gain_own[0:1, cols(t)] = jnp.sum(value * normed, axis=0, keepdims=True)
+
+    after_in = Reduce(3, by_turned([(gqkv, weights[0])]), s_buf, r_buf, add_gain)
+    out_g_grad = Grad(1, t_one, mixed, emit_out)
+    qkv_g = Grad(0, t_two, gqkv, emit_qkv)
+
+    after_in.compute()
+    quarter = width // 4
+    gain_mine = block(gain_z, d, 8)
+    for i in range(8):
+        gain_mine[i : i + 1, :] = gain_own[i // 4 : i // 4 + 1, pl.ds(i % 4 * quarter, quarter)]
+    for k in range(1, n):
+        gain_swap(k).start()
+    after_in.launch(False)
+    qkv_g.send_all()
+    for k in range(1, n):
+        gain_got(k)
+    block(gain_f, f, 8)[...] = total_of(gain_z[8 * k : 8 * k + 8, :] for k in range(n))
+    gain_back = Gather(6, gain_f, 8, plain=True)
+    gain_back.start()
+    qkv_g.own_all()
+
+    def output_end():
+        for h in range(2):
+            output.final_into(middle, h)
+        out_own[...] = middle[...].astype(BF)
+        store(out_own, out_ref)
+
+    def gain_end():
+        gain_back.forward()
+        gain_back.finish()
+        gain_all = total_of(gain_f[8 * k : 8 * k + 8, :] for k in range(nf))
+        for i in range(8):
+            gain_own[i // 4 : i // 4 + 1, pl.ds(i % 4 * quarter, quarter)] = gain_all[i : i + 1, :]
+        gain_all = pltpu.roll(gain_own[...], (width - f * shard) % width, 1)
+        out_ga[...] = gain_all[0:1, 0:shard]
+        out_gm[...] = gain_all[1:2, 0:shard]
+
+    def turn_gm():
+        turn(gm_buf, t_one)
+
+    def output_later():
+        while later:
+            output.advance(*later.pop(0))
+
+    work = [
+        both(turn_gm, out_g_grad.send_all),
+        both(output_later, out_g_grad.own_all),
+        gain_end,
+    ]
+    for s in range(n - 2, 0, -1):
+        for h in range(2):
+            after_in.advance(s, h)
+            run(work)
     while work:
         run(work)
-    for h in range(2):
-        output.final(h)
-        write_out(h)
-
-    after_in = Reduce(3, by_turned([(gqkv, weights[0])], add_gain), s_buf, r_buf)
-    out_g_grad = Grad(1, t_one, mixed, emit_out)
-    qkv_g = Grad(0, t_two, gqkv, emit_qkv)
-
-    def turn_attn_in():
-        def one(b):
-            there = span(b, rows)
-
-            def lane_block(t):
-                value = x_buf[there, cols(t, LANES)].astype(F32) * sc_one[there, :]
-                value = (value * gain_row[0:1, cols(t, LANES)]).astype(BF)
-                t_two[cols(t, LANES), cols(b, rows)] = value.T
-
-            loop(width // LANES, lane_block)
-
-        loop(n, one)
-
-    def turn_gm():
-        turn(gm_buf, t_one)
-
-    after_in.compute()
-    gain_line.start()
-    turn_attn_in()
-    qkv_g.send_all()
-    work = [qkv_g.own_all, turn_gm, out_g_grad.send_all, out_g_grad.own_all]
-    steps = list(range(1, n))
-    for s in range(n - 1, 0, -1):
-        if s < n - 1:
-            after_in.advance(s, 0)
-        after_in.advance(s, 1)
-        run(work)
-        if steps:
-            gain_line.step(steps.pop(0))
-    while work:
-        run(work)
-    block(gain_f, f, 8)[...] = total_of(gain_z[pl.ds(8 * k, 8), :] for k in range(n))
-    gain_back = Gather(6, gain_f, 8)
-    gain_back.start()
-    down.finish()
-    gate_g.finish()
-    gain_back.relay()
-    gain_back.forward()
-    up_g.finish()
+    output_end()
+    for grad in (down, gate_g, up_g):
+        grad.collect()
+        grad.finish()
 
     def back_one(h):
         def some(i):
             r = pl.ds(pl.multiple_of(h * half + i * CHUNK, CHUNK), CHUNK)
             there = pl.ds(pl.multiple_of(d * rows + h * half + i * CHUNK, CHUNK), CHUNK)
             scale = sc_one[there, :]
-            normed = tokens[r, :].astype(F32) * scale
+            normed = x_buf[there, :].astype(F32) * scale
             dm = own_sum[r, :] * gain_row[0:1, :]
             mean = jnp.sum(dm * normed, axis=-1, keepdims=True) / width
-            gtok_ref[r, :] = gmid[r, :] + scale * (dm - normed * mean)
+            gmid[r, :] = gmid[r, :] + scale * (dm - normed * mean)
 
         loop(half // CHUNK, some)
 
     for h in range(2):
         after_in.final(h)
         back_one(h)
-    qkv_g.finish()
-    out_g_grad.finish()
-    gain_back.finish()
-    gain_sum = total_of(gain_f[pl.ds(8 * k, 8), :] for k in range(nf))
-    gain_sum = pltpu.roll(gain_sum, (width - f * shard) % width, 1)
-    out_ga[...] = gain_sum[0:1, 0:shard]
-    out_gm[...] = gain_sum[1:2, 0:shard]
-
+        part = pl.ds(h * half, half)
+        store(gmid.at[part], gtok_ref.at[part])
+    for grad in (qkv_g, out_g_grad):
+        grad.collect()
+        grad.finish()
+
+    handing.pop().release()
     output.drain()
     after_in.drain()
-    for line in (tok_line, gm_line, gain_line):
-        line.drain()
+    tok_line.drain()
+    gm_line.drain()
+    for k in range(1, n):
+        gain_swap(k).wait_send()
     for gather in gathers + [gain_gather, gain_back]:
         gather.drain()
+    big_stores.pop().wait()
+    for copy in stores:
+        copy.wait()
 
 
 def pass_on(*refs):
@@ -1001,17 +1102,18 @@
     widths = (q_wide + 2 * kv_wide, q_wide, ff, ff, ff)
     dims = (n, chips, rows, width, nq, nkv, ff, lengths.shape[1])
     vmem = pl.BlockSpec(memory_space=pltpu.VMEM)
-    anywhere = pl.BlockSpec(memory_space=pl.ANY)
+    hbm = pl.BlockSpec(memory_space=pltpu.HBM)
     results = [
         jax.ShapeDtypeStruct((rows, width), BF),
         jax.ShapeDtypeStruct((rows, width), F32),
         jax.ShapeDtypeStruct((1, shard), F32),
         jax.ShapeDtypeStruct((1, shard), F32),
     ] + [jax.ShapeDtypeStruct(w.shape, F32) for w in (w_q, w_k, w_v, w_o, w_g, w_u, w_d)]
-    out_shape = results + [jax.ShapeDtypeStruct((chips - 1, shard, w), BF) for w in widths]
+    out_shape = results + [jax.ShapeDtypeStruct((chips - 1, shard, w), BF) for w in widths[2:]]
     widest = max(widths)
     scratch = (
-        [pltpu.VMEM((width, w), BF) for w in widths]
+        [pltpu.VMEM((chips - 1, shard, w), BF) for w in widths[:2]]
+        + [pltpu.VMEM((width, w), BF) for w in widths]
         + [
             pltpu.VMEM((total, width), BF),
             pltpu.VMEM((total, width), BF),
@@ -1032,19 +1134,24 @@
             pltpu.VMEM((rows, width), F32),
             pltpu.VMEM((rows, width), F32),
             pltpu.VMEM((rows, width), F32),
+            pltpu.VMEM((total, TILE), F32),
             pltpu.VMEM((total, 1), F32),
             pltpu.VMEM((rows, 1), F32),
             pltpu.VMEM((total, LANES), F32),
             pltpu.VMEM((total, LANES), F32),
+            pltpu.VMEM((nf * 8, -(-shard // LANES) * LANES), F32),
             pltpu.VMEM((8, width), F32),
-            pltpu.VMEM((nf * 8, width), F32),
             pltpu.VMEM((8, width), F32),
-            pltpu.VMEM((n * 8, width), F32),
-            pltpu.VMEM((nf * 8, width), F32),
+            pltpu.VMEM((n * 8, width // 4), F32),
+            pltpu.VMEM((nf * 8, width // 4), F32),
             pltpu.VMEM((chips - 1, shard, widest), BF),
             pltpu.VMEM((nq * HD, q_wide), BF),
             pltpu.VMEM((nq * HD, q_wide), BF),
-            pltpu.VMEM((TILE, TILE), BF),
+        ]
+        + [pltpu.VMEM(w.shape, BF) for w in (w_q, w_k, w_v, w_o)]
+        + [pltpu.VMEM((rows, width), BF)]
+        + [pltpu.VMEM(w.shape, F32) for w in (w_q, w_k, w_v, w_o, w_g)]
+        + [
             pltpu.VMEM((chips, shard, widest), BF),
         ]
         + [pltpu.VMEM((chips, shard, w), BF) for w in widths]
@@ -1059,33 +1166,35 @@
             pltpu.SemaphoreType.DMA((5, 2, n)),
             pltpu.SemaphoreType.DMA((4, 2, n)),
             pltpu.SemaphoreType.DMA((4, 2, n + 1)),
-            pltpu.SemaphoreType.DMA((5, chips)),
-            pltpu.SemaphoreType.DMA((5, chips)),
+            pltpu.SemaphoreType.DMA((5,)),
+            pltpu.SemaphoreType.DMA((5,)),
             pltpu.SemaphoreType.DMA((5, chips)),
             pltpu.SemaphoreType.DMA((5, chips)),
             pltpu.SemaphoreType.DMA((chips,)),
+            pltpu.SemaphoreType.DMA((6,)),
+            pltpu.SemaphoreType.DMA((7,)),
         ]
     )
     made = pl.pallas_call(
         partial(layer_kernel, dims),
         out_shape=out_shape,
-        in_specs=[pl.BlockSpec(memory_space=pltpu.SMEM)] + [vmem] * 10 + [anywhere] * 2,
-        out_specs=[vmem] * 11 + [anywhere] * 5,
+        in_specs=[pl.BlockSpec(memory_space=pltpu.SMEM)] + [vmem] * 3 + [hbm] * 9,
+        out_specs=[hbm] * 2 + [vmem] * 2 + [hbm] * 10,
         scratch_shapes=scratch,
         compiler_params=pltpu.CompilerParams(
             collective_id=0, has_side_effects=True, vmem_limit_bytes=67043328
         ),
         name="layer",
-    )(lengths, freq, tokens, cot, gain_a, gain_m, w_q, w_k, w_v, w_o, w_d, w_g, w_u)
+    )(lengths, freq, gain_a, gain_m, tokens, cot, w_q, w_k, w_v, w_o, w_d, w_g, w_u)
     count = len(results)
     return pl.pallas_call(
         pass_on,
         out_shape=results,
-        in_specs=[anywhere] * count,
-        out_specs=[anywhere] * count,
+        in_specs=[hbm] * count,
+        out_specs=[hbm] * count,
         scratch_shapes=[pltpu.VMEM(r.shape, r.dtype) for r in results]
         + [pltpu.SemaphoreType.DMA((count,)), pltpu.SemaphoreType.DMA((count,))],
-        compiler_params=pltpu.CompilerParams(vmem_limit_bytes=32 * 2**20),
+        compiler_params=pltpu.CompilerParams(vmem_limit_bytes=67043328),
         name="results",
     )(*made[:count])
 
@@ -1119,8 +1228,8 @@
         w_query[0],
         w_key[0],
         w_value[0],
-        w_out[0],
-        w_down[0],
+        w_out[0].T,
+        w_down[0].T,
         w_gate[0],
         w_up[0],
         n,
@@ -1134,11 +1243,11 @@
         g_q[None],
         g_k[None],
         g_v[None],
-        g_o[None],
+        g_o.T[None],
         g_mgain,
         g_gate[None],
         g_up[None],
-        g_down[None],
+        g_down.T[None],
     )
 
 

time: 303 us -> 214 us (0.71)
  Pallas kernels: 284 us -> 213 us
  local copies, waits for them, and re-layouts: 16.4 us -> 0.01 us
    pallas_call x1, Pallas kernels: 281 us -> 209 us  [run_layer(): pl.pallas_call(partial(layer_kernel, dims), out_shape=out_shape, in_specs...]
    unnamed x26 -> x0, local copies, waits for them, and re-layouts: 16.4 us -> none
where the time goes in v4:
time: 214 us
  Pallas kernels  213 us (100%)
    pallas_call x1, Pallas kernels, run_layer(): pl.pallas_call(partial(layer_kernel, dims), out_shape=out_shape, in_specs...  209 us

profile of v4, /device:TPU:8, one launch (start us, length us, event | category | flops | bytes accessed | tf_op | source)
XLA Modules:
  0.0 214.2 jit_solution(11255020280701936237)
XLA Ops:
  0.7 0.6 maximum_bitcast_fusion.refs_1_
  1.3 208.7 %layer.1 = (bf16[128,1536]{1,0:T(8,128)(2,1)}, f32[128,1536]{1,0:T(8,128)}, f32[1,192]{1,0:T(1,128)}, f32[1,192]{1,0:T(1,128)}, f32[192,384]{1,0:T(8,128)}, /*in...) custom-call(s32[4,4]{1,0:T(4,128)} %refs_0_.1, ...), custom_call_target="tpu_custom_call" | custom-call | tf_op jit(solution)/shard_map/layer/pallas_call | solution.py:1178
  209.9 4.1 %results.1 = (bf16[128,1536]{1,0:T(8,128)(2,1)}, f32[128,1536]{1,0:T(8,128)}, f32[1,192]{1,0:T(1,128)}, f32[1,192]{1,0:T(1,128)}, f32[192,384]{1,0:T(8,128)}, /*...) custom-call(bf16[128,1536]{1,0:T(8,128)(2,1)} %get-tuple-element.33., ...), custom_call_target="tpu_custom_call" | custom-call | tf_op jit(solution)/shard_map/results/pallas_call | solution.py:1190
  (2 shorter events, 0.0 us)

commit v5 on v4

--- a/solution.py
+++ b/solution.py
@@ -40,6 +40,14 @@
     lax.fori_loop(0, count, step, 0)
 
 
+def whole_lanes(count):
+    return -(-count // LANES) * LANES
+
+
+def packed_widths(nq, nkv, ff):
+    return (whole_lanes((nq + 2 * nkv) * HD), whole_lanes(nq * HD), ff, ff, ff)
+
+
 def flip(chip, bits):
     other, bit = chip, 1
     while bit <= bits:
@@ -57,7 +65,8 @@
     half = rows // 2
     q_wide, kv_wide = nq * LANES, nkv * LANES
     widths = (q_wide + 2 * kv_wide, q_wide, ff, ff, ff)
-    widest = max(widths)
+    gwidths = packed_widths(nq, nkv, ff)
+    widest = max(gwidths)
     near = [1] if chips > 1 else []
     far = [2 * k for k in range(1, chips // 2)]
     refs = list(refs)
@@ -74,8 +83,8 @@
     near_landing = take(2)
     landing = near_landing + far_landing
     weights = take(5)
-    (x_buf, ct_buf, mi_buf, gm_buf) = take(4)
-    (qkv, gqkv, probs, mixed, gmixed, hid, gg, gu) = take(8)
+    (x_buf, ct_buf, mi_buf, gm_buf, r_two, cot_own) = take(6)
+    (qkv, gqkv, probs, mixed, gmixed, hid, gg, gu, gqkv_pack, mixed_pack) = take(10)
     (t_one, t_two) = take(2)
     (s_buf, r_buf, own_sum, middle, gmid, wide_tile) = take(6)
     (sc_one, sc_two, cos_t, sin_t) = take(4)
@@ -103,6 +112,9 @@
         return {"fsdp": f, "dp": index}
 
     partner = p * 2 + 1 - c
+    low = 1 - d // (n // 2)
+    inner, outer = d - 1 + 2 * low, d + 1 - 2 * low
+    end = (d == 0) | (d == n - 1)
 
     def remote(src, dst, ss, rs, where):
         return pltpu.make_async_remote_copy(
@@ -128,6 +140,7 @@
                 (w_o, o_in),
                 (tokens, block(x_buf, d)),
                 (cot, block(ct_buf, d)),
+                (cot, cot_own),
             )
         )
     ]
@@ -359,16 +372,74 @@
         def left(self, index, h, last):
             return self.copy(index, d - 1, n if last else index, h)
 
-        def compute(self):
+        def compute(self, keep=True):
             def tile(t):
-                value = self.tile_of(t)
-                wide_tile[...] = value
-                own_sum[:, cols(t)] = wide_tile[span(d, rows), :]
+                value = self.tile_of(t, pl.ds(0, total))
+                if keep:
+                    wide_tile[...] = value
+                    own_sum[:, cols(t)] = wide_tile[span(d, rows), :]
                 self.sends[pl.ds(0, total), cols(t)] = value.astype(BF)
+
+            loop(width // TILE, tile)
+
+        def pair(self):
+            first = d - 1 + low
+
+            def tile(t):
+                value = self.tile_of(t, pl.ds(pl.multiple_of(first * rows, rows), 2 * rows))
+                wide_tile[0 : 2 * rows, :] = value
+                own_sum[:, cols(t)] = wide_tile[span(1 - low, rows), :]
+                self.sends[span(inner, rows), cols(t)] = wide_tile[span(low, rows), :].astype(BF)
                 if self.also is not None:
-                    self.also(t, value)
+                    self.also(t, value, pl.ds(pl.multiple_of(first * rows, rows), 2 * rows))
 
             loop(width // TILE, tile)
+
+        def single(self, j):
+            def tile(t):
+                value = self.tile_of(t, span(j, rows))
+                self.sends[span(j, rows), cols(t)] = value.astype(BF)
+                if self.also is not None:
+                    self.also(t, value, span(j, rows))
+
+            loop(width // TILE, tile)
+
+        def send_at(self, s):
+            @pl.when(d == 0)
+            def _():
+                for h in range(2):
+                    self.right(d + s, h).start()
+
+            @pl.when(d == n - 1)
+            def _():
+                for h in range(2):
+                    self.left(d - s, h, s == 1).start()
+
+        def add_right(self, index, h):
+            self.add_into(index, h)
+            self.right(index, h).start()
+
+        def add_left(self, index, h, last):
+            self.add_into(index, h)
+            self.left(index, h, last).start()
+
+        def out_adv(self, s, h):
+            @pl.when((d > 0) & (d < n // 2) & (d + s < n))
+            def _():
+                self.add_right(d + s, h)
+
+            @pl.when((d < n - 1) & (d >= n // 2) & (d - s >= 0))
+            def _():
+                self.add_left(d - s, h, s == 1)
+
+        def in_adv(self, s, h):
+            @pl.when((d < n // 2) & (d - s >= 0))
+            def _():
+                self.add_left(d - s, h, s == 1)
+
+            @pl.when((d >= n // 2) & (d + s < n))
+            def _():
+                self.add_right(d + s, h)
 
         def launch(self, halves_first):
             order = [(s, h) for h in range(2) for s in range(n - 1, 0, -1)]
@@ -441,12 +512,19 @@
                     def _():
                         self.copy(j, d, j, h).wait_send()
 
+    def tiles(wide, body):
+        if wide % TILE == 0:
+            loop(wide // TILE, lambda t: body(cols(t)))
+        else:
+            for start in range(0, wide, TILE):
+                body(pl.ds(start, min(TILE, wide - start)))
+
     handing = []
 
     class Grad:
         def __init__(self, group, turned, terms, emit):
             self.group, self.turned, self.terms, self.emit = group, turned, terms, emit
-            self.width = widths[group]
+            self.width = gwidths[group]
 
         def hand_over(self):
             src = send_b if self.width == widest else send_b.at[:, :, pl.ds(0, self.width)]
@@ -468,11 +546,11 @@
                 at_f(chip * 2 + c),
             )
 
-        def blocks_of(self, core, t):
+        def blocks_of(self, core, lanes):
             left = jnp.concatenate(
                 [self.turned[span(q * 2 + core, shard), :] for q in range(chips)], axis=0
             )
-            value = mm(left, self.terms[:, cols(t)])
+            value = mm(left, self.terms[:, lanes])
             return [value[q * shard : (q + 1) * shard] for q in range(chips)]
 
         def release(self):
@@ -482,25 +560,31 @@
             if handing:
                 handing.pop().release()
 
-            def tile(t):
-                for q, value in enumerate(self.blocks_of(1 - c, t)):
-                    send_b[q, :, cols(t)] = value.astype(BF)
-
-            loop(self.width // TILE, tile)
+            def tile(lanes):
+                for q, value in enumerate(self.blocks_of(1 - c, lanes)):
+                    send_b[q, :, lanes] = value.astype(BF)
+
+            tiles(self.width, tile)
             self.hand_over().start()
             handing.append(self)
 
-        def own_all(self):
+        def own_sums(self):
             self.hand_over().wait_recv()
 
-            def tile(t):
-                for q, value in enumerate(self.blocks_of(c, t)):
-                    other = from_partner[self.group][q, :, cols(t)].astype(F32)
-                    sums[self.group][q, :, cols(t)] = (value + other).astype(BF)
-
-            loop(self.width // TILE, tile)
+            def tile(lanes):
+                for q, value in enumerate(self.blocks_of(c, lanes)):
+                    other = from_partner[self.group][q, :, lanes].astype(F32)
+                    sums[self.group][q, :, lanes] = (value + other).astype(BF)
+
+            tiles(self.width, tile)
+
+        def ship_all(self):
             for k in range(1, chips):
                 self.ship(k).start()
+
+        def own_all(self):
+            self.own_sums()
+            self.ship_all()
 
         def fetch(self, k):
             return pltpu.make_async_copy(
@@ -559,24 +643,52 @@
 
     big_stores = []
 
+    def summed(parts, start, size):
+        return total_of(v.astype(F32) for v in parts(pl.ds(start, size)))
+
+    q_real, kv_real = nq * HD, nkv * HD
+
     def emit_out(parts):
-        lanes = pl.ds(0, q_wide)
-        o_own[...] = total_of(mm_nt(v, pick_end[...]) for v in parts(lanes))
+        o_own[...] = summed(parts, 0, q_real)
         store(o_own, out_o)
 
     def emit_qkv(parts):
-        kv_rows = nkv * HD
-        lanes = pl.ds(0, q_wide)
-        q_own[...] = total_of(mm_nt(v, pick_rope[...]) for v in parts(lanes))
+        q_own[...] = summed(parts, 0, q_real)
         store(q_own, out_q)
-        lanes = pl.ds(q_wide, kv_wide)
-        pick = pick_rope[0:kv_rows, 0:kv_wide]
-        k_own[...] = total_of(mm_nt(v, pick) for v in parts(lanes))
+        k_own[...] = summed(parts, q_real, kv_real)
         store(k_own, out_k)
-        lanes = pl.ds(q_wide + kv_wide, kv_wide)
-        pick = pick_end[0:kv_rows, 0:kv_wide]
-        v_own[...] = total_of(mm_nt(v, pick) for v in parts(lanes))
+        v_own[...] = summed(parts, q_real + kv_real, kv_real)
         store(v_own, out_v)
+
+    def fill(dst, r, value):
+        spare = dst.shape[1] - value.shape[1]
+        if spare:
+            value = jnp.concatenate([value, jnp.zeros((value.shape[0], spare), F32)], axis=1)
+        dst[r, :] = value.astype(BF)
+
+    def pack_mixed():
+        def one(b):
+            r = span(b, rows)
+            fill(mixed_pack, r, mm_nt(mixed[r, :], pick_end[...]))
+
+        loop(n, one)
+
+    def pack_gqkv():
+        def one(b):
+            r = span(b, rows)
+            keys = slice(q_wide, q_wide + kv_wide)
+            vals = slice(q_wide + kv_wide, q_wide + 2 * kv_wide)
+            value = jnp.concatenate(
+                [
+                    mm_nt(gqkv[r, 0:q_wide], pick_rope[...]),
+                    mm_nt(gqkv[r, keys], pick_rope[0:kv_real, 0:kv_wide]),
+                    mm_nt(gqkv[r, vals], pick_end[0:kv_real, 0:kv_wide]),
+                ],
+                axis=1,
+            )
+            fill(gqkv_pack, r, value)
+
+        loop(n, one)
 
     def turn(src, dst):
         def lane_block(t):
@@ -616,18 +728,6 @@
 
     pick_rope[...] = one_hot(True)
     pick_end[...] = one_hot(False)
-    mine = span(f, shard)
-    kv_rows = nkv * HD
-    for copy in loads[:4]:
-        copy.wait()
-    weights[0][mine, 0:q_wide] = mm(q_in[...], pick_rope[...]).astype(BF)
-    weights[0][mine, q_wide : q_wide + kv_wide] = mm(
-        k_in[...], pick_rope[0:kv_rows, 0:kv_wide]
-    ).astype(BF)
-    weights[0][mine, q_wide + kv_wide : q_wide + 2 * kv_wide] = mm(
-        v_in[...], pick_end[0:kv_rows, 0:kv_wide]
-    ).astype(BF)
-    weights[1][mine, :] = mm(o_in[...], pick_end[...]).astype(BF)
     gain_mine = block(gain_in, f, 8)
     gain_mine[...] = jnp.zeros(gain_mine.shape, F32)
     gain_mine[0:1, 0:shard] = gain_a[...].astype(F32)
@@ -677,20 +777,31 @@
         block(cos_t, b)[...] = jnp.cos(angle)
         block(sin_t, b)[...] = jnp.where(lane < LANES // 2, -sine, sine)
 
-    loop(n, tables)
     pl.semaphore_wait(barrier, chips + n - 1)
     for h in range(2):
         tok_line.start(h)
-    gain_gather.start()
-    gathers[0].start()
-    gathers[1].start()
-
-    @pl.when((d == 0) | (d == n - 1))
+
+    @pl.when(end)
     def _():
         cot_line.start()
 
-    for g in range(2, 5):
+    gain_gather.start()
+    mine = span(f, shard)
+    kv_rows = nkv * HD
+    for copy in loads[:4]:
+        copy.wait()
+    weights[0][mine, 0:q_wide] = mm(q_in[...], pick_rope[...]).astype(BF)
+    weights[0][mine, q_wide : q_wide + kv_wide] = mm(
+        k_in[...], pick_rope[0:kv_rows, 0:kv_wide]
+    ).astype(BF)
+    weights[0][mine, q_wide + kv_wide : q_wide + 2 * kv_wide] = mm(
+        v_in[...], pick_end[0:kv_rows, 0:kv_wide]
+    ).astype(BF)
+    gathers[0].start()
+    weights[1][mine, :] = mm(o_in[...], pick_end[...]).astype(BF)
+    for g in range(1, 5):
         gathers[g].start()
+    loop(n, tables)
     loads[4].wait()
     gain_gather.forward()
     gain_gather.finish()
@@ -778,8 +889,8 @@
     gathers[1].finish()
 
     def by_turned(pairs):
-        def tile_of(t):
-            return total_of(mm_nt(left[...], weight[cols(t), :]) for left, weight in pairs)
+        def tile_of(t, r):
+            return total_of(mm_nt(left[r, :], weight[cols(t), :]) for left, weight in pairs)
 
         return tile_of
 
@@ -853,11 +964,13 @@
     reduce_then_gather(after_attn, norm_two, mi_line, work)
     while work:
         run(work)
+    pack_mixed()
     gathers[3].forward()
     gathers[4].forward()
     for g in (2, 3, 4):
         gathers[g].finish()
     loads[5].wait()
+    loads[6].wait()
 
     def feed(j):
         r = span(j, rows)
@@ -874,18 +987,29 @@
 
         loop(ff // TILE, tile)
 
+    def at_outer(work):
+        @pl.when((outer >= 0) & (outer < n))
+        def _():
+            work(outer)
+
+    after_mlp = Reduce(1, by_turned([(gg, weights[2]), (gu, weights[3])]), s_buf, r_buf)
+    after_attn.drain()
     at(0, feed)
+    mi_line.step(1, 1)
     for s in range(1, n):
-        arrived(mi_line, s)
+        for h in range(2):
+            mi_line.arrive(s, h)
         cot_line.arrive(s)
-        if s == n - 1:
-            at(s, feed)
-            turn(ct_buf, t_one)
+        at(s, feed)
+        if s + 1 < n:
+            mi_line.step(s + 1, 1)
+        if s == 1:
+            after_mlp.pair()
+            after_mlp.send_at(1)
+            at_outer(after_mlp.single)
         else:
-            at(s, feed)
-    after_attn.drain()
-    mi_line.drain()
-    cot_line.drain()
+            at(s, after_mlp.single)
+            after_mlp.send_at(s)
 
     gain_own[...] = jnp.zeros((8, width), F32)
 
@@ -899,14 +1023,13 @@
             dn = term * gain_row[1:2, :]
             mean = jnp.sum(dn * normed, axis=-1, keepdims=True) / width
             here = pl.ds(pl.multiple_of(d * rows + h * half + i * CHUNK, CHUNK), CHUNK)
-            value = ct_buf[here, :].astype(F32) + scale * (dn - normed * mean)
+            value = cot_own[r, :].astype(F32) + scale * (dn - normed * mean)
             gmid[r, :] = value
             gm_buf[here, :] = value.astype(BF)
             gain_own[1:2, :] = gain_own[1:2, :] + gain_sum
 
         loop(half // CHUNK, some)
 
-    after_mlp = Reduce(1, by_turned([(gg, weights[2]), (gu, weights[3])]), s_buf, r_buf)
     down = Grad(4, t_one, hid, emit_plain(out_d))
     gate_g = Grad(2, t_two, gg, emit_plain(out_g))
     up_g = Grad(3, t_two, gu, emit_plain(out_u))
@@ -922,17 +1045,59 @@
 
         loop(rows // CHUNK, some)
 
-    work = [
-        both(turn_mi, down.send_all),
-        down.own_all,
-        gate_g.send_all,
-        both(gate_g.own_all, up_g.send_all),
-        up_g.own_all,
-    ]
-    reduce_then_gather(after_mlp, back_two, gm_line, work)
-    while work:
-        run(work)
+    output = Reduce(2, by_turned([(hid, weights[4])]), ct_buf, r_two)
+
+    def finish_mlp():
+        for h in range(2):
+            after_mlp.final(h)
+            back_two(h)
+            if h == 0:
+                gm_line.start(h)
+
+    turn(ct_buf, t_one)
+    cot_line.drain()
+    turn_mi()
+    down.send_all()
+    for h in range(2):
+        after_mlp.out_adv(1, h)
+    output.compute(keep=False)
+    for s in range(n - 1, 1, -1):
+        output.send_at(s)
+    if n == 2:
+        output.send_at(1)
+    down.own_all()
+    for s in range(2, n - 1):
+        for h in range(2):
+            after_mlp.out_adv(s, h)
+
+    @pl.when(jnp.logical_not(end))
+    def _():
+        finish_mlp()
+
+    gate_g.send_all()
+    for s in range(1, n - 1):
+        for h in range(2):
+            after_mlp.in_adv(s, h)
+
+    @pl.when(jnp.logical_not(end))
+    def _():
+        gm_line.start(1)
+
+    for h in range(2):
+        gm_line.inward(1, h)
+    gate_g.own_all()
+    up_g.send_all()
+    gm_line.outward(1, 0)
+    up_g.own_all()
+    gm_line.outward(1, 1)
+
+    @pl.when(end)
+    def _():
+        finish_mlp()
+        gm_line.start(1)
+
     after_mlp.drain()
+    mi_line.drain()
 
     def back(b):
         r = span(b, rows)
@@ -963,46 +1128,81 @@
             gqkv[r, k_at : k_at + LANES] = rope(grad_k, -1.0, cos_v, sin_v).astype(BF)
             gqkv[r, v_at : v_at + LANES] = grad_v.astype(BF)
 
-    output = Reduce(2, by_turned([(hid, weights[4])]), ct_buf, mi_buf)
-
-    output.compute()
-    output.launch(False)
-    middle[...] = middle[...] + own_sum[...]
+    def add_gain(t, value, r):
+        normed = x_buf[r, cols(t)].astype(F32) * sc_one[r, :]
+        gain_own[0:1, cols(t)] = gain_own[0:1, cols(t)] + jnp.sum(
+            value * normed, axis=0, keepdims=True
+        )
+
+    after_in = Reduce(3, by_turned([(gqkv, weights[0])]), s_buf, r_buf, add_gain)
+    out_g_grad = Grad(1, t_one, mixed_pack, emit_out)
+    qkv_g = Grad(0, t_two, gqkv_pack, emit_qkv)
+
+    def pass_gm(h):
+        for s in range(2, n - 1):
+            gm_line.inward(s, h)
+            gm_line.outward(s, h)
+
     at(0, back)
+    pass_gm(0)
+    for h in range(2):
+        gm_line.arrive(1, h)
+    back(inner)
+    pass_gm(1)
+    for s in range(n - 2, 1, -1):
+        for h in range(2):
+            output.out_adv(s, h)
     loop(n, attn_in_again)
     turn(s_buf, t_two)
-    later = [(s, h) for s in range(n - 2, 0, -1) for h in range(2)]
-    for s in range(1, n):
-        arrived(gm_line, s)
-        at(s, back)
-        if s < n - 1 and later:
-            output.advance(*later.pop(0))
-
-    def add_gain(t, value):
-        normed = x_buf[:, cols(t)].astype(F32) * sc_one[...]
-        gain_own[0:1, cols(t)] = jnp.sum(value * normed, axis=0, keepdims=True)
-
-    after_in = Reduce(3, by_turned([(gqkv, weights[0])]), s_buf, r_buf, add_gain)
-    out_g_grad = Grad(1, t_one, mixed, emit_out)
-    qkv_g = Grad(0, t_two, gqkv, emit_qkv)
-
-    after_in.compute()
+    after_in.pair()
+    after_in.send_at(1)
+    if n > 2:
+        for h in range(2):
+            output.out_adv(1, h)
+
+    def outer_back(j):
+        back(j)
+        after_in.single(j)
+
+    at_outer(outer_back)
+    for s in range(2, n):
+        for h in range(2):
+            gm_line.arrive(s, h)
+        at(s, outer_back)
+        if s < n - 1:
+            after_in.send_at(s)
     quarter = width // 4
     gain_mine = block(gain_z, d, 8)
     for i in range(8):
         gain_mine[i : i + 1, :] = gain_own[i // 4 : i // 4 + 1, pl.ds(i % 4 * quarter, quarter)]
     for k in range(1, n):
         gain_swap(k).start()
-    after_in.launch(False)
+    if n > 2:
+        after_in.send_at(n - 1)
+        output.send_at(1)
+    for s in range(1, n - 1):
+        for h in range(2):
+            output.in_adv(s, h)
+    turn(gm_buf, t_one)
+    out_g_grad.send_all()
+    pack_gqkv()
+    out_g_grad.own_all()
     qkv_g.send_all()
+    for h in range(2):
+        after_in.out_adv(n - 2, h)
+    qkv_g.own_sums()
     for k in range(1, n):
         gain_got(k)
     block(gain_f, f, 8)[...] = total_of(gain_z[8 * k : 8 * k + 8, :] for k in range(n))
     gain_back = Gather(6, gain_f, 8, plain=True)
     gain_back.start()
-    qkv_g.own_all()
+    qkv_g.ship_all()
+    for s in range(n - 3, 0, -1):
+        for h in range(2):
+            after_in.out_adv(s, h)
 
     def output_end():
+        middle[...] = middle[...] + block(ct_buf, d)[...].astype(F32)
         for h in range(2):
             output.final_into(middle, h)
         out_own[...] = middle[...].astype(BF)
@@ -1018,28 +1218,14 @@
         out_ga[...] = gain_all[0:1, 0:shard]
         out_gm[...] = gain_all[1:2, 0:shard]
 
-    def turn_gm():
-        turn(gm_buf, t_one)
-
-    def output_later():
-        while later:
-            output.advance(*later.pop(0))
-
-    work = [
-        both(turn_gm, out_g_grad.send_all),
-        both(output_later, out_g_grad.own_all),
-        gain_end,
-    ]
-    for s in range(n - 2, 0, -1):
+    work = [gain_end]
+    for grad in (down, gate_g, up_g):
+        work.append(both(grad.collect, grad.finish))
+    for s in range(1, n - 1):
         for h in range(2):
-            after_in.advance(s, h)
-            run(work)
+            after_in.in_adv(s, h)
     while work:
         run(work)
-    output_end()
-    for grad in (down, gate_g, up_g):
-        grad.collect()
-        grad.finish()
 
     def back_one(h):
         def some(i):
@@ -1058,6 +1244,7 @@
         back_one(h)
         part = pl.ds(h * half, half)
         store(gmid.at[part], gtok_ref.at[part])
+    output_end()
     for grad in (qkv_g, out_g_grad):
         grad.collect()
         grad.finish()
@@ -1110,15 +1297,18 @@
         jax.ShapeDtypeStruct((1, shard), F32),
     ] + [jax.ShapeDtypeStruct(w.shape, F32) for w in (w_q, w_k, w_v, w_o, w_g, w_u, w_d)]
     out_shape = results + [jax.ShapeDtypeStruct((chips - 1, shard, w), BF) for w in widths[2:]]
-    widest = max(widths)
+    gwidths = packed_widths(nq, nkv, ff)
+    widest = max(gwidths)
     scratch = (
-        [pltpu.VMEM((chips - 1, shard, w), BF) for w in widths[:2]]
+        [pltpu.VMEM((chips - 1, shard, w), BF) for w in gwidths[:2]]
         + [pltpu.VMEM((width, w), BF) for w in widths]
         + [
             pltpu.VMEM((total, width), BF),
             pltpu.VMEM((total, width), BF),
+            pltpu.VMEM((total, width), BF),
+            pltpu.VMEM((total, width), BF),
             pltpu.VMEM((total + rows, width), BF),
-            pltpu.VMEM((total, width), BF),
+            pltpu.VMEM((rows, width), BF),
             pltpu.VMEM((total, widths[0]), BF),
             pltpu.VMEM((total, widths[0]), BF),
             pltpu.VMEM((n * nq, rows, rows), F32),
@@ -1127,6 +1317,8 @@
             pltpu.VMEM((total, ff), BF),
             pltpu.VMEM((total, ff), BF),
             pltpu.VMEM((total, ff), BF),
+            pltpu.VMEM((total, gwidths[0]), BF),
+            pltpu.VMEM((total, gwidths[1]), BF),
             pltpu.VMEM((width, total), BF),
             pltpu.VMEM((width, total), BF),
             pltpu.VMEM((total, width), BF),
@@ -1154,8 +1346,8 @@
         + [
             pltpu.VMEM((chips, shard, widest), BF),
         ]
-        + [pltpu.VMEM((chips, shard, w), BF) for w in widths]
-        + [pltpu.VMEM((chips, shard, w), BF) for w in widths]
+        + [pltpu.VMEM((chips, shard, w), BF) for w in gwidths]
+        + [pltpu.VMEM((chips, shard, w), BF) for w in gwidths]
         + [
             pltpu.SemaphoreType.DMA((7, chips)),
             pltpu.SemaphoreType.DMA((7, chips)),
@@ -1171,7 +1363,7 @@
             pltpu.SemaphoreType.DMA((5, chips)),
             pltpu.SemaphoreType.DMA((5, chips)),
             pltpu.SemaphoreType.DMA((chips,)),
-            pltpu.SemaphoreType.DMA((6,)),
+            pltpu.SemaphoreType.DMA((7,)),
             pltpu.SemaphoreType.DMA((7,)),
         ]
     )

time: 214 us -> 198 us (0.925)
  Pallas kernels: 213 us -> 196 us
    pallas_call x1, Pallas kernels: 209 us -> 192 us  [run_layer(): pl.pallas_call(partial(layer_kernel, dims), out_shape=out_shape, in_specs...]
where the time goes in v5:
time: 198 us
  Pallas kernels  196 us (99%)
    pallas_call x1, Pallas kernels, run_layer(): pl.pallas_call(partial(layer_kernel, dims), out_shape=out_shape, in_specs...  192 us
    pallas_call x1, Pallas kernels, run_layer(): pl.pallas_call(pass_on, out_shape=results, in_specs=[hbm] * count, out_sp...  4.09 us

profile of v5, /device:TPU:8, one launch (start us, length us, event | category | flops | bytes accessed | tf_op | source)
XLA Modules:
  0.0 197.7 jit_solution(10621871005585083308)
XLA Ops:
  0.7 0.6 maximum_bitcast_fusion.refs_1_
  1.3 192.2 %layer.1 = (bf16[128,1536]{1,0:T(8,128)(2,1)}, f32[128,1536]{1,0:T(8,128)}, f32[1,192]{1,0:T(1,128)}, f32[1,192]{1,0:T(1,128)}, f32[192,384]{1,0:T(8,128)}, /*in...) custom-call(s32[4,4]{1,0:T(4,128)} %refs_0_.1, ...), custom_call_target="tpu_custom_call" | custom-call | tf_op jit(solution)/shard_map/layer/pallas_call | solution.py:1370
  193.5 4.1 %results.1 = (bf16[128,1536]{1,0:T(8,128)(2,1)}, f32[128,1536]{1,0:T(8,128)}, f32[1,192]{1,0:T(1,128)}, f32[1,192]{1,0:T(1,128)}, f32[192,384]{1,0:T(8,128)}, /*...) custom-call(bf16[128,1536]{1,0:T(8,128)(2,1)} %get-tuple-element.33., ...), custom_call_target="tpu_custom_call" | custom-call | tf_op jit(solution)/shard_map/results/pallas_call | solution.py:1382
  (2 shorter events, 0.0 us)

commit v6 on v5

--- a/solution.py
+++ b/solution.py
@@ -1061,10 +1061,7 @@
     for h in range(2):
         after_mlp.out_adv(1, h)
     output.compute(keep=False)
-    for s in range(n - 1, 1, -1):
-        output.send_at(s)
-    if n == 2:
-        output.send_at(1)
+    output.send_at(n - 1)
     down.own_all()
     for s in range(2, n - 1):
         for h in range(2):
@@ -1075,26 +1072,31 @@
         finish_mlp()
 
     gate_g.send_all()
+    work = [gate_g.own_all, up_g.send_all]
     for s in range(1, n - 1):
         for h in range(2):
             after_mlp.in_adv(s, h)
+            run(work)
+    while work:
+        run(work)
 
     @pl.when(jnp.logical_not(end))
     def _():
         gm_line.start(1)
 
-    for h in range(2):
-        gm_line.inward(1, h)
-    gate_g.own_all()
-    up_g.send_all()
+    gm_line.inward(1, 0)
+    up_g.own_all()
+    gm_line.inward(1, 1)
     gm_line.outward(1, 0)
-    up_g.own_all()
     gm_line.outward(1, 1)
 
     @pl.when(end)
     def _():
         finish_mlp()
         gm_line.start(1)
+
+    for s in range(n - 2, 1, -1):
+        output.send_at(s)
 
     after_mlp.drain()
     mi_line.drain()
@@ -1169,16 +1171,15 @@
         for h in range(2):
             gm_line.arrive(s, h)
         at(s, outer_back)
-        if s < n - 1:
-            after_in.send_at(s)
     quarter = width // 4
     gain_mine = block(gain_z, d, 8)
     for i in range(8):
         gain_mine[i : i + 1, :] = gain_own[i // 4 : i // 4 + 1, pl.ds(i % 4 * quarter, quarter)]
     for k in range(1, n):
         gain_swap(k).start()
+    for s in range(n - 1, 1, -1):
+        after_in.send_at(s)
     if n > 2:
-        after_in.send_at(n - 1)
         output.send_at(1)
     for s in range(1, n - 1):
         for h in range(2):
@@ -1197,9 +1198,12 @@
     gain_back = Gather(6, gain_f, 8, plain=True)
     gain_back.start()
     qkv_g.ship_all()
-    for s in range(n - 3, 0, -1):
+    for s in range(n - 2, 0, -1):
         for h in range(2):
-            after_in.out_adv(s, h)
+            after_in.in_adv(s, h)
+        if s < n - 2:
+            for h in range(2):
+                after_in.out_adv(s, h)
 
     def output_end():
         middle[...] = middle[...] + block(ct_buf, d)[...].astype(F32)
@@ -1221,9 +1225,6 @@
     work = [gain_end]
     for grad in (down, gate_g, up_g):
         work.append(both(grad.collect, grad.finish))
-    for s in range(1, n - 1):
-        for h in range(2):
-            after_in.in_adv(s, h)
     while work:
         run(work)
 

time: 198 us -> 194 us (0.980)
  Pallas kernels: 196 us -> 191 us
    pallas_call x1, Pallas kernels: 192 us -> 187 us  [run_layer(): pl.pallas_call(partial(layer_kernel, dims), out_shape=out_shape, in_specs...]
where the time goes in v6:
time: 194 us; the launch traced here: 193 us
  Pallas kernels  191 us (98%)
    pallas_call x1, Pallas kernels, run_layer(): pl.pallas_call(partial(layer_kernel, dims), out_shape=out_shape, in_specs...  187 us
    pallas_call x1, Pallas kernels, run_layer(): pl.pallas_call(pass_on, out_shape=results, in_specs=[hbm] * count, out_sp...  4.09 us

profile of v6, /device:TPU:8, one launch (start us, length us, event | category | flops | bytes accessed | tf_op | source)
XLA Modules:
  0.0 192.7 jit_solution(2945409885864771479)
XLA Ops:
  0.7 0.6 maximum_bitcast_fusion.refs_1_
  1.3 187.2 %layer.1 = (bf16[128,1536]{1,0:T(8,128)(2,1)}, f32[128,1536]{1,0:T(8,128)}, f32[1,192]{1,0:T(1,128)}, f32[1,192]{1,0:T(1,128)}, f32[192,384]{1,0:T(8,128)}, /*in...) custom-call(s32[4,4]{1,0:T(4,128)} %refs_0_.1, ...), custom_call_target="tpu_custom_call" | custom-call | tf_op jit(solution)/shard_map/layer/pallas_call | solution.py:1371
  188.5 4.1 %results.1 = (bf16[128,1536]{1,0:T(8,128)(2,1)}, f32[128,1536]{1,0:T(8,128)}, f32[1,192]{1,0:T(1,128)}, f32[1,192]{1,0:T(1,128)}, f32[192,384]{1,0:T(8,128)}, /*...) custom-call(bf16[128,1536]{1,0:T(8,128)(2,1)} %get-tuple-element.33., ...), custom_call_target="tpu_custom_call" | custom-call | tf_op jit(solution)/shard_map/results/pallas_call | solution.py:1383
  (2 shorter events, 0.0 us)

commit v7 on v6

--- a/solution.py
+++ b/solution.py
@@ -2,6 +2,7 @@
 
 import jax
 import jax.numpy as jnp
+import numpy as np
 from jax import lax
 from jax.experimental import pallas as pl
 from jax.experimental.pallas import tpu as pltpu
@@ -69,6 +70,7 @@
     widest = max(gwidths)
     near = [1] if chips > 1 else []
     far = [2 * k for k in range(1, chips // 2)]
+    both_axes = [k + other for k in near for other in far]
     refs = list(refs)
 
     def take(count):
@@ -76,7 +78,7 @@
         del refs[:count]
         return taken
 
-    (lengths, freq, gain_a, gain_m) = take(4)
+    (lengths_in, freq_in, gain_a_in, gain_m_in) = take(4)
     (tokens, cot, w_q, w_k, w_v, w_o, w_d, w_g, w_u) = take(9)
     (out_ref, gtok_ref, out_ga, out_gm, out_q, out_k, out_v, out_o, out_g, out_u, out_d) = take(11)
     far_landing = take(3)
@@ -91,6 +93,7 @@
     (gain_in, gain_row, gain_own, gain_z, gain_f, stage) = take(6)
     (pick_rope, pick_end) = take(2)
     (q_in, k_in, v_in, o_in) = take(4)
+    (lengths, freq, gain_a, gain_m) = take(4)
     (out_own, q_own, k_own, v_own, o_own, big_own) = take(6)
     send_b = take(1)[0]
     sums = take(5)
@@ -98,7 +101,8 @@
     (w_ss, w_fs, w_qs, w_rs, w_ls) = take(5)
     (z_ss, z_rs) = take(2)
     (rs_ss, rs_rs) = take(2)
-    (b_ss, b_rs, i_ss, i_rs, l_sem, in_sem, out_sem) = take(7)
+    (b_ss, b_rs, i_ss, i_rs, l_sem, in_sem, out_sem, v_ss, v_rs) = take(9)
+    between = take(3)
 
     f = lax.axis_index("fsdp")
     d = lax.axis_index("dp")
@@ -128,6 +132,8 @@
         return ref.at[span(index, size)]
 
     def cols(index, size=TILE):
+        if isinstance(index, int):
+            return pl.ds(index * size, size)
         return span(index, size)
 
     loads = [
@@ -141,6 +147,10 @@
                 (tokens, block(x_buf, d)),
                 (cot, block(ct_buf, d)),
                 (cot, cot_own),
+                (lengths_in, lengths),
+                (freq_in, freq),
+                (gain_a_in, gain_a),
+                (gain_m_in, gain_m),
             )
         )
     ]
@@ -347,9 +357,16 @@
                         self.copy(j, 1, h).wait_send()
 
     class Reduce:
-        def __init__(self, slot, tile_of, sends, gets, also=None):
+        def __init__(self, slot, tile_of, sends, gets, also=None, plain=False):
             self.slot, self.tile_of, self.sends, self.gets = slot, tile_of, sends, gets
-            self.also = also
+            self.also, self.plain = also, plain
+
+        def over_tiles(self, tile):
+            if self.plain:
+                for t in range(width // TILE):
+                    tile(t)
+            else:
+                loop(width // TILE, tile)
 
         def copy(self, index, where, slot, h):
             return remote(
@@ -393,7 +410,7 @@
                 if self.also is not None:
                     self.also(t, value, pl.ds(pl.multiple_of(first * rows, rows), 2 * rows))
 
-            loop(width // TILE, tile)
+            self.over_tiles(tile)
 
         def single(self, j):
             def tile(t):
@@ -402,7 +419,7 @@
                 if self.also is not None:
                     self.also(t, value, span(j, rows))
 
-            loop(width // TILE, tile)
+            self.over_tiles(tile)
 
         def send_at(self, s):
             @pl.when(d == 0)
@@ -579,8 +596,50 @@
             tiles(self.width, tile)
 
         def ship_all(self):
-            for k in range(1, chips):
-                self.ship(k).start()
+            if self.group < 2:
+                for k in range(1, chips):
+                    self.ship(k).start()
+                return
+
+            for core, first, second in ((0, near, far), (1, far, near)):
+
+                @pl.when(c == core)
+                def _():
+                    for k in second:
+                        for other in first:
+                            self.via(other, k).start()
+                        self.ship(k).start()
+
+        def via(self, first, second):
+            return remote(
+                sums[self.group].at[flip(p, first + second)],
+                between[self.group - 2].at[both_axes.index(first + second)],
+                v_ss.at[self.group, first + second],
+                v_rs.at[self.group, first + second],
+                at_f(flip(p, second) * 2 + c),
+            )
+
+        def relay(self):
+            for core, first, second in ((0, near, far), (1, far, near)):
+
+                @pl.when(c == core)
+                def _():
+                    for k in first:
+                        chip = flip(p, k)
+                        for other in second:
+                            self.via(k, other).wait_recv()
+                            held = between[self.group - 2].at[both_axes.index(k + other)]
+
+                            def tile(lanes):
+                                total_here = sums[self.group][chip, :, lanes].astype(F32)
+                                total_here = total_here + held[:, lanes].astype(F32)
+                                sums[self.group][chip, :, lanes] = total_here.astype(BF)
+
+                            tiles(self.width, tile)
+                        self.ship(k).start()
+
+        def partners(self):
+            return near + far if self.group >= 2 else list(range(1, chips))
 
         def own_all(self):
             self.own_sums()
@@ -594,19 +653,23 @@
             )
 
         def collect(self):
-            for k in range(1, chips):
+            for k in self.partners():
                 self.ship(k).wait()
                 if self.group >= 2:
                     self.fetch(k).start()
+            if self.group >= 2:
+                for k in near:
+                    for other in far:
+                        self.via(k, other).wait_send()
 
         def finish(self):
             if self.group >= 2:
-                for k in range(1, chips):
+                for k in self.partners():
                     self.fetch(k).wait()
 
             def parts(lanes):
                 yield sums[self.group][p, :, lanes]
-                for k in range(1, chips):
+                for k in self.partners():
                     if self.group >= 2:
                         yield stage[k - 1, :, lanes]
                     else:
@@ -728,6 +791,8 @@
 
     pick_rope[...] = one_hot(True)
     pick_end[...] = one_hot(False)
+    for copy in loads[7:]:
+        copy.wait()
     gain_mine = block(gain_in, f, 8)
     gain_mine[...] = jnp.zeros(gain_mine.shape, F32)
     gain_mine[0:1, 0:shard] = gain_a[...].astype(F32)
@@ -1047,6 +1112,16 @@
 
     output = Reduce(2, by_turned([(hid, weights[4])]), ct_buf, r_two)
 
+    fits = widths[0] <= width and 3 * ff >= width and ff % TILE == 0
+
+    def turn_qkv():
+        for t in range(width // LANES if fits else 0):
+            at_lane = t * LANES
+            dst = weights[2 + at_lane // ff]
+            dst[0 : widths[0], at_lane % ff : at_lane % ff + LANES] = weights[0][
+                at_lane : at_lane + LANES, :
+            ].T
+
     def finish_mlp():
         for h in range(2):
             after_mlp.final(h)
@@ -1072,7 +1147,10 @@
         finish_mlp()
 
     gate_g.send_all()
-    work = [gate_g.own_all, up_g.send_all]
+    for g in (2, 3, 4):
+        gathers[g].drain()
+    turn_qkv()
+    work = [both(gate_g.own_all, down.relay), up_g.send_all]
     for s in range(1, n - 1):
         for h in range(2):
             after_mlp.in_adv(s, h)
@@ -1098,6 +1176,7 @@
     for s in range(n - 2, 1, -1):
         output.send_at(s)
 
+    gate_g.relay()
     after_mlp.drain()
     mi_line.drain()
 
@@ -1136,7 +1215,18 @@
             value * normed, axis=0, keepdims=True
         )
 
-    after_in = Reduce(3, by_turned([(gqkv, weights[0])]), s_buf, r_buf, add_gain)
+    def by_qkv():
+        if not fits:
+            return by_turned([(gqkv, weights[0])])
+
+        def tile_of(t, r):
+            at_lane = t * TILE
+            held = weights[2 + at_lane // ff]
+            return mm(gqkv[r, :], held[0 : widths[0], at_lane % ff : at_lane % ff + TILE])
+
+        return tile_of
+
+    after_in = Reduce(3, by_qkv(), s_buf, r_buf, add_gain, plain=fits)
     out_g_grad = Grad(1, t_one, mixed_pack, emit_out)
     qkv_g = Grad(0, t_two, gqkv_pack, emit_qkv)
 
@@ -1171,6 +1261,10 @@
         for h in range(2):
             gm_line.arrive(s, h)
         at(s, outer_back)
+        if s == 2:
+            up_g.relay()
+    if n == 2:
+        up_g.relay()
     quarter = width // 4
     gain_mine = block(gain_z, d, 8)
     for i in range(8):
@@ -1257,7 +1351,7 @@
     gm_line.drain()
     for k in range(1, n):
         gain_swap(k).wait_send()
-    for gather in gathers + [gain_gather, gain_back]:
+    for gather in gathers[:2] + [gain_gather, gain_back]:
         gather.drain()
     big_stores.pop().wait()
     for copy in stores:
@@ -1342,6 +1436,12 @@
             pltpu.VMEM((nq * HD, q_wide), BF),
         ]
         + [pltpu.VMEM(w.shape, BF) for w in (w_q, w_k, w_v, w_o)]
+        + [
+            pltpu.SMEM(lengths.shape, jnp.int32),
+            pltpu.VMEM(freq.shape, F32),
+            pltpu.VMEM(gain_a.shape, BF),
+            pltpu.VMEM(gain_m.shape, BF),
+        ]
         + [pltpu.VMEM((rows, width), BF)]
         + [pltpu.VMEM(w.shape, F32) for w in (w_q, w_k, w_v, w_o, w_g)]
         + [
@@ -1364,14 +1464,17 @@
             pltpu.SemaphoreType.DMA((5, chips)),
             pltpu.SemaphoreType.DMA((5, chips)),
             pltpu.SemaphoreType.DMA((chips,)),
+            pltpu.SemaphoreType.DMA((11,)),
             pltpu.SemaphoreType.DMA((7,)),
-            pltpu.SemaphoreType.DMA((7,)),
+            pltpu.SemaphoreType.DMA((5, chips)),
+            pltpu.SemaphoreType.DMA((5, chips)),
         ]
+        + [pltpu.VMEM((max(1, chips // 2 - 1), shard, ff), BF)] * 3
     )
     made = pl.pallas_call(
         partial(layer_kernel, dims),
         out_shape=out_shape,
-        in_specs=[pl.BlockSpec(memory_space=pltpu.SMEM)] + [vmem] * 3 + [hbm] * 9,
+        in_specs=[hbm] * 13,
         out_specs=[hbm] * 2 + [vmem] * 2 + [hbm] * 10,
         scratch_shapes=scratch,
         compiler_params=pltpu.CompilerParams(
@@ -1408,9 +1511,9 @@
     w_up,
     w_down,
 ):
-    frequency = ROPE_BASE ** (-jnp.arange(HALF, dtype=F32) / HALF)
-    frequency = jnp.pad(frequency, (0, LANES // 2 - HALF))
-    freq = jnp.concatenate([frequency, frequency])[None, :]
+    frequency = np.float64(ROPE_BASE) ** (-np.arange(HALF) / HALF)
+    frequency = np.pad(frequency, (0, LANES // 2 - HALF))
+    freq = jnp.asarray(np.concatenate([frequency, frequency])[None, :], F32)
     results = run_layer(
         lengths,
         freq,

time: 194 us -> 191 us (0.985)
  no operation moved by 1% of the time
where the time goes in v7:
time: 191 us
  Pallas kernels  190 us (99%)
    pallas_call x1, Pallas kernels, run_layer(): pl.pallas_call(partial(layer_kernel, dims), out_shape=out_shape, in_specs...  186 us
    pallas_call x1, Pallas kernels, run_layer(): pl.pallas_call(pass_on, out_shape=results, in_specs=[hbm] * count, out_sp...  4.09 us

profile of v7, /device:TPU:8, one launch (start us, length us, event | category | flops | bytes accessed | tf_op | source)
XLA Modules:
  0.0 190.8 jit_solution(11778330441907900174)
XLA Ops:
  0.6 185.8 %layer.1 = (bf16[128,1536]{1,0:T(8,128)(2,1)}, f32[128,1536]{1,0:T(8,128)}, f32[1,192]{1,0:T(1,128)}, f32[1,192]{1,0:T(1,128)}, f32[192,384]{1,0:T(8,128)}, /*in...) custom-call(s32[4,4]{1,0:T(4,128)} %refs_0_.1, ...), custom_call_target="tpu_custom_call" | custom-call | tf_op jit(solution)/shard_map/layer/pallas_call | solution.py:1474
  186.5 4.1 %results.1 = (bf16[128,1536]{1,0:T(8,128)(2,1)}, f32[128,1536]{1,0:T(8,128)}, f32[1,192]{1,0:T(1,128)}, f32[1,192]{1,0:T(1,128)}, f32[192,384]{1,0:T(8,128)}, /*...) custom-call(bf16[128,1536]{1,0:T(8,128)(2,1)} %get-tuple-element.33., ...), custom_call_target="tpu_custom_call" | custom-call | tf_op jit(solution)/shard_map/results/pallas_call | solution.py:1486

commit v8 on v7

--- a/solution.py
+++ b/solution.py
@@ -95,7 +95,7 @@
     (q_in, k_in, v_in, o_in) = take(4)
     (lengths, freq, gain_a, gain_m) = take(4)
     (out_own, q_own, k_own, v_own, o_own, big_own) = take(6)
-    send_b = take(1)[0]
+    send_b, send_c = take(2)
     sums = take(5)
     from_partner = take(5)
     (w_ss, w_fs, w_qs, w_rs, w_ls) = take(5)
@@ -421,16 +421,24 @@
 
             self.over_tiles(tile)
 
-        def send_at(self, s):
+        def send_at(self, s, halves=(0, 1)):
             @pl.when(d == 0)
             def _():
-                for h in range(2):
+                for h in halves:
                     self.right(d + s, h).start()
 
             @pl.when(d == n - 1)
             def _():
-                for h in range(2):
+                for h in halves:
                     self.left(d - s, h, s == 1).start()
+
+        def send_on(self, s):
+            if s < n - 1:
+                self.send_at(s, (0,))
+            else:
+                self.send_at(s)
+                for nearer in range(2, n - 1):
+                    self.send_at(nearer, (1,))
 
         def add_right(self, index, h):
             self.add_into(index, h)
@@ -542,9 +550,12 @@
         def __init__(self, group, turned, terms, emit):
             self.group, self.turned, self.terms, self.emit = group, turned, terms, emit
             self.width = gwidths[group]
+            self.buffer = send_c if group == 1 else send_b
 
         def hand_over(self):
-            src = send_b if self.width == widest else send_b.at[:, :, pl.ds(0, self.width)]
+            src = self.buffer
+            if self.group != 1 and self.width != widest:
+                src = send_b.at[:, :, pl.ds(0, self.width)]
             return remote(
                 src,
                 from_partner[self.group],
@@ -574,16 +585,17 @@
             self.hand_over().wait_send()
 
         def send_all(self):
-            if handing:
+            if self.group != 1 and handing:
                 handing.pop().release()
 
             def tile(lanes):
                 for q, value in enumerate(self.blocks_of(1 - c, lanes)):
-                    send_b[q, :, lanes] = value.astype(BF)
+                    self.buffer[q, :, lanes] = value.astype(BF)
 
             tiles(self.width, tile)
             self.hand_over().start()
-            handing.append(self)
+            if self.group != 1:
+                handing.append(self)
 
         def own_sums(self):
             self.hand_over().wait_recv()
@@ -736,22 +748,20 @@
 
         loop(n, one)
 
-    def pack_gqkv():
-        def one(b):
-            r = span(b, rows)
-            keys = slice(q_wide, q_wide + kv_wide)
-            vals = slice(q_wide + kv_wide, q_wide + 2 * kv_wide)
-            value = jnp.concatenate(
-                [
-                    mm_nt(gqkv[r, 0:q_wide], pick_rope[...]),
-                    mm_nt(gqkv[r, keys], pick_rope[0:kv_real, 0:kv_wide]),
-                    mm_nt(gqkv[r, vals], pick_end[0:kv_real, 0:kv_wide]),
-                ],
-                axis=1,
-            )
-            fill(gqkv_pack, r, value)
-
-        loop(n, one)
+    def pack_gqkv(b):
+        r = span(b, rows)
+        keys = slice(q_wide, q_wide + kv_wide)
+        vals = slice(q_wide + kv_wide, q_wide + 2 * kv_wide)
+        value = jnp.concatenate(
+            [
+                mm_nt(gqkv[r, 0:q_wide], pick_rope[...]),
+                mm_nt(gqkv[r, keys], pick_rope[0:kv_real, 0:kv_wide]),
+                mm_nt(gqkv[r, vals], pick_end[0:kv_real, 0:kv_wide]),
+            ],
+            axis=1,
+        )
+        fill(gqkv_pack, r, value)
+
 
     def turn(src, dst):
         def lane_block(t):
@@ -1137,6 +1147,8 @@
         after_mlp.out_adv(1, h)
     output.compute(keep=False)
     output.send_at(n - 1)
+    for s in range(2, n - 1):
+        output.send_at(s, (0,))
     down.own_all()
     for s in range(2, n - 1):
         for h in range(2):
@@ -1173,8 +1185,8 @@
         finish_mlp()
         gm_line.start(1)
 
-    for s in range(n - 2, 1, -1):
-        output.send_at(s)
+    for s in range(2, n - 1):
+        output.send_at(s, (1,))
 
     gate_g.relay()
     after_mlp.drain()
@@ -1256,13 +1268,29 @@
         back(j)
         after_in.single(j)
 
+    def ready(j):
+        pack_gqkv(j)
+
+        def lane_block(t):
+            t_one[cols(t, LANES), span(j, rows)] = gm_buf[span(j, rows), cols(t, LANES)].T
+
+        loop(width // LANES, lane_block)
+
+
+    ready(d)
+    ready(inner)
     at_outer(outer_back)
+    at_outer(ready)
     for s in range(2, n):
         for h in range(2):
             gm_line.arrive(s, h)
         at(s, outer_back)
+        if s < n - 1:
+            after_in.send_on(s)
         if s == 2:
             up_g.relay()
+        if s < n - 1:
+            at(s, ready)
     if n == 2:
         up_g.relay()
     quarter = width // 4
@@ -1271,18 +1299,17 @@
         gain_mine[i : i + 1, :] = gain_own[i // 4 : i // 4 + 1, pl.ds(i % 4 * quarter, quarter)]
     for k in range(1, n):
         gain_swap(k).start()
-    for s in range(n - 1, 1, -1):
-        after_in.send_at(s)
     if n > 2:
+        after_in.send_on(n - 1)
         output.send_at(1)
     for s in range(1, n - 1):
         for h in range(2):
             output.in_adv(s, h)
-    turn(gm_buf, t_one)
+    if n > 2:
+        at(n - 1, ready)
     out_g_grad.send_all()
-    pack_gqkv()
+    qkv_g.send_all()
     out_g_grad.own_all()
-    qkv_g.send_all()
     for h in range(2):
         after_in.out_adv(n - 2, h)
     qkv_g.own_sums()
@@ -1293,11 +1320,12 @@
     gain_back.start()
     qkv_g.ship_all()
     for s in range(n - 2, 0, -1):
+        if s < n - 2:
+            after_in.out_adv(s, 0)
         for h in range(2):
             after_in.in_adv(s, h)
         if s < n - 2:
-            for h in range(2):
-                after_in.out_adv(s, h)
+            after_in.out_adv(s, 1)
 
     def output_end():
         middle[...] = middle[...] + block(ct_buf, d)[...].astype(F32)
@@ -1345,6 +1373,7 @@
         grad.finish()
 
     handing.pop().release()
+    out_g_grad.release()
     output.drain()
     after_in.drain()
     tok_line.drain()
@@ -1446,6 +1475,7 @@
         + [pltpu.VMEM(w.shape, F32) for w in (w_q, w_k, w_v, w_o, w_g)]
         + [
             pltpu.VMEM((chips, shard, widest), BF),
+            pltpu.VMEM((chips, shard, gwidths[1]), BF),
         ]
         + [pltpu.VMEM((chips, shard, w), BF) for w in gwidths]
         + [pltpu.VMEM((chips, shard, w), BF) for w in gwidths]

time: 191 us -> 190 us (level)
  Pallas kernels: 190 us -> 188 us
where the time goes in v8:
time: 190 us; the launch traced here: 189 us
  Pallas kernels  188 us (99%)
    pallas_call x1, Pallas kernels, run_layer(): pl.pallas_call(partial(layer_kernel, dims), out_shape=out_shape, in_specs...  184 us
    pallas_call x1, Pallas kernels, run_layer(): pl.pallas_call(pass_on, out_shape=results, in_specs=[hbm] * count, out_sp...  4.09 us

profile of v8, /device:TPU:8, one launch (start us, length us, event | category | flops | bytes accessed | tf_op | source)
XLA Modules:
  0.0 188.9 jit_solution(6768543922224624788)
XLA Ops:
  0.6 184.0 %layer.1 = (bf16[128,1536]{1,0:T(8,128)(2,1)}, f32[128,1536]{1,0:T(8,128)}, f32[1,192]{1,0:T(1,128)}, f32[1,192]{1,0:T(1,128)}, f32[192,384]{1,0:T(8,128)}, /*in...) custom-call(s32[4,4]{1,0:T(4,128)} %refs_0_.1, ...), custom_call_target="tpu_custom_call" | custom-call | tf_op jit(solution)/shard_map/layer/pallas_call | solution.py:1504
  184.6 4.1 %results.1 = (bf16[128,1536]{1,0:T(8,128)(2,1)}, f32[128,1536]{1,0:T(8,128)}, f32[1,192]{1,0:T(1,128)}, f32[1,192]{1,0:T(1,128)}, f32[192,384]{1,0:T(8,128)}, /*...) custom-call(bf16[128,1536]{1,0:T(8,128)(2,1)} %get-tuple-element.33., ...), custom_call_target="tpu_custom_call" | custom-call | tf_op jit(solution)/shard_map/results/pallas_call | solution.py:1516
